TPU v7x, 32 devices: a whole 2x2x4 slice. The times are simulated.
32 devices in a mesh: wide: 2 (over x), context: 4 (over z), tensor: 4 (over y, core).
Axes of the slice: x: 2, y: 2, z: 4, core: 2. Of those that a mesh axis runs over, the one named last changes fastest.
Arguments:
- layer_input: bfloat16 [96, 197, 768], P(('wide', 'tensor')), may hold values from -6 to 6
- qkv_weight: bfloat16 [768, 3, 768], P(('wide', 'tensor'), None, 'context'), may hold values from -0.21875 to 0.21875
- proj_weight: bfloat16 [768, 768], P('context', ('wide', 'tensor')), may hold values from -0.875 to 0.875
- norm_gains: bfloat16 [2, 768], P(None, ('wide', 'tensor')), may hold values from 0.5 to 1.5
- norm_biases: bfloat16 [2, 768], P(None, ('wide', 'tensor')), may hold values from -1.796875 to 1.796875
- router_keys: bfloat16 [768, 8], P(('wide', 'tensor')), may hold values from -0.21875 to 0.21875
- up_weight: bfloat16 [8, 768, 3072], P(('wide', 'context'), None, 'tensor'), may hold values from -0.4375 to 0.4375
- down_weight: bfloat16 [8, 3072, 768], P(('wide', 'context'), 'tensor'), may hold values from -0.4375 to 0.4375
- out_cotangent: bfloat16 [96, 197, 768], P(('wide', 'tensor')), may hold values from -6 to 6
Outputs:
- layer_output: bfloat16 [96, 197, 768], P(('wide', 'tensor'))
- rms_stats: float32 [96, 3], P(('wide', 'tensor'))
- input_grad: bfloat16 [96, 197, 768], P(('wide', 'tensor'))
- qkv_grad: float32 [768, 3, 768], P(('wide', 'tensor'), None, 'context')
- proj_grad: float32 [768, 768], P('context', ('wide', 'tensor'))
- gains_grad: float32 [2, 768], P(None, ('wide', 'tensor'))
- biases_grad: float32 [2, 768], P(None, ('wide', 'tensor'))
- router_grad: float32 [768, 8], P(('wide', 'tensor'))
- up_grad: float32 [8, 768, 3072], P(('wide', 'context'), None, 'tensor')
- down_grad: float32 [8, 3072, 768], P(('wide', 'context'), 'tensor')
All inputs are finite; a program needn't handle non-finite values.
Results may differ from a plain program's by a relative error of at most 0.02.
Values may be sent and summed in bfloat16 or wider, within the bound.
A program may use at most 192 MiB of HBM per device.

v0:
```python
import math

import jax
import jax.numpy as jnp
from jax import lax
from jax.sharding import PartitionSpec as P

HEAD_DIM = 64


norm_eps = 1e-06
highest = lax.Precision.HIGHEST


def layer_stats(values):
    center = values - jnp.mean(values, axis=-1, keepdims=True)
    spread = lax.rsqrt(jnp.mean(center * center, axis=-1, keepdims=True) + norm_eps)
    return (center * spread, spread)


def norm_back(upstream, scaled, spread):
    return spread * (
        upstream
        - jnp.mean(upstream, axis=-1, keepdims=True)
        - scaled * jnp.mean(upstream * scaled, axis=-1, keepdims=True)
    )


def root_mean(values):
    return jnp.sqrt(jnp.mean(values * values, axis=(1, 2)))


def on_device(
    layer_input,
    qkv_weight,
    proj_weight,
    norm_gains,
    norm_biases,
    router_keys,
    up_weight,
    down_weight,
    out_cotangent,
):
    images, length, model_width = layer_input.shape
    token_rows = images * length
    wide_count = lax.axis_size("wide")
    context_count = lax.axis_size("context")
    context_pos = lax.axis_index("context")
    share = images // context_count
    local_experts = up_weight.shape[0]
    expert_count = local_experts * wide_count * context_count
    head_width = qkv_weight.shape[2]
    local_heads = head_width // HEAD_DIM
    logit_scale = 1.6 * math.sqrt(model_width)

    def share_of(array):
        return lax.dynamic_slice_in_dim(array, context_pos * share, share, 0)

    qkv_full, proj_rows, gain_full, bias_full, router_full = (
        lax.all_gather(qkv_weight, ("wide", "tensor"), axis=0, tiled=True),
        lax.all_gather(proj_weight, ("wide", "tensor"), axis=1, tiled=True),
        lax.all_gather(norm_gains, ("wide", "tensor"), axis=1, tiled=True),
        lax.all_gather(norm_biases, ("wide", "tensor"), axis=1, tiled=True),
        lax.all_gather(router_keys, ("wide", "tensor"), axis=0, tiled=True),
    )
    gain_vals = gain_full.astype(jnp.float32)
    bias_vals = bias_full.astype(jnp.float32)
    input_rows = layer_input.astype(jnp.float32).reshape(token_rows, model_width)
    first_hat, first_spread = layer_stats(input_rows)
    first_normed = (first_hat * gain_vals[0] + bias_vals[0]).astype(jnp.bfloat16)
    qkv_flat = qkv_full.reshape(model_width, 3 * head_width)
    projected = jnp.dot(first_normed, qkv_flat, preferred_element_type=jnp.float32).astype(
        jnp.bfloat16
    )
    heads_view = projected.reshape(images, length, 3, local_heads, HEAD_DIM)
    queries = heads_view[:, :, 0]
    keyset = heads_view[:, :, 1]
    valueset = heads_view[:, :, 2]
    scores = (
        jnp.einsum("bqhd,bkhd->bhqk", queries, keyset, preferred_element_type=jnp.float32) * 0.125
    )
    top_score = jnp.max(scores, axis=-1, keepdims=True)
    exp_scores = jnp.exp(scores - top_score)
    score_total = jnp.sum(exp_scores, axis=-1, keepdims=True)
    attn_probs = exp_scores / score_total
    log_total = top_score + jnp.log(score_total)
    head_mix = jnp.einsum(
        "bhqk,bkhd->bqhd",
        attn_probs.astype(jnp.bfloat16),
        valueset,
        preferred_element_type=jnp.float32,
    ).astype(jnp.bfloat16)
    head_rows = head_mix.reshape(token_rows, head_width)
    attention = lax.psum(
        jnp.dot(head_rows, proj_rows, preferred_element_type=jnp.float32).astype(jnp.bfloat16),
        "context",
    ).astype(jnp.float32)
    part_rows = images * length

    def pick_share(array):
        return share_of(array)

    def fan_copies(row_block):
        spread_view = row_block.reshape(local_experts, wide_count, 1, images, model_width)
        return jnp.broadcast_to(
            spread_view, (local_experts, wide_count, context_count, images, model_width)
        ).reshape(local_experts, wide_count * context_count * images, model_width)

    def reply_rows(row_block):
        return fan_copies(row_block)

    residual = input_rows + attention
    second_hat, second_spread = layer_stats(residual)
    second = second_hat * gain_vals[1] + bias_vals[1]
    tokens = second.astype(jnp.bfloat16)
    row_scale = lax.rsqrt(jnp.sum(second * second, axis=-1, keepdims=True) + norm_eps)
    unit_rows = second * row_scale
    router_vals = router_full.astype(jnp.float32)
    col_scale = lax.rsqrt(jnp.sum(router_vals * router_vals, axis=0, keepdims=True) + norm_eps)
    keys_unit = router_vals * col_scale
    cosine = jnp.dot(unit_rows, keys_unit, precision=highest)
    logits = (logit_scale * cosine).reshape(images, length, expert_count)
    dispatch = jax.nn.softmax(logits, axis=1)
    combine = jax.nn.softmax(logits, axis=2)
    dispatch_low = dispatch.astype(jnp.bfloat16)
    combine_low = combine.astype(jnp.bfloat16)
    token_grid = tokens.reshape(images, length, model_width)
    slot_send = jnp.einsum(
        "bls,bld->sbd",
        pick_share(dispatch_low),
        pick_share(token_grid),
        preferred_element_type=jnp.float32,
    ).astype(jnp.bfloat16)
    slot_recv = lax.all_to_all(
        slot_send, ("wide", "context"), split_axis=0, concat_axis=1, tiled=True
    )
    slot_all = lax.all_gather(slot_recv, "tensor", axis=1, tiled=True)
    hidden = jnp.einsum("erd,edf->erf", slot_all, up_weight, preferred_element_type=jnp.float32)
    active = jax.nn.gelu(hidden).astype(jnp.bfloat16)
    partial_out = jnp.einsum(
        "erf,efd->erd", active, down_weight, preferred_element_type=jnp.float32
    )
    expert_rows = lax.psum_scatter(
        partial_out.astype(jnp.bfloat16), "tensor", scatter_dimension=1, tiled=True
    )
    expert_all = lax.all_to_all(
        reply_rows(expert_rows), ("wide", "context"), split_axis=1, concat_axis=0, tiled=True
    )
    mixture = jnp.einsum(
        "bls,sbd->bld", combine_low, expert_all, preferred_element_type=jnp.float32
    ).reshape(part_rows, model_width)
    result = residual + mixture
    rms_part = jnp.stack(
        [
            root_mean(result.reshape(images, length, model_width)),
            root_mean(attention.reshape(images, length, model_width)),
            root_mean(mixture.reshape(images, length, model_width)),
        ],
        axis=-1,
    )
    grad_rows = out_cotangent.astype(jnp.float32).reshape(part_rows, model_width)
    comb_grad = jnp.einsum(
        "bld,sbd->bls", out_cotangent, expert_all, preferred_element_type=jnp.float32
    )
    logit_grad = combine * (comb_grad - jnp.sum(combine * comb_grad, axis=2, keepdims=True))
    out_send = jnp.einsum(
        "bls,bld->sbd",
        pick_share(combine_low),
        pick_share(out_cotangent),
        preferred_element_type=jnp.float32,
    ).astype(jnp.bfloat16)
    out_recv = lax.all_to_all(
        out_send, ("wide", "context"), split_axis=0, concat_axis=1, tiled=True
    )
    out_all = lax.all_gather(out_recv, "tensor", axis=1, tiled=True)
    active_grad = jnp.einsum(
        "erd,efd->erf", out_all, down_weight, preferred_element_type=jnp.float32
    )
    gelu_back = jax.vjp(jax.nn.gelu, hidden)[1]
    hidden_grad = gelu_back(active_grad)[0].astype(jnp.bfloat16)
    down_grad = jnp.einsum("erf,erd->efd", active, out_all, preferred_element_type=jnp.float32)
    up_grad = jnp.einsum("erd,erf->edf", slot_all, hidden_grad, preferred_element_type=jnp.float32)
    slot_part = jnp.einsum(
        "erf,edf->erd", hidden_grad, up_weight, preferred_element_type=jnp.float32
    )
    slot_back = lax.psum_scatter(
        slot_part.astype(jnp.bfloat16), "tensor", scatter_dimension=1, tiled=True
    )
    slot_grads = lax.all_to_all(
        reply_rows(slot_back), ("wide", "context"), split_axis=1, concat_axis=0, tiled=True
    )
    token_grad = jnp.einsum(
        "bls,sbd->bld", dispatch_low, slot_grads, preferred_element_type=jnp.float32
    ).reshape(part_rows, model_width)
    disp_grad = jnp.einsum(
        "bld,sbd->bls", token_grid, slot_grads, preferred_element_type=jnp.float32
    )
    logit_grad = logit_grad + dispatch * (
        disp_grad - jnp.sum(dispatch * disp_grad, axis=1, keepdims=True)
    )
    logit_flat = logit_grad.reshape(part_rows, expert_count)
    unit_grad = logit_scale * jnp.dot(logit_flat, keys_unit.T, precision=highest)
    keys_grad = logit_scale * jnp.dot(unit_rows.T, logit_flat, precision=highest)
    router_part = col_scale * (
        keys_grad - keys_unit * jnp.sum(keys_unit * keys_grad, axis=0, keepdims=True)
    )
    second_grad = token_grad + row_scale * (
        unit_grad - unit_rows * jnp.sum(unit_rows * unit_grad, axis=-1, keepdims=True)
    )
    gain_two = jnp.sum(second_grad * second_hat, axis=0)
    bias_two = jnp.sum(second_grad, axis=0)
    resid_part = grad_rows + norm_back(second_grad * gain_vals[1], second_hat, second_spread)
    layer_output = result.reshape(images, length, model_width).astype(jnp.bfloat16)
    attn_grad = resid_part.astype(jnp.bfloat16)
    mix_grad = jnp.einsum(
        "re,he->rh", attn_grad, proj_rows, preferred_element_type=jnp.float32
    ).astype(jnp.bfloat16)
    proj_part = jnp.einsum("rh,re->he", head_rows, attn_grad, preferred_element_type=jnp.float32)
    mix_heads = mix_grad.reshape(images, length, local_heads, HEAD_DIM)
    probs_again = jnp.exp(
        jnp.einsum("bqhd,bkhd->bhqk", queries, keyset, preferred_element_type=jnp.float32) * 0.125
        - log_total
    )
    prob_grad = jnp.einsum(
        "bqhd,bkhd->bhqk", mix_heads, valueset, preferred_element_type=jnp.float32
    )
    value_grad = jnp.einsum(
        "bhqk,bqhd->bkhd",
        probs_again.astype(jnp.bfloat16),
        mix_heads,
        preferred_element_type=jnp.float32,
    )
    score_grad = (
        probs_again * (prob_grad - jnp.sum(probs_again * prob_grad, axis=-1, keepdims=True))
    ).astype(jnp.bfloat16)
    query_grad = (
        jnp.einsum("bhqk,bkhd->bqhd", score_grad, keyset, preferred_element_type=jnp.float32)
        * 0.125
    )
    key_grad = (
        jnp.einsum("bhqk,bqhd->bkhd", score_grad, queries, preferred_element_type=jnp.float32)
        * 0.125
    )
    qkv_rows = (
        jnp.stack([query_grad, key_grad, value_grad], axis=2)
        .astype(jnp.bfloat16)
        .reshape(token_rows, 3 * head_width)
    )
    qkv_part = jnp.einsum(
        "rd,rk->dk", first_normed, qkv_rows, preferred_element_type=jnp.float32
    ).reshape(model_width, 3, head_width)
    normed_part = jnp.einsum("rk,dk->rd", qkv_rows, qkv_flat, preferred_element_type=jnp.float32)
    normed_grad = lax.psum(normed_part.astype(jnp.bfloat16), "context").astype(jnp.float32)
    gain_one = jnp.sum(normed_grad * first_hat, axis=0)
    bias_one = jnp.sum(normed_grad, axis=0)
    input_grad = (
        (resid_part + norm_back(normed_grad * gain_vals[0], first_hat, first_spread))
        .reshape(images, length, model_width)
        .astype(jnp.bfloat16)
    )
    qkv_grad, proj_grad, gains_grad, biases_grad, router_grad = (
        lax.psum_scatter(qkv_part, ("wide", "tensor"), scatter_dimension=0, tiled=True),
        lax.psum_scatter(proj_part, ("wide", "tensor"), scatter_dimension=1, tiled=True),
        lax.psum_scatter(
            jnp.stack([gain_one, gain_two]), ("wide", "tensor"), scatter_dimension=1, tiled=True
        ),
        lax.psum_scatter(
            jnp.stack([bias_one, bias_two]), ("wide", "tensor"), scatter_dimension=1, tiled=True
        ),
        lax.psum_scatter(router_part, ("wide", "tensor"), scatter_dimension=0, tiled=True),
    )
    return (
        layer_output,
        rms_part,
        input_grad,
        qkv_grad,
        proj_grad,
        gains_grad,
        biases_grad,
        router_grad,
        up_grad,
        down_grad,
    )


def solution(mesh):
    placed = (
        P(("wide", "tensor"), None, None),
        P(("wide", "tensor"), None, "context"),
        P("context", ("wide", "tensor")),
        P(None, ("wide", "tensor")),
        P(None, ("wide", "tensor")),
        P(("wide", "tensor"), None),
        P(("wide", "context"), None, "tensor"),
        P(("wide", "context"), "tensor", None),
        P(("wide", "tensor"), None, None),
    )
    return jax.shard_map(
        on_device,
        mesh=mesh,
        in_specs=placed,
        out_specs=(
            P(("wide", "tensor"), None, None),
            P(("wide", "tensor"), None),
            P(("wide", "tensor"), None, None),
            P(("wide", "tensor"), None, "context"),
            P("context", ("wide", "tensor")),
            P(None, ("wide", "tensor")),
            P(None, ("wide", "tensor")),
            P(("wide", "tensor"), None),
            P(("wide", "context"), None, "tensor"),
            P(("wide", "context"), "tensor", None),
        ),
        check_vma=False,
    )
```

profile of v0, /device:TPU:0, one launch (start us, length us, event | category | flops | bytes accessed | tf_op | source)
XLA Modules:
  0.0 813.4 jit_solution(3464455596057130943)
XLA Ops:
  7.2 10.5 %all-gather.1 = bf16[8,96,2]{1,2,0:T(2,128)(2,1)S(1)} all-gather(bf16[1,96,2]{1,2,0:T(2,128)(2,1)} %bitcast.162), channel_id=1, replica_groups=mesh['wide'=2,'context'=4,'tensor'=4] {'wide','tensor'}, dimensions={0}, use_global_device_ids=true | all-gather | bytes 3456 | tf_op jit(solution)/shard_map/all_gather | solution.py:63
  17.8 8.6 %all-gather = bf16[8,96,2]{1,2,0:T(2,128)(2,1)S(1)} all-gather(bf16[1,96,2]{1,2,0:T(2,128)(2,1)} %bitcast.163), channel_id=1, replica_groups=mesh['wide'=2,'context'=4,'tensor'=4] {'wide','tensor'}, dimensions={0}, use_global_device_ids=true | all-gather | bytes 3456 | tf_op jit(solution)/shard_map/all_gather | solution.py:62
  40.0 12.5 %all_gather.23 = bf16[768,3,192]{2,1,0:T(4,128)(2,1)S(1)} all-gather(bf16[96,3,192]{2,1,0:T(4,128)(2,1)S(1)} %copy.115), channel_id=1, replica_groups=mesh['wide'=2,'context'=4,'tensor'=4] {'wide','tensor'}, dimensions={0}, use_global_device_ids=true | all-gather | bytes 995328 | tf_op jit(solution)/shard_map/all_gather | solution.py:60
  54.9 6.3 convolution_convert_fusion.2
  61.2 12.9 %reshape.339 = bf16[12,197,3,3,64]{1,0,4,3,2:T(8,128)(2,1)} reshape(bf16[2364,576]{0,1:T(8,128)(2,1)} %convolution_convert_fusion.2) | data formatting | bytes 5446656 | tf_op jit(solution)/shard_map/reshape | solution.py:75
  89.0 19.8 %all_gather.24 = bf16[192,768]{0,1:T(8,128)(2,1)S(1)} all-gather(bf16[192,96]{0,1:T(8,128)(2,1)S(1)} %copy.122), channel_id=1, replica_groups=mesh['wide'=2,'context'=4,'tensor'=4] {'wide','tensor'}, dimensions={1}, use_global_device_ids=true | all-gather | bytes 331776 | tf_op jit(solution)/shard_map/all_gather | solution.py:61
  112.7 7.5 reshape.337
  120.2 8.0 all-gather.2
  128.4 121.6 %all-reduce.3.cloned.1.call-done = bf16[2364,768]{1,0:T(8,128)(2,1)} async-done(((bf16[2364,768]{1,0:T(8,128)(2,1)}), bf16[2364,768]{1,0:T(8,128)(2,1)}) %all-reduce.3.cloned.1.call-update) | async-done | bytes 3631120 | tf_op jit(solution)/shard_map/psum | solution.py:94
  250.0 6.3 fusion.114
  261.7 8.1 fusion.116
  299.0 5.7 all_gather.26
  308.9 5.7 all_gather.27
  318.6 9.9 %reduce-scatter.16.cloned.1.call-done = bf16[1,24,768]{2,1,0:T(8,128)(2,1)} async-done(((bf16[1,96,768]{2,1,0:T(8,128)(2,1)}), bf16[1,24,768]{2,1,0:T(8,128)(2,1)}) %reduce-scatter.16.cloned.1.call-update) | async-done | bytes 36880 | tf_op jit(solution)/shard_map/reduce_scatter | solution.py:143
  337.6 7.5 reshape.354
  373.1 8.8 %reshape.346 = f32[2364,768]{1,0:T(8,128)} reshape(f32[12,197,768]{2,1,0:T(8,128)} %get-tuple-element.42) | data formatting | bytes 14524416 | tf_op jit(solution)/shard_map/reshape | solution.py:151
  382.0 8.7 %reshape.350 = f32[2364,768]{1,0:T(8,128)} reshape(f32[12,197,768]{2,1,0:T(8,128)} %fusion.90) | data formatting | bytes 14524416 | tf_op jit(solution)/shard_map/reshape | solution.py:194
  393.7 12.7 %multiply_reduce_fusion.5 = (f32[2364]{0:T(1024)S(1)}, f32[2364,768]{1,0:T(8,128)}) fusion(f32[2364]{0:T(1024)S(1)} %copy-done.47, f32[768]{0:T(1024)S(1)} %copy-done.50, f32[768]{0:T(1024)S(1)} %copy-done.44, f32[2364]{0:T(1024)S(1)} %copy-done.36, f32[2364,768]{1,0:T(8,128)} %copy-done.3, f32[2364]{0:T(1024)S(1)} %copy-done.28, ...), kind=kOutput, calls=%fused_computation.30 | convolution fusion | flops 188821184 | bytes 14668640 | tf_op jit(solution)/shard_map/dot_general | solution.py:202
  406.5 15.8 %multiply_reduce_fusion.3 = (f32[768]{0:T(1024)S(1)}, f32[2364]{0:T(1024)S(1)}, f32[2364]{0:T(1024)S(1)}, f32[768]{0:T(1024)S(1)}, f32[2364]{0:T(1024)S(1)}, /*index=5*/f32[2364,768]{1,0:T(8,128)}, bf16[2364,768]{1,0:T(8,128)(2,1)}) fusion(f32[2364,768]{1,0:T(8,128)} %copy-done.3, f32[2364]{0:T(1024)S(1)} %copy-done.36, f32[2364]{0:T(1024)S(1)} %copy-done.28, ...), kind=kLoop, calls=%fused_computation.25 | loop fusion | flops 38117964 | bytes 40020624 | tf_op jit(solution)/shard_map/reduce_sum | solution.py:210
  422.3 8.4 %multiply_add_fusion = f32[2364,768]{1,0:T(8,128)S(1)} fusion(f32[2364,768]{1,0:T(8,128)} %reshape.354, f32[2364,768]{1,0:T(8,128)} %get-tuple-element.23, f32[2364,768]{1,0:T(8,128)} %copy-done.3, f32[2364]{0:T(1024)S(1)} %broadcast_multiply_fusion.3, f32[2364]{0:T(1024)S(1)} %broadcast_multiply_fusion.4, f32[768]{0:T(1024)S(1)} %copy-done.44, ...), kind=kLoop, calls=%fused_computation.27 | loop fusion | flops 14524416 | bytes 29089728 | tf_op jit(solution)/shard_map/add | solution.py:212
  460.4 8.8 %convert_element_type.155 = bf16[2364,576]{0,1:T(8,128)(2,1)} reshape(bf16[12,197,3,3,64]{1,0,4,3,2:T(8,128)(2,1)} %copy.141) | data formatting | bytes 5446656 | tf_op jit(solution)/shard_map/convert_element_type | solution.py:246
  469.2 6.7 convolution_convert_fusion
  480.7 8.3 %multiply_reduce_fusion.13 = (f32[8]{0:T(128)S(1)}, f32[768,8]{0,1:T(8,128)S(1)}) fusion(f32[768,8]{0,1:T(8,128)S(1)} %copy-done.34, f32[8]{0:T(128)S(1)} %copy-done.54, f32[2364,8]{0,1:T(8,128)S(1)} %reshape.351, f32[2364]{0:T(1024)S(1)} %copy-done.47, f32[768]{0:T(1024)S(1)} %copy-done.50, f32[768]{0:T(1024)S(1)} %copy-done.44, f32[2364]{0:T(1024)S(1)} %copy-done.36, ...), kind=kOutput, calls=%fused_computation.133 | convolution fusion | flops 183395328 | bytes 7421584 | tf_op jit(solution)/shard_map/dot_general | solution.py:203
  495.7 116.4 %all-reduce.5.cloned.1.call-done = bf16[2364,768]{1,0:T(8,128)(2,1)} async-done(((bf16[2364,768]{1,0:T(8,128)(2,1)}), bf16[2364,768]{1,0:T(8,128)(2,1)}) %all-reduce.5.cloned.1.call-update) | async-done | bytes 3631120 | tf_op jit(solution)/shard_map/psum | solution.py:253
  612.1 7.3 fusion.11
  621.7 7.7 fusion.117
  638.4 9.5 %reduce-scatter.28.cloned.1.call-done = f32[96,8]{1,0:T(8,128)} async-done(((f32[768,8]{1,0:T(8,128)}), f32[96,8]{1,0:T(8,128)}) %reduce-scatter.28.cloned.1.call-update) | async-done | bytes 3088
  649.4 37.1 %reduce-scatter.22.cloned.1.call-done = f32[96,192]{1,0:T(8,128)} async-done(((f32[768,192]{1,0:T(8,128)}), f32[96,192]{1,0:T(8,128)}) %reduce-scatter.22.cloned.1.call-update) | async-done | bytes 73744
  688.1 9.5 %fusion.9 = bf16[2364,768]{1,0:T(8,128)(2,1)} fusion(f32[2364,768]{1,0:T(8,128)} %copy-done.4, bf16[2364,768]{1,0:T(8,128)(2,1)} %all-reduce.5.cloned.1.call-done, f32[2364,768]{1,0:T(8,128)} %reshape.337, f32[2364]{0:T(1024)S(1)} %broadcast_multiply_fusion.1, f32[2364]{0:T(1024)S(1)} %div.78, f32[2364]{0:T(1024)S(1)} %broadcast_multiply_fusion.2, ...), kind=kLoop, calls=%fused_computation.22 | loop fusion | flops 18155520 | bytes 21827520 | tf_op jit(solution)/shard_map/convert_element_type | solution.py:259
  701.9 21.6 %reduce-scatter.24.cloned.1.call-done = f32[96,2]{1,0:T(8,128)} async-done(((f32[768,2]{1,0:T(8,128)}), f32[96,2]{1,0:T(8,128)}) %reduce-scatter.24.cloned.1.call-update) | async-done | bytes 784
  724.9 35.5 %reduce-scatter.26.cloned.1.call-done = f32[96,2]{1,0:T(8,128)} async-done(((f32[768,2]{1,0:T(8,128)}), f32[96,2]{1,0:T(8,128)}) %reduce-scatter.26.cloned.1.call-update) | async-done | bytes 784
  761.8 44.9 %reduce-scatter.20.cloned.1.call-done = f32[96,3,192]{2,0,1:T(8,128)} async-done(((f32[768,3,192]{2,0,1:T(8,128)}), f32[96,3,192]{2,0,1:T(8,128)}) %reduce-scatter.20.cloned.1.call-update) | async-done | bytes 221200 | tf_op jit(solution)/shard_map/reduce_scatter | solution.py:262
  (260 shorter events, 179.9 us)
Async XLA Ops:
  7.2 299.2 %copy-start = (bf16[1,768,768]{2,1,0:T(8,128)(2,1)S(1)}, bf16[1,768,768]{2,1,0:T(8,128)(2,1)}, u32[]{:S(2)}) copy-start(bf16[1,768,768]{2,1,0:T(8,128)(2,1)} %param.16) | copy-start | bytes 3538948
  7.2 242.8 %all-reduce.3.cloned.1.call-start = ((), (), s32[]{:S(2)}) async-start(), calls=%async_computation.11 | async-start | bytes 7274496 | tf_op jit(solution)/shard_map/psum | solution.py:94
  32.3 228.7 %copy-start.43 = (f32[768]{0:T(1024)}, f32[768]{0:T(1024)S(1)}, u32[]{:S(2)}) copy-start(f32[768]{0:T(1024)S(1)} %get-tuple-element.48) | copy-start | bytes 9220
  32.4 228.7 %copy-start.49 = (f32[768]{0:T(1024)}, f32[768]{0:T(1024)S(1)}, u32[]{:S(2)}) copy-start(f32[768]{0:T(1024)S(1)} %get-tuple-element.21) | copy-start | bytes 9220
  128.3 132.8 %copy-start.33 = (f32[768,8]{0,1:T(8,128)}, f32[768,8]{0,1:T(8,128)S(1)}, u32[]{:S(2)}) copy-start(f32[768,8]{0,1:T(8,128)S(1)} %reshape.361) | copy-start | bytes 73732
  128.4 132.7 %copy-start.53 = (f32[8]{0:T(128)}, f32[8]{0:T(128)S(1)}, u32[]{:S(2)}) copy-start(f32[8]{0:T(128)S(1)} %add_rsqrt_fusion.3) | copy-start | bytes 100
  269.8 35.5 %copy-start.15 = (bf16[1,768,768]{2,1,0:T(8,128)(2,1)S(1)}, bf16[1,768,768]{2,1,0:T(8,128)(2,1)}, u32[]{:S(2)}) copy-start(bf16[1,768,768]{2,1,0:T(8,128)(2,1)} %param.15) | copy-start | bytes 3538948
  282.7 10.8 %all-to-all-start = ((bf16[8,3,768]{2,1,0:T(4,128)(2,1)}), bf16[8,3,768]{2,1,0:T(4,128)(2,1)}, u32[]{:S(2)}, u32[]{:S(2)}) async-start(bf16[8,3,768]{2,1,0:T(4,128)(2,1)} %copy.127), calls=%async_computation | async-start | bytes 98304 | tf_op jit(solution)/shard_map/all_to_all | solution.py:134
  293.5 13.9 %all-to-all-start.2 = ((bf16[8,3,768]{2,1,0:T(4,128)(2,1)}), bf16[8,3,768]{2,1,0:T(4,128)(2,1)}, u32[]{:S(2)}, u32[]{:S(2)}) async-start(bf16[8,3,768]{2,1,0:T(4,128)(2,1)} %copy.130), calls=%async_computation.3 | async-start | bytes 98304 | tf_op jit(solution)/shard_map/all_to_all | solution.py:172
  297.5 31.0 %reduce-scatter.16.cloned.1.call-start = ((), (), s32[]{:S(2)}) async-start(), calls=%async_computation.12 | async-start | bytes 184320 | tf_op jit(solution)/shard_map/reduce_scatter | solution.py:143
  307.4 43.2 %reduce-scatter.18.cloned.1.call-start = ((), (), s32[]{:S(2)}) async-start(), calls=%async_computation.13 | async-start | bytes 184320 | tf_op jit(solution)/shard_map/reduce_scatter | solution.py:186
  317.4 27.7 %copy-start.38 = (f32[12,3,197]{2,1,0:T(4,128)S(1)}, f32[12,3,197]{2,1,0:T(4,128)}, u32[]{:S(2)}) copy-start(f32[12,3,197]{2,1,0:T(4,128)} %copy-done.37) | copy-start | bytes 85108
  332.1 21.6 %all-to-all-start.1 = ((bf16[8,2,4608]{2,1,0:T(2,128)(2,1)}), bf16[8,2,4608]{2,1,0:T(2,128)(2,1)S(1)}, u32[]{:S(2)}, u32[]{:S(2)}) async-start(bf16[8,2,4608]{2,1,0:T(2,128)(2,1)} %reshape.380), calls=%async_computation.2 | async-start | bytes 294912 | tf_op jit(solution)/shard_map/all_to_all | solution.py:146
  353.0 14.9 %copy-start.32 = (bf16[12,197,8]{1,2,0:T(8,128)(2,1)S(1)}, bf16[12,197,8]{1,2,0:T(8,128)(2,1)}, u32[]{:S(2)}) copy-start(bf16[12,197,8]{1,2,0:T(8,128)(2,1)} %copy-done.31) | copy-start | bytes 113476
  353.8 13.2 %all-to-all-start.3 = ((bf16[8,2,4608]{2,1,0:T(2,128)(2,1)}), bf16[8,2,4608]{2,1,0:T(2,128)(2,1)S(1)}, u32[]{:S(2)}, u32[]{:S(2)}) async-start(bf16[8,2,4608]{2,1,0:T(2,128)(2,1)} %reshape.382), calls=%async_computation.5 | async-start | bytes 294912 | tf_op jit(solution)/shard_map/all_to_all | solution.py:189
  359.3 252.8 %all-reduce.5.cloned.1.call-start = ((), (), s32[]{:S(2)}) async-start(), calls=%async_computation.14 | async-start | bytes 7274496 | tf_op jit(solution)/shard_map/psum | solution.py:253
  381.9 11.8 %copy-start.28 = (f32[2364]{0:T(1024)S(1)}, f32[2364]{0:T(1024)}, u32[]{:S(2)}) copy-start(f32[2364]{0:T(1024)} %copy-done.27) | copy-start | bytes 28372
  381.9 11.8 %copy-start.34 = (f32[768,8]{0,1:T(8,128)S(1)}, f32[768,8]{0,1:T(8,128)}, u32[]{:S(2)}) copy-start(f32[768,8]{0,1:T(8,128)} %copy-done.33) | copy-start | bytes 73732
  381.9 11.8 %copy-start.36 = (f32[2364]{0:T(1024)S(1)}, f32[2364]{0:T(1024)}, u32[]{:S(2)}) copy-start(f32[2364]{0:T(1024)} %copy-done.35) | copy-start | bytes 28372
  381.9 11.8 %copy-start.44 = (f32[768]{0:T(1024)S(1)}, f32[768]{0:T(1024)}, u32[]{:S(2)}) copy-start(f32[768]{0:T(1024)} %copy-done.43) | copy-start | bytes 9220
  381.9 11.8 %copy-start.47 = (f32[2364]{0:T(1024)S(1)}, f32[2364]{0:T(1024)}, u32[]{:S(2)}) copy-start(f32[2364]{0:T(1024)} %copy-done.46) | copy-start | bytes 28372
  381.9 11.8 %copy-start.50 = (f32[768]{0:T(1024)S(1)}, f32[768]{0:T(1024)}, u32[]{:S(2)}) copy-start(f32[768]{0:T(1024)} %copy-done.49) | copy-start | bytes 9220
  381.9 11.8 %copy-start.54 = (f32[8]{0:T(128)S(1)}, f32[8]{0:T(128)}, u32[]{:S(2)}) copy-start(f32[8]{0:T(128)} %copy-done.53) | copy-start | bytes 100
  422.2 11.4 %copy-start.17 = (bf16[192,768]{0,1:T(8,128)(2,1)S(1)}, bf16[192,768]{0,1:T(8,128)(2,1)}, u32[]{:S(2)}) copy-start(bf16[192,768]{0,1:T(8,128)(2,1)} %copy-done.16) | copy-start | bytes 884740
  439.6 11.1 %slice-start = ((s8[7372800]{0:T(1024)(128)(4,1)}), s8[4194304]{0:T(1024)(128)(4,1)S(1)}, s32[]{:S(2)}) async-start(s8[7372800]{0:T(1024)(128)(4,1)} %bitcast.147), calls=%async_computation.20 | async-start | bytes 8388608
  455.8 13.4 %copy-start.22 = (bf16[768,3,192]{0,2,1:T(8,128)(2,1)S(1)}, bf16[768,3,192]{0,2,1:T(8,128)(2,1)}, u32[]{:S(2)}) copy-start(bf16[768,3,192]{0,2,1:T(8,128)(2,1)} %copy.116) | copy-start | bytes 2654212
  475.9 172.0 %reduce-scatter.28.cloned.1.call-start = ((), (), s32[]{:S(2)}) async-start(), calls=%async_computation.19 | async-start | bytes 442368
  490.1 196.4 %reduce-scatter.22.cloned.1.call-start = ((), (), s32[]{:S(2)}) async-start(), calls=%async_computation.16 | async-start | bytes 884736
  495.7 227.8 %reduce-scatter.24.cloned.1.call-start = ((), (), s32[]{:S(2)}) async-start(), calls=%async_computation.17 | async-start | bytes 442368
  620.4 140.0 %reduce-scatter.26.cloned.1.call-start = ((), (), s32[]{:S(2)}) async-start(), calls=%async_computation.18 | async-start | bytes 442368
  621.4 185.3 %reduce-scatter.20.cloned.1.call-start = ((), (), s32[]{:S(2)}) async-start(), calls=%async_computation.15 | async-start | bytes 2654208 | tf_op jit(solution)/shard_map/reduce_scatter | solution.py:262
  688.1 118.6 %copy-start.1 = (bf16[1,768,768]{2,1,0:T(8,128)(2,1)S(1)}, bf16[1,768,768]{2,1,0:T(8,128)(2,1)}, u32[]{:S(2)}) copy-start(bf16[1,768,768]{2,1,0:T(8,128)(2,1)} %param.16) | copy-start | bytes 3538948
  (38 other events, 171.0 us)
Sparse Core Ops, SparseCore 0:
  112.8 137.2 all-reduce.2
  307.5 20.9 reduce-scatter.15
  331.0 19.6 reduce-scatter.17
  476.0 136.0 all-reduce.4
  615.0 32.8 reduce-scatter.27
  651.5 34.9 reduce-scatter.21
  689.5 33.8 reduce-scatter.23
  726.5 33.8 reduce-scatter.25
  764.3 42.3 reduce-scatter.19
where the time goes:
time: 814 us; the launch traced here: 813 us
  waiting for transfers between devices  408 us (50%)
  local copies, waits for them, and re-layouts  127 us (16%)
  matrix products  98.5 us (12%)
  other arithmetic  74.8 us (9%)
  blocking collectives  70.8 us (9%)
  starting transfers between devices  19.4 us (2%)
  between operations  15 us (2%)
    psum x1, waiting for transfers between devices, on_device(): lax.psum(jnp.dot(head_rows, proj_rows, preferred_element_type=jnp.float32...  122 us
    psum x1, waiting for transfers between devices, on_device(): lax.psum(normed_part.astype(jnp.bfloat16), 'context').astype(jnp.float32)  116 us
    unnamed x13, waiting for transfers between devices  104 us
    reduce_scatter x1, waiting for transfers between devices, on_device(): lax.psum_scatter(qkv_part, ('wide', 'tensor'), scatter_dimension=0, tiled...  44.9 us
    unnamed x128, local copies, waits for them, and re-layouts  20.7 us
    all_gather x1, blocking collectives, on_device(): lax.all_gather(proj_weight, ('wide', 'tensor'), axis=1, tiled=True)  19.8 us
  transfers between devices with their start and end apart: 13, of which 11 were waited for; matrix products, arithmetic and copies ran while one was open for 12% of the time, Pallas kernels for 0%

commit v1 on v0

v1 whole, which is shorter than its diff:
```python
import math

import jax
import jax.numpy as jnp
from jax import lax
from jax.sharding import PartitionSpec as P

HEAD_DIM = 64

norm_eps = 1e-06
highest = lax.Precision.HIGHEST
f32 = jnp.float32
bf16 = jnp.bfloat16


def layer_stats(values):
    center = values - jnp.mean(values, axis=-1, keepdims=True)
    spread = lax.rsqrt(jnp.mean(center * center, axis=-1, keepdims=True) + norm_eps)
    return (center * spread, spread)


def norm_back(upstream, scaled, spread):
    return spread * (
        upstream
        - jnp.mean(upstream, axis=-1, keepdims=True)
        - scaled * jnp.mean(upstream * scaled, axis=-1, keepdims=True)
    )


def root_mean(values):
    return jnp.sqrt(jnp.mean(values * values, axis=(1, 2)))


def dot32(spec, a, b, **kw):
    return jnp.einsum(spec, a, b, preferred_element_type=f32, **kw)


def on_device(
    layer_input,
    qkv_weight,
    proj_weight,
    norm_gains,
    norm_biases,
    router_keys,
    up_weight,
    down_weight,
    out_cotangent,
):
    images, length, width = layer_input.shape
    wide_n = lax.axis_size("wide")
    ctx_n = lax.axis_size("context")
    ten_n = lax.axis_size("tensor")
    share = images // ctx_n
    start = lax.axis_index("context") * share
    slots_n = router_keys.shape[1]
    cols = qkv_weight.shape[2]
    rows = qkv_weight.shape[0]
    heads_b = cols // HEAD_DIM
    logit_scale = 1.6 * math.sqrt(width)
    everyone = ("context", "wide", "tensor")
    plane = ("wide", "tensor")

    pack = jnp.concatenate([qkv_weight.reshape(rows, 3 * cols), proj_weight.T], axis=1)
    weights = lax.all_gather(pack, everyone, axis=0, tiled=True).reshape(ctx_n, width, 4 * cols)
    small = jnp.concatenate([norm_gains, norm_biases, router_keys.T], axis=0)
    small = lax.all_gather(small, plane, axis=1, tiled=True).astype(f32)
    gain_vals, bias_vals, router_vals = small[0:2], small[2:4], small[4:].T
    qkv_full = weights[:, :, : 3 * cols]
    proj_t = weights[:, :, 3 * cols :]

    x = lax.dynamic_slice_in_dim(layer_input, start, share, 0).astype(f32)
    g = lax.dynamic_slice_in_dim(out_cotangent, start, share, 0)
    hat1, spread1 = layer_stats(x)
    normed1 = (hat1 * gain_vals[0] + bias_vals[0]).astype(bf16)
    qkv = dot32("bld,cdk->cblk", normed1, qkv_full).astype(bf16)
    qkv = qkv.reshape(ctx_n, share, length, 3, heads_b, HEAD_DIM)
    q, k, v = qkv[:, :, :, 0], qkv[:, :, :, 1], qkv[:, :, :, 2]
    scores = dot32("cbqhd,cbkhd->cbhqk", q, k) * 0.125
    top = jnp.max(scores, axis=-1, keepdims=True)
    exps = jnp.exp(scores - top)
    probs = exps / jnp.sum(exps, axis=-1, keepdims=True)
    probs_low = probs.astype(bf16)
    heads = dot32("cbhqk,cbkhd->cbqhd", probs_low, v).astype(bf16)
    heads = heads.reshape(ctx_n, share, length, cols)
    attention = dot32("cblh,ceh->ble", heads, proj_t)

    residual = x + attention
    hat2, spread2 = layer_stats(residual)
    second = hat2 * gain_vals[1] + bias_vals[1]
    tokens = second.astype(bf16)
    row_scale = lax.rsqrt(jnp.sum(second * second, axis=-1, keepdims=True) + norm_eps)
    unit = second * row_scale
    col_scale = lax.rsqrt(jnp.sum(router_vals * router_vals, axis=0, keepdims=True) + norm_eps)
    keys_unit = router_vals * col_scale
    logits = logit_scale * jnp.einsum("bld,ds->bls", unit, keys_unit, precision=highest)
    dispatch = jax.nn.softmax(logits, axis=1)
    combine = jax.nn.softmax(logits, axis=2)
    dispatch_low = dispatch.astype(bf16)
    combine_low = combine.astype(bf16)
    slots = dot32("bls,bld->sbd", dispatch_low, tokens).astype(bf16)
    dexp = dot32("bls,bld->sbd", combine_low, g).astype(bf16)

    out = jnp.concatenate([slots, dexp], axis=1)
    got = lax.all_to_all(out, ("wide", "context"), split_axis=0, concat_axis=0, tiled=True)
    got = lax.all_gather(got, "tensor", axis=0, tiled=True)
    n = got.shape[0]
    slot_all = got[:, :share].reshape(n * share, width)
    dexp_all = got[:, share:].reshape(n * share, width)
    up, down = up_weight[0], down_weight[0]
    hidden = dot32("rd,df->rf", slot_all, up)
    active = jax.nn.gelu(hidden).astype(bf16)
    part_out = dot32("rf,fd->rd", active, down)
    active_grad = dot32("rd,fd->rf", dexp_all, down)
    hidden_grad = jax.vjp(jax.nn.gelu, hidden)[1](active_grad)[0].astype(bf16)
    down_grad = dot32("rf,rd->fd", active, dexp_all)[None]
    up_grad = dot32("rd,rf->df", slot_all, hidden_grad)[None]
    part_slot = dot32("rf,df->rd", hidden_grad, up)
    back = jnp.concatenate(
        [part_out.reshape(n, share, width), part_slot.reshape(n, share, width)], axis=1
    ).astype(bf16)
    back = lax.psum_scatter(back, "tensor", scatter_dimension=0, tiled=True)
    back = lax.all_to_all(back, ("wide", "context"), split_axis=0, concat_axis=0, tiled=True)
    expert_out = back[:, :share]
    dslots = back[:, share:]

    mixture = dot32("bls,sbd->bld", combine_low, expert_out)
    result = residual + mixture
    rms = jnp.stack([root_mean(result), root_mean(attention), root_mean(mixture)], axis=-1)
    layer_output = lax.all_gather(result.astype(bf16), "context", axis=0, tiled=True)
    dcomb = dot32("bld,sbd->bls", g, expert_out)
    ddisp = dot32("bld,sbd->bls", tokens, dslots)
    dtokens = dot32("bls,sbd->bld", dispatch_low, dslots)
    dlogits = combine * (dcomb - jnp.sum(combine * dcomb, axis=2, keepdims=True)) + dispatch * (
        ddisp - jnp.sum(dispatch * ddisp, axis=1, keepdims=True)
    )
    dunit = logit_scale * jnp.einsum("bls,ds->bld", dlogits, keys_unit, precision=highest)
    dkeys = logit_scale * jnp.einsum("bld,bls->ds", unit, dlogits, precision=highest)
    drouter = col_scale * (dkeys - keys_unit * jnp.sum(keys_unit * dkeys, axis=0, keepdims=True))
    dsecond = dtokens + row_scale * (dunit - unit * jnp.sum(unit * dunit, axis=-1, keepdims=True))
    dgain2 = jnp.sum(dsecond * hat2, axis=(0, 1))
    dbias2 = jnp.sum(dsecond, axis=(0, 1))
    dresid = g.astype(f32) + norm_back(dsecond * gain_vals[1], hat2, spread2)
    dattn = dresid.astype(bf16)
    dproj = dot32("ble,cblh->ceh", dattn, heads)
    dheads = dot32("ble,ceh->cblh", dattn, proj_t).astype(bf16)
    dheads = dheads.reshape(ctx_n, share, length, heads_b, HEAD_DIM)
    dprobs = dot32("cbqhd,cbkhd->cbhqk", dheads, v)
    dv = dot32("cbhqk,cbqhd->cbkhd", probs_low, dheads)
    ds = (probs * (dprobs - jnp.sum(probs * dprobs, axis=-1, keepdims=True))).astype(bf16)
    dq = dot32("cbhqk,cbkhd->cbqhd", ds, k) * 0.125
    dk = dot32("cbhqk,cbqhd->cbkhd", ds, q) * 0.125
    dqkv = jnp.stack([dq, dk, dv], axis=3).astype(bf16).reshape(ctx_n, share, length, 3 * cols)
    dqkv_w = dot32("bld,cblk->cdk", normed1, dqkv)
    dnormed1 = dot32("cblk,cdk->bld", dqkv, qkv_full)
    dgain1 = jnp.sum(dnormed1 * hat1, axis=(0, 1))
    dbias1 = jnp.sum(dnormed1, axis=(0, 1))
    dx = (dresid + norm_back(dnormed1 * gain_vals[0], hat1, spread1)).astype(bf16)
    input_grad = lax.all_gather(dx, "context", axis=0, tiled=True)
    rms = lax.all_gather(rms, "context", axis=0, tiled=True)

    dpack = jnp.concatenate([dqkv_w, dproj], axis=2).reshape(ctx_n * width, 4 * cols)
    dpack = lax.psum_scatter(dpack.astype(bf16), everyone, scatter_dimension=0, tiled=True)
    dpack = dpack.astype(f32)
    dsmall = jnp.concatenate(
        [jnp.stack([dgain1, dgain2, dbias1, dbias2], axis=1), drouter], axis=1
    )
    dsmall = lax.psum(dsmall, "context")
    dsmall = lax.psum_scatter(dsmall, plane, scatter_dimension=0, tiled=True)
    return (
        layer_output,
        rms,
        input_grad,
        dpack[:, : 3 * cols].reshape(rows, 3, cols),
        dpack[:, 3 * cols :].T,
        dsmall[:, 0:2].T,
        dsmall[:, 2:4].T,
        dsmall[:, 4:],
        up_grad,
        down_grad,
    )


def solution(mesh):
    images = P(("wide", "tensor"), None, None)
    qkv = P(("wide", "tensor"), None, "context")
    proj = P("context", ("wide", "tensor"))
    lane = P(None, ("wide", "tensor"))
    rowed = P(("wide", "tensor"), None)
    up = P(("wide", "context"), None, "tensor")
    down = P(("wide", "context"), "tensor", None)
    return jax.shard_map(
        on_device,
        mesh=mesh,
        in_specs=(images, qkv, proj, lane, lane, rowed, up, down, images),
        out_specs=(images, rowed, images, qkv, proj, lane, lane, rowed, up, down),
        check_vma=False,
    )
```

time: 814 us -> 552 us (0.68); the launches traced: 813 us -> 542 us
  waiting for transfers between devices: 408 us -> 310 us
  local copies, waits for them, and re-layouts: 127 us -> 35.6 us
  other arithmetic: 74.8 us -> 47.8 us
  matrix products: 98.5 us -> 72.2 us
  starting transfers between devices: 19.4 us -> 0.24 us
  blocking collectives: 70.8 us -> 61 us
    psum x2 -> x0, waiting for transfers between devices: 238 us -> none  [the longest x1 122 us: on_device(): lax.psum(jnp.dot(head_rows, proj_rows, preferred_element_type=jnp.float32...]
    all_gather x0 -> x3, waiting for transfers between devices: none -> 181 us  [the longest x1 72.3 us: on_device(): lax.all_gather(result.astype(bf16), 'context', axis=0, tiled=True)]
    unnamed x13 -> x8, waiting for transfers between devices: 104 us -> 17.4 us
    reshape x10 -> x2, local copies, waits for them, and re-layouts: 58 us -> 0.91 us  [the longest x1 0.78 us: on_device(): dexp_all = got[:, share:].reshape(n * share, width)]
    reduce_scatter x3 -> x1, waiting for transfers between devices: 60.3 us -> 111 us  [on_device(): lax.psum_scatter(dpack.astype(bf16), everyone, scatter_dimension=0, tiled...]
    all_gather x7 -> x3, blocking collectives: 70.8 us -> 28.7 us  [the longest x1 11.9 us: on_device(): rms = lax.all_gather(rms, 'context', axis=0, tiled=True)]
    convert_element_type x13 -> x2, local copies, waits for them, and re-layouts: 33.8 us -> 5.87 us  [the longest x1 5.79 us: on_device(): qkv = dot32('bld,cdk->cblk', normed1, qkv_full).astype(bf16)]
    reduce_sum x7 -> x1, other arithmetic: 27 us -> 0.58 us  [on_device(): jnp.sum(second * second, axis=-1, keepdims=True) + norm_eps]
  transfers between devices with their start and end apart: 13 -> 6, of which waited for: 11 -> 5; matrix products, arithmetic and copies ran while one was open for 12% -> 6% of each run, Pallas kernels for 0% -> 0%
where the time goes in v1:
time: 552 us; the launch traced here: 542 us
  waiting for transfers between devices  310 us (56%)
  matrix products  72.2 us (13%)
  blocking collectives  61 us (11%)
  other arithmetic  47.8 us (9%)
  local copies, waits for them, and re-layouts  35.6 us (6%)
  between operations  15.1 us (3%)
    reduce_scatter x1, waiting for transfers between devices, on_device(): lax.psum_scatter(dpack.astype(bf16), everyone, scatter_dimension=0, tiled...  111 us
    all_gather x1, waiting for transfers between devices, on_device(): lax.all_gather(result.astype(bf16), 'context', axis=0, tiled=True)  72.3 us
    dot_general x24, matrix products, dot32(): return jnp.einsum(spec, a, b, preferred_element_type=f32, **kw)  65.1 us
    all_gather x1, waiting for transfers between devices, on_device(): input_grad = lax.all_gather(dx, 'context', axis=0, tiled=True)  55.5 us
    all_gather x1, waiting for transfers between devices, on_device(): lax.all_gather(pack, everyone, axis=0, tiled=True)  53 us
    unnamed x8, waiting for transfers between devices  17.4 us
    convert_element_type x1, other arithmetic, on_device(): (probs * (dprobs - jnp.sum(probs * dprobs, axis=-1, keepdims=True))).asty...  13.9 us
    unnamed x103, local copies, waits for them, and re-layouts  13.7 us
  transfers between devices with their start and end apart: 6, of which 5 were waited for; matrix products, arithmetic and copies ran while one was open for 6% of the time, Pallas kernels for 0%

profile of v1, /device:TPU:0, one launch (start us, length us, event | category | flops | bytes accessed | tf_op | source)
XLA Modules:
  0.0 541.6 jit_solution(13824113739327236245)
XLA Ops:
  10.8 10.6 %all-gather = bf16[8,96,12]{1,2,0:T(8,128)(2,1)S(1)} all-gather(bf16[1,96,12]{1,2,0:T(8,128)(2,1)S(1)} %maximum_bitcast_fusion.1), channel_id=1, replica_groups=mesh['wide'=2,'context'=4,'tensor'=4] {'wide','tensor'}, dimensions={0}, use_global_device_ids=true | all-gather | bytes 20736 | tf_op jit(solution)/shard_map/all_gather | solution.py:66
  24.8 53.0 %all-gather.6.cloned.1.call-done = bf16[3072,768]{1,0:T(8,128)(2,1)} async-done(((bf16[96,768]{1,0:T(8,128)(2,1)}), bf16[3072,768]{1,0:T(8,128)(2,1)}) %all-gather.6.cloned.1.call-update) | async-done | bytes 4718608 | tf_op jit(solution)/shard_map/all_gather | solution.py:64
  77.8 6.6 %convert_bitcast_fusion = bf16[4,3,197,576]{3,2,1,0:T(8,128)(2,1)} fusion(bf16[4,768,768]{2,1,0:T(8,128)(2,1)} %bitcast.228, f32[768]{0:T(1024)S(1)} %get-tuple-element.62, f32[768]{0:T(1024)S(1)} %get-tuple-element.63, f32[3,197]{1,0:T(4,128)S(1)} %add_rsqrt_fusion.2, f32[3,197]{1,0:T(4,128)S(1)} %broadcast_multiply_fusion.5, ...), kind=kOutput, calls=%fused_computation.16 | convolution fusion | flops 2095600896 | bytes 7587964 | tf_op jit(solution)/shard_map/bld,cdk->cblk/dot_general | solution.py:35
  84.4 5.8 %copy.124 = bf16[4,3,197,576]{2,3,1,0:T(8,128)(2,1)} copy(bf16[4,3,197,576]{3,2,1,0:T(8,128)(2,1)} %convert_bitcast_fusion) | data formatting | bytes 5446656 | tf_op jit(solution)/shard_map/convert_element_type | solution.py:75
  90.2 2.8 fusion.84
  93.0 6.5 %fusion.140 = (f32[4,3,3,197]{3,2,1,0:T(4,128)S(1)}, f32[4,3,3,197,197]{3,4,2,1,0:T(8,128)S(1)}) fusion(f32[4,3,3,197,197]{3,4,2,1,0:T(8,128)S(1)} %fusion.84), kind=kOutput, calls=%fused_computation.195 | output fusion | flops 5588692 | bytes 11205360 | tf_op jit(solution)/shard_map/sub | solution.py:80
  99.5 3.0 fusion.36
  102.6 4.7 fusion.137
  113.2 10.8 %all_to_all.10 = bf16[8,6,768]{2,1,0:T(8,128)(2,1)S(1)} all-to-all(bf16[8,6,768]{2,1,0:T(8,128)(2,1)S(1)} %copy.130), channel_id=1, replica_groups=mesh['wide'=2,'context'=4,'tensor'=4] {'wide','context'}, dimensions={0} | all-to-all | bytes 147456 | tf_op jit(solution)/shard_map/all_to_all | solution.py:104
  124.1 6.1 %all_gather.20 = bf16[32,6,768]{2,0,1:T(8,128)(2,1)S(1)} all-gather(bf16[8,6,768]{2,0,1:T(8,128)(2,1)S(1)} %copy.131), channel_id=1, replica_groups=mesh['wide'=2,'context'=4,'tensor'=4] {'tensor'}, dimensions={0}, use_global_device_ids=true | all-gather | bytes 368640 | tf_op jit(solution)/shard_map/all_gather | solution.py:105
  133.3 2.6 fusion.106
  142.2 16.8 %reduce-scatter.10.cloned.1.call-done = bf16[8,4608]{1,0:T(8,128)(2,1)} async-done(((bf16[32,4608]{1,0:T(8,128)(2,1)}), bf16[8,4608]{1,0:T(8,128)(2,1)}) %reduce-scatter.10.cloned.1.call-update) | async-done | bytes 73744
  159.9 12.6 %all_to_all.11 = bf16[8,6,768]{2,1,0:T(8,128)(2,1)S(1)} all-to-all(bf16[8,6,768]{2,1,0:T(8,128)(2,1)S(1)} %copy.136), channel_id=1, replica_groups=mesh['wide'=2,'context'=4,'tensor'=4] {'wide','context'}, dimensions={0} | all-to-all | bytes 147456 | tf_op jit(solution)/shard_map/all_to_all | solution.py:122
  174.9 2.2 fusion.119
  177.0 2.9 fusion.122
  183.5 11.0 %multiply_reduce_fusion.2 = (f32[768]{0:T(1024)}, f32[3,197]{1,0:T(4,128)S(1)}, f32[3,197]{1,0:T(4,128)S(1)}, f32[768]{0:T(1024)}, f32[3]{0:T(128)}, /*index=5*/...) fusion(f32[3,197,768]{2,1,0:T(8,128)S(1)} %get-tuple-element.65, f32[3,197]{1,0:T(4,128)S(1)} %copy-done.18, ...), kind=kOutput, calls=%fused_computation.44 | output fusion | flops 13615274 | bytes 10009668 | tf_op jit(solution)/shard_map/mul | solution.py:139
  196.5 4.0 convolution_convert_fusion
  200.6 5.2 multiply_reduce_fusion
  205.8 13.9 %multiply_convert_fusion = bf16[4,3,3,197,197]{3,4,2,1,0:T(8,128)(2,1)S(1)} fusion(f32[4,3,3,197,197]{3,4,2,1,0:T(8,128)} %get-tuple-element.88, f32[4,3,3,197]{3,2,1,0:T(4,128)} %get-tuple-element.87, f32[4,3,3,197,197]{3,4,2,1,0:T(8,128)S(1)} %bitcast.206, f32[4,3,3,197]{3,2,1,0:T(4,128)S(1)} %copy-done.13), kind=kLoop, calls=%fused_computation.4 | loop fusion | flops 5588496 | bytes 14027976 | tf_op jit(solution)/shard_map/convert_element_type | solution.py:149
  221.8 2.7 fusion.48
  227.5 7.0 %fusion.24 = (f32[768]{0:T(1024)S(1)}, f32[3,197]{1,0:T(4,128)S(1)}, f32[3,197]{1,0:T(4,128)S(1)}, f32[768]{0:T(1024)S(1)}, f32[3,197,768,1]{2,1,0,3:T(8,128)}) fusion(f32[3,197]{1,0:T(4,128)S(1)} %copy-done.26, f32[3,197]{1,0:T(4,128)S(1)} %copy-done.16, bf16[12,197,768]{2,1,0:T(8,128)(2,1)} %param.9, s32[]{:T(128)S(6)} %select_n.4, ...), kind=kOutput, calls=%fused_computation.38 | convolution fusion | flops 2096051968 | bytes 10217596 | tf_op jit(solution)/shard_map/cblk,cdk->bld/dot_general | solution.py:35
  235.9 3.3 fusion.23
  239.9 2.6 fusion.49
  242.5 5.1 fusion.8
  247.5 2.5 pad_maximum_fusion
  250.0 6.6 %copy.147 = bf16[4,768,768]{2,1,0:T(8,128)(2,1)} copy(bf16[4,768,768]{1,2,0:T(8,128)(2,1)} %pad_maximum_fusion) | data formatting | bytes 9437184 | tf_op jit(solution)/shard_map/concatenate | solution.py:161
  261.5 11.9 %all-gather.1 = f32[4,3,3]{2,1,0:T(4,128)S(1)} all-gather(f32[1,3,3]{2,1,0:T(4,128)S(1)} %bitcast.226), channel_id=1, replica_groups=mesh['wide'=2,'context'=4,'tensor'=4] {'context'}, dimensions={0}, use_global_device_ids=true | all-gather | bytes 180 | tf_op jit(solution)/shard_map/all_gather | solution.py:159
  275.1 9.0 %psum.8 = f32[96,12]{0,1:T(8,128)S(1)} all-reduce(f32[96,12]{0,1:T(8,128)S(1)} %copy.164), channel_id=1, replica_groups=mesh['wide'=2,'context'=4,'tensor'=4] {'context'}, use_global_device_ids=true, to_apply=%region_30.0 | all-reduce | flops 1152 | bytes 9216 | tf_op jit(solution)/shard_map/psum | solution.py:167
  285.2 55.5 %all-gather.10.cloned.1.call-done = bf16[12,197,768]{2,1,0:T(8,128)(2,1)} async-done(((bf16[3,197,768]{2,1,0:T(8,128)(2,1)}), bf16[12,197,768]{2,1,0:T(8,128)(2,1)}) %all-gather.10.cloned.1.call-update) | async-done | bytes 3631120 | tf_op jit(solution)/shard_map/all_gather | solution.py:158
  340.7 72.3 %all-gather.8.cloned.1.call-done = bf16[12,197,768]{2,1,0:T(8,128)(2,1)} async-done(((bf16[3,197,768]{2,1,0:T(8,128)(2,1)}), bf16[12,197,768]{2,1,0:T(8,128)(2,1)}) %all-gather.8.cloned.1.call-update) | async-done | bytes 3631120 | tf_op jit(solution)/shard_map/all_gather | solution.py:129
  413.1 111.4 %reduce-scatter.8.cloned.1.call-done = bf16[96,768]{1,0:T(8,128)(2,1)} async-done(((bf16[3072,768]{1,0:T(8,128)(2,1)}), bf16[96,768]{1,0:T(8,128)(2,1)}) %reduce-scatter.8.cloned.1.call-update) | async-done | bytes 147472 | tf_op jit(solution)/shard_map/reduce_scatter | solution.py:162
  528.2 4.3 copy.192
  (187 shorter events, 51.2 us)
Async XLA Ops:
  7.2 125.8 %copy-start = (bf16[1,768,768]{2,1,0:T(8,128)(2,1)S(1)}, bf16[1,768,768]{2,1,0:T(8,128)(2,1)}, u32[]{:S(2)}) copy-start(bf16[1,768,768]{2,1,0:T(8,128)(2,1)} %param.15) | copy-start | bytes 3538948
  7.2 70.6 %all-gather.6.cloned.1.call-start = ((), (), s32[]{:S(2)}) async-start(), calls=%async_computation.5 | async-start | bytes 4866048 | tf_op jit(solution)/shard_map/all_gather | solution.py:64
  10.1 148.9 %reduce-scatter.10.cloned.1.call-start = ((), (), s32[]{:S(2)}) async-start(), calls=%async_computation.9 | async-start | bytes 368640
  23.1 61.3 %copy-start.21 = (f32[768]{0:T(1024)}, f32[768]{0:T(1024)S(1)}, u32[]{:S(2)}) copy-start(f32[768]{0:T(1024)S(1)} %get-tuple-element.63) | copy-start | bytes 9220
  23.1 61.3 %copy-start.30 = (f32[768]{0:T(1024)}, f32[768]{0:T(1024)S(1)}, u32[]{:S(2)}) copy-start(f32[768]{0:T(1024)S(1)} %get-tuple-element.62) | copy-start | bytes 9220
  23.1 88.1 %copy-start.23 = (f32[768]{0:T(1024)}, f32[768]{0:T(1024)S(1)}, u32[]{:S(2)}) copy-start(f32[768]{0:T(1024)S(1)} %get-tuple-element.61) | copy-start | bytes 9220
  23.1 61.3 %copy-start.15 = (f32[3,197]{1,0:T(4,128)}, f32[3,197]{1,0:T(4,128)S(1)}, u32[]{:S(2)}) copy-start(f32[3,197]{1,0:T(4,128)S(1)} %broadcast_multiply_fusion.5) | copy-start | bytes 7096
  24.8 83.5 %copy-start.27 = (f32[8]{0:T(128)}, f32[8]{0:T(128)S(1)}, u32[]{:S(2)}) copy-start(f32[8]{0:T(128)S(1)} %add_rsqrt_fusion.3) | copy-start | bytes 100
  24.8 59.6 %copy-start.25 = (f32[3,197]{1,0:T(4,128)}, f32[3,197]{1,0:T(4,128)S(1)}, u32[]{:S(2)}) copy-start(f32[3,197]{1,0:T(4,128)S(1)} %add_rsqrt_fusion.2) | copy-start | bytes 7096
  102.6 4.8 copy-start.39
  141.3 32.8 %copy-start.14 = (f32[3,197,8]{1,2,0:T(8,128)S(1)}, f32[3,197,8]{1,2,0:T(8,128)}, u32[]{:S(2)}) copy-start(f32[3,197,8]{1,2,0:T(8,128)} %get-tuple-element.79) | copy-start | bytes 56740
  141.3 32.8 %copy-start.18 = (f32[3,197]{1,0:T(4,128)S(1)}, f32[3,197]{1,0:T(4,128)}, u32[]{:S(2)}) copy-start(f32[3,197]{1,0:T(4,128)} %copy-done.17) | copy-start | bytes 7096
  141.4 32.8 %copy-start.20 = (f32[3,8]{1,0:T(4,128)S(1)}, f32[3,8]{1,0:T(4,128)}, u32[]{:S(2)}) copy-start(f32[3,8]{1,0:T(4,128)} %copy-done.19) | copy-start | bytes 292
  141.4 32.8 %copy-start.24 = (f32[768]{0:T(1024)S(1)}, f32[768]{0:T(1024)}, u32[]{:S(2)}) copy-start(f32[768]{0:T(1024)} %copy-done.23) | copy-start | bytes 9220
  142.2 132.0 %reduce-scatter.12.cloned.1.call-start = ((), (), s32[]{:S(2)}) async-start(), calls=%async_computation.10 | async-start | bytes 442368
  194.4 6.1 %slice-start = ((s8[7372800]{0:T(1024)(128)(4,1)}), s8[4194304]{0:T(1024)(128)(4,1)S(1)}, s32[]{:S(2)}) async-start(s8[7372800]{0:T(1024)(128)(4,1)} %bitcast.205), calls=%async_computation.11 | async-start | bytes 8388608
  196.4 4.1 copy-start.4
  196.5 4.1 slice-start.1
  196.5 4.2 copy-start.3
  196.5 4.1 copy-start.13
  200.6 5.3 copy-start.40
  221.8 5.4 %slice-start.2 = ((s8[4718592]{0:T(1024)(128)(4,1)}), s8[4194304]{0:T(1024)(128)(4,1)S(1)}, s32[]{:S(2)}) async-start(s8[4718592]{0:T(1024)(128)(4,1)} %bitcast.231), calls=%async_computation.13 | async-start | bytes 8388608
  227.3 7.3 %copy-start.7 = (bf16[4,3,197,3,3,64]{2,5,4,3,1,0:T(8,128)(2,1)}, bf16[4,3,197,3,3,64]{2,5,4,3,1,0:T(8,128)(2,1)S(1)}, u32[]{:S(2)}) copy-start(bf16[4,3,197,3,3,64]{2,5,4,3,1,0:T(8,128)(2,1)S(1)} %copy.144) | copy-start | bytes 8169988
  227.5 7.1 %copy-start.33 = (f32[768]{0:T(1024)S(1)}, f32[768]{0:T(1024)}, u32[]{:S(2)}) copy-start(f32[768]{0:T(1024)} %get-tuple-element.52) | copy-start | bytes 9220
  227.5 7.1 %copy-start.32 = (f32[768]{0:T(1024)S(1)}, f32[768]{0:T(1024)}, u32[]{:S(2)}) copy-start(f32[768]{0:T(1024)} %get-tuple-element.56) | copy-start | bytes 9220
  227.5 7.1 %copy-start.29 = (f32[8]{0:T(128)S(1)}, f32[8]{0:T(128)}, u32[]{:S(2)}) copy-start(f32[8]{0:T(128)} %copy-done.27) | copy-start | bytes 100
  227.5 7.1 %copy-start.36 = (f32[8]{0:T(128)S(1)}, f32[8]{0:T(128)}, u32[]{:S(2)}) copy-start(f32[8]{0:T(128)} %get-tuple-element.90) | copy-start | bytes 100
  227.5 8.4 %copy-start.5 = (f32[3,197,768]{2,1,0:T(8,128)S(1)}, f32[3,197,768]{2,1,0:T(8,128)}, u32[]{:S(2)}) copy-start(f32[3,197,768]{2,1,0:T(8,128)} %copy-done.4) | copy-start | bytes 5446660
  235.8 105.0 %all-gather.10.cloned.1.call-start = ((), (), s32[]{:S(2)}) async-start(), calls=%async_computation.7 | async-start | bytes 4608000 | tf_op jit(solution)/shard_map/all_gather | solution.py:158
  239.2 173.9 %all-gather.8.cloned.1.call-start = ((), (), s32[]{:S(2)}) async-start(), calls=%async_computation.6 | async-start | bytes 4608000 | tf_op jit(solution)/shard_map/all_gather | solution.py:129
  239.8 284.7 %reduce-scatter.8.cloned.1.call-start = ((), (), s32[]{:S(2)}) async-start(), calls=%async_computation.8 | async-start | bytes 4866048 | tf_op jit(solution)/shard_map/reduce_scatter | solution.py:162
  528.2 4.3 copy-start.6
  (21 other events, 41.7 us)
Sparse Core Ops, SparseCore 0:
  11.5 66.2 all-gather.5
  142.3 16.6 reduce-scatter.9
  235.9 30.2 reduce-scatter.11
  268.2 72.5 all-gather.9
  342.2 70.8 all-gather.7
  418.4 106.0 reduce-scatter.7

commit v2 on v1

v2 whole, which is shorter than its diff:
```python
import functools
import math

import jax
import jax.numpy as jnp
from jax import lax
from jax.experimental import pallas as pl
from jax.experimental.pallas import tpu as pltpu
from jax.sharding import PartitionSpec as P

f32 = jnp.float32
bf16 = jnp.bfloat16

HEAD_DIM = 64
norm_eps = 1e-06
highest = lax.Precision.HIGHEST
NN = (((1,), (0,)), ((), ()))
NT = (((1,), (1,)), ((), ()))
TN = (((0,), (0,)), ((), ()))


def mm(a, b, dims=NN, precision=None):
    return lax.dot_general(a, b, dims, precision=precision, preferred_element_type=f32)


def layer_stats(values):
    center = values - jnp.mean(values, axis=-1, keepdims=True)
    spread = lax.rsqrt(jnp.mean(center * center, axis=-1, keepdims=True) + norm_eps)
    return (center * spread, spread)


def norm_back(upstream, scaled, spread):
    return spread * (
        upstream
        - jnp.mean(upstream, axis=-1, keepdims=True)
        - scaled * jnp.mean(upstream * scaled, axis=-1, keepdims=True)
    )


def soft(values, axis):
    e = jnp.exp(values - jnp.max(values, axis=axis, keepdims=True))
    return e / jnp.sum(e, axis=axis, keepdims=True)


def pick_rows(slots_n, row):
    r = lax.broadcasted_iota(jnp.int32, (slots_n * 8, slots_n), 0)
    s = lax.broadcasted_iota(jnp.int32, (slots_n * 8, slots_n), 1)
    return jnp.where(r == s * 8 + row, 1.0, 0.0).astype(bf16)


def router_unit(keys):
    scale = lax.rsqrt(jnp.sum(keys * keys, axis=1, keepdims=True) + norm_eps)
    return keys * scale, scale


def head_parts(block, h, per):
    at = [j * per * HEAD_DIM + h * HEAD_DIM for j in range(3)]
    return [block[:, a : a + HEAD_DIM] for a in at]


def forward_kernel(share, x_all, g_all, full, small, qkv, heads, resid, logits, asq, send, x_s, g_s, rows_s, sems):
    c0 = lax.axis_index("context") * share
    ctx_n, width, packed = full.shape
    cols = packed // 4
    per = cols // HEAD_DIM
    slots_n = small.shape[0] - 4
    length = x_s.shape[1]
    ins = [
        pltpu.make_async_copy(x_all.at[pl.ds(c0, share)], x_s, sems.at[0]),
        pltpu.make_async_copy(g_all.at[pl.ds(c0, share)], g_s, sems.at[1]),
    ]
    for cp in ins:
        cp.start()
    rows_s[...] = jnp.zeros_like(rows_s)
    keys, _ = router_unit(small[4:, :].astype(f32))
    logit_scale = 1.6 * math.sqrt(width)
    for cp in ins:
        cp.wait()

    def image(i, carry):
        x = x_s[i].astype(f32)
        hat, spread = layer_stats(x)
        normed = (hat * small[0:1, :].astype(f32) + small[2:3, :].astype(f32)).astype(bf16)
        resid[i] = x

        def block(cb, carry):
            qkv_c = mm(normed, full[cb, :, : 3 * cols]).astype(bf16)
            qkv[i, cb] = qkv_c
            mixed = []
            for h in range(per):
                q, k, v = head_parts(qkv_c, h, per)
                p = soft(mm(q, k, NT) * 0.125, 1)
                mixed.append(mm(p.astype(bf16), v).astype(bf16))
            heads_c = jnp.concatenate(mixed, axis=1)
            heads[i, cb] = heads_c
            resid[i] += mm(heads_c, full[cb, :, 3 * cols :], NT)
            return carry

        lax.fori_loop(0, ctx_n, block, 0)
        res = resid[i]
        att = res - x
        asq[i] = jnp.full(asq.shape[1:], jnp.sum(att * att), f32)
        hat2, _ = layer_stats(res)
        second = hat2 * small[1:2, :].astype(f32) + small[3:4, :].astype(f32)
        unit = second * lax.rsqrt(jnp.sum(second * second, axis=-1, keepdims=True) + norm_eps)
        lg = logit_scale * mm(keys, unit, NT, highest)
        logits[i] = lg
        disp = soft(lg, 1).astype(bf16)
        comb = soft(lg, 0).astype(bf16)
        slots = mm(disp, second.astype(bf16)).astype(bf16)
        dexp = mm(comb, g_s[i]).astype(bf16)
        rows_s[...] += mm(pick_rows(slots_n, i), slots) + mm(pick_rows(slots_n, i + 4), dexp)
        return carry

    lax.fori_loop(0, share, image, 0)
    send[...] = rows_s[...].astype(bf16)


def run_forward(x_all, g_all, full, small, share):
    ctx_n, width, packed = full.shape
    length = x_all.shape[1]
    cols = packed // 4
    slots_n = small.shape[0] - 4
    vm = pl.BlockSpec(memory_space=pltpu.VMEM)
    hbm = pl.BlockSpec(memory_space=pl.ANY)
    return pl.pallas_call(
        functools.partial(forward_kernel, share),
        out_shape=(
            jax.ShapeDtypeStruct((share, ctx_n, length, 3 * cols), bf16),
            jax.ShapeDtypeStruct((share, ctx_n, length, cols), bf16),
            jax.ShapeDtypeStruct((share, length, width), f32),
            jax.ShapeDtypeStruct((share, slots_n, length), f32),
            jax.ShapeDtypeStruct((share, 8, 128), f32),
            jax.ShapeDtypeStruct((slots_n * 8, width), bf16),
        ),
        in_specs=[hbm, hbm, vm, vm],
        out_specs=(vm,) * 6,
        scratch_shapes=[
            pltpu.VMEM((share, length, width), bf16),
            pltpu.VMEM((share, length, width), bf16),
            pltpu.VMEM((slots_n * 8, width), f32),
            pltpu.SemaphoreType.DMA((2,)),
        ],
        compiler_params=pltpu.CompilerParams(vmem_limit_bytes=60 << 20),
    )(x_all, g_all, full, small)


def backward_kernel(share, x_all, g_all, full, small, qkv, heads, resid, logits, asq, back, low_out, dx, dfull, dsmall, rms, x_s, g_s, acc, dres_s, dn_s, sems):
    c0 = lax.axis_index("context") * share
    ctx_n, width, packed = full.shape
    cols = packed // 4
    per = cols // HEAD_DIM
    slots_n = small.shape[0] - 4
    length = x_s.shape[1]
    ins = [
        pltpu.make_async_copy(x_all.at[pl.ds(c0, share)], x_s, sems.at[0]),
        pltpu.make_async_copy(g_all.at[pl.ds(c0, share)], g_s, sems.at[1]),
    ]
    for cp in ins:
        cp.start()
    acc[...] = jnp.zeros_like(acc)
    dsmall[...] = jnp.zeros_like(dsmall)
    keys, key_scale = router_unit(small[4:, :].astype(f32))
    logit_scale = 1.6 * math.sqrt(width)
    for cp in ins:
        cp.wait()

    def image(i, carry):
        gain1, gain2 = small[0:1, :].astype(f32), small[1:2, :].astype(f32)
        g_low = g_s[i]
        res = resid[i]
        hat2, spread2 = layer_stats(res)
        second = hat2 * gain2 + small[3:4, :].astype(f32)
        tokens = second.astype(bf16)
        row_scale = lax.rsqrt(jnp.sum(second * second, axis=-1, keepdims=True) + norm_eps)
        unit = second * row_scale
        eo = mm(pick_rows(slots_n, i), back[...], TN).astype(bf16)
        ds = mm(pick_rows(slots_n, i + 4), back[...], TN).astype(bf16)
        lg = logits[i]
        disp = soft(lg, 1)
        comb = soft(lg, 0)
        mixture = mm(comb.astype(bf16), eo, TN)
        result = res + mixture
        low_out[i] = result.astype(bf16)
        count = 1.0 / (length * width)
        lane = lax.broadcasted_iota(jnp.int32, rms.shape[1:], 1)
        total = jnp.where(
            lane == 0,
            jnp.sum(result * result),
            jnp.where(lane == 1, asq[i], jnp.sum(mixture * mixture)),
        )
        rms[i] = jnp.sqrt(total * count)
        dcomb = mm(eo, g_low, NT)
        ddisp = mm(ds, tokens, NT)
        dtok = mm(disp.astype(bf16), ds, TN)
        dlg = comb * (dcomb - jnp.sum(comb * dcomb, axis=0, keepdims=True)) + disp * (
            ddisp - jnp.sum(disp * ddisp, axis=1, keepdims=True)
        )
        dunit = logit_scale * mm(dlg, keys, TN, highest)
        dsmall[4 : 4 + slots_n, :] += logit_scale * mm(dlg, unit, NN, highest)
        dsec = dtok + row_scale * (dunit - unit * jnp.sum(unit * dunit, axis=-1, keepdims=True))
        dsmall[1:2, :] += jnp.sum(dsec * hat2, axis=0, keepdims=True)
        dsmall[3:4, :] += jnp.sum(dsec, axis=0, keepdims=True)
        dres = g_low.astype(f32) + norm_back(dsec * gain2, hat2, spread2)
        dres_s[...] = dres
        dattn = dres.astype(bf16)
        dattn_t = dattn.T
        hat, spread = layer_stats(x_s[i].astype(f32))
        normed = (hat * gain1 + small[2:3, :].astype(f32)).astype(bf16)
        normed_t = normed.T
        dn_s[...] = jnp.zeros_like(dn_s)

        def block(cb, carry):
            proj = full[cb, :, 3 * cols :]
            dheads = mm(dattn, proj).astype(bf16)
            acc[cb, :, 3 * cols :] += mm(dattn_t, heads[i, cb])
            qkv_c = qkv[i, cb]
            grads = [[], [], []]
            for h in range(per):
                q, k, v = head_parts(qkv_c, h, per)
                dh = dheads[:, h * HEAD_DIM : (h + 1) * HEAD_DIM]
                p = soft(mm(q, k, NT) * 0.125, 1)
                dp = mm(dh, v, NT)
                dsc = (p * (dp - jnp.sum(p * dp, axis=1, keepdims=True))).astype(bf16)
                grads[0].append((mm(dsc, k) * 0.125).astype(bf16))
                grads[1].append((mm(dsc, q, TN) * 0.125).astype(bf16))
                grads[2].append(mm(p.astype(bf16), dh, TN).astype(bf16))
            dqkv = jnp.concatenate(grads[0] + grads[1] + grads[2], axis=1)
            acc[cb, :, : 3 * cols] += mm(normed_t, dqkv)
            dn_s[...] += mm(dqkv, full[cb, :, : 3 * cols], NT)
            return carry

        lax.fori_loop(0, ctx_n, block, 0)
        dn = dn_s[...]
        dsmall[0:1, :] += jnp.sum(dn * hat, axis=0, keepdims=True)
        dsmall[2:3, :] += jnp.sum(dn, axis=0, keepdims=True)
        dx[i] = (dres_s[...] + norm_back(dn * gain1, hat, spread)).astype(bf16)
        return carry

    lax.fori_loop(0, share, image, 0)
    dkeys = dsmall[4 : 4 + slots_n, :]
    dsmall[4 : 4 + slots_n, :] = key_scale * (dkeys - keys * jnp.sum(keys * dkeys, axis=1, keepdims=True))
    for cb in range(ctx_n):
        dfull[cb] = acc[cb].astype(bf16)


def run_backward(x_all, g_all, full, small, saved, back, share):
    ctx_n, width, packed = full.shape
    length = x_all.shape[1]
    slots_n = small.shape[0] - 4
    vm = pl.BlockSpec(memory_space=pltpu.VMEM)
    hbm = pl.BlockSpec(memory_space=pl.ANY)
    acts = jax.ShapeDtypeStruct((share, length, width), bf16)
    return pl.pallas_call(
        functools.partial(backward_kernel, share),
        out_shape=(
            acts,
            acts,
            jax.ShapeDtypeStruct((ctx_n, width, packed), bf16),
            jax.ShapeDtypeStruct((4 + slots_n + -(4 + slots_n) % 8, width), f32),
            jax.ShapeDtypeStruct((share, 8, 128), f32),
        ),
        in_specs=[hbm, hbm] + [vm] * 8,
        out_specs=(vm,) * 5,
        scratch_shapes=[
            pltpu.VMEM((share, length, width), bf16),
            pltpu.VMEM((share, length, width), bf16),
            pltpu.VMEM((ctx_n, width, packed), f32),
            pltpu.VMEM((length, width), f32),
            pltpu.VMEM((length, width), f32),
            pltpu.SemaphoreType.DMA((2,)),
        ],
        compiler_params=pltpu.CompilerParams(vmem_limit_bytes=60 << 20),
    )(x_all, g_all, full, small, *saved, back)


def remote(src, dst, ssem, rsem, **where):
    return pltpu.make_async_remote_copy(
        src_ref=src,
        dst_ref=dst,
        send_sem=ssem,
        recv_sem=rsem,
        device_id=where,
        device_id_type=pl.DeviceIdType.MESH,
    )


def spot():
    wide_n, ctx_n, ten_n = (lax.axis_size(a) for a in ("wide", "context", "tensor"))
    w, c, t = (lax.axis_index(a) for a in ("wide", "context", "tensor"))
    return wide_n, ctx_n, ten_n // 2, w, c, t // 2, lax.rem(t, 2)


def greet_plane(bar, wide_n, y_n, w, y, k):
    for o in range(1, wide_n * y_n * 2):
        j = lax.rem((w * y_n + y) * 2 + k + o, wide_n * y_n * 2)
        pl.semaphore_signal(
            bar,
            inc=1,
            device_id={"wide": j // (y_n * 2), "tensor": lax.rem(j, y_n * 2)},
            device_id_type=pl.DeviceIdType.MESH,
        )
    return wide_n * y_n * 2 - 1


def near_first(c, ctx_n):
    seq = []
    for j in range(ctx_n):
        cb = 0
        for p in range(ctx_n):
            order = sorted(range(ctx_n), key=lambda q: (abs(q - p), q))
            cb = jnp.where(c == p, order[j], cb)
        seq.append(cb)
    return seq


def gather_kernel(pack, small, full, smalls, csem, crecv, wsem, wrecv, ysem, yrecv, ksem, krecv, ssem, srecv, local):
    wide_n, ctx_n, y_n, w, c, y, k = spot()
    bar = pltpu.get_barrier_semaphore()
    met = greet_plane(bar, wide_n, y_n, w, y, k)

    @pl.when(c > 0)
    def _():
        pl.semaphore_signal(bar, inc=1, device_id={"context": c - 1}, device_id_type=pl.DeviceIdType.MESH)

    @pl.when(c < ctx_n - 1)
    def _():
        pl.semaphore_signal(bar, inc=1, device_id={"context": c + 1}, device_id_type=pl.DeviceIdType.MESH)

    mine = pltpu.make_async_copy(pack, full.at[c, w, y, k], local.at[0])
    mine_small = pltpu.make_async_copy(small, smalls.at[w, y, k], local.at[1])
    mine.start()
    mine_small.start()
    pl.semaphore_wait(bar, met + (c + ctx_n - 1) // ctx_n + (2 * ctx_n - 2 - c) // ctx_n)

    def along(cb, side, src):
        return remote(src, full.at[cb, w, y, k], csem.at[side, cb], crecv.at[cb], context=c + 2 * side - 1)

    for side in (0, 1):

        @pl.when((c > 0) if side == 0 else (c < ctx_n - 1))
        def _():
            along(c, side, pack).start()

    def small_copy(o):
        j = lax.rem((w * y_n + y) * 2 + k + o, wide_n * y_n * 2)
        return remote(
            small, smalls.at[w, y, k], ssem.at[o], srecv.at[o], wide=j // (y_n * 2), tensor=lax.rem(j, y_n * 2)
        )

    for o in range(1, wide_n * y_n * 2):
        small_copy(o).start()

    seq = near_first(c, ctx_n)

    def leg(cb, number, o, start):
        even = lax.rem(cb, 2) == 0
        for on_wide in (True, False):
            n = wide_n if on_wide else y_n
            if o >= n:
                continue
            first = number == 0
            want_even = on_wide == first

            @pl.when(even if want_even else jnp.logical_not(even))
            def _():
                if on_wide:
                    ref = full.at[cb, w, y, k] if first else full.at[cb, w, :, k]
                    to = {"wide": lax.rem(w + o, wide_n)}
                    sems = (wsem.at[cb, o], wrecv.at[cb, o])
                else:
                    ref = full.at[cb, w, y, k] if first else full.at[cb, :, y, k]
                    to = {"tensor": lax.rem(y + o, y_n) * 2 + k}
                    sems = (ysem.at[cb, o], yrecv.at[cb, o])
                cp = remote(ref, ref, *sems, **to)
                if start == "start":
                    cp.start()
                elif start == "recv":
                    cp.wait_recv()
                else:
                    cp.wait_send()

    most = max(wide_n, y_n)

    def core(cb):
        ref = full.at[cb, :, :, k]
        return remote(ref, ref, ksem.at[cb], krecv.at[cb], tensor=y * 2 + 1 - k)

    mine.wait()
    mine_small.wait()
    for step in range(ctx_n + 2):
        if step < ctx_n:
            cb = seq[step]
            if step > 0:
                along(cb, 0, pack).wait_recv()
                for side in (0, 1):
                    go = jnp.logical_and(cb > c, c > 0) if side == 0 else jnp.logical_and(cb < c, c < ctx_n - 1)

                    @pl.when(go)
                    def _():
                        along(cb, side, full.at[cb, w, y, k]).start()

            for o in range(1, most):
                leg(cb, 0, o, "start")
        if 0 < step <= ctx_n:
            cb = seq[step - 1]
            for o in range(1, most):
                leg(cb, 0, o, "recv")
            for o in range(1, most):
                leg(cb, 1, o, "start")
        if step > 1:
            cb = seq[step - 2]
            for o in range(1, most):
                leg(cb, 1, o, "recv")
            core(cb).start()
    for step in range(ctx_n):
        core(seq[step]).wait_recv()
    for o in range(1, wide_n * y_n * 2):
        cp = small_copy(o)
        cp.wait_recv()
        cp.wait_send()
    for step in range(ctx_n):
        cb = seq[step]
        for side in (0, 1):
            go = jnp.logical_and(cb >= c, c > 0) if side == 0 else jnp.logical_and(cb <= c, c < ctx_n - 1)

            @pl.when(go)
            def _():
                along(cb, side, pack).wait_send()

        for number in (0, 1):
            for o in range(1, most):
                leg(cb, number, o, "send")
        core(cb).wait_send()


def gather_weights(pack, small):
    wide_n, ctx_n, ten_n = (lax.axis_size(a) for a in ("wide", "context", "tensor"))
    y_n = ten_n // 2
    dma = pltpu.SemaphoreType.DMA
    vm = pl.BlockSpec(memory_space=pltpu.VMEM)
    return pl.pallas_call(
        gather_kernel,
        out_shape=(
            jax.ShapeDtypeStruct((ctx_n, wide_n, y_n, 2) + pack.shape, pack.dtype),
            jax.ShapeDtypeStruct((wide_n, y_n, 2) + small.shape, small.dtype),
        ),
        in_specs=[vm, vm],
        out_specs=(vm, vm),
        scratch_shapes=[
            dma((2, ctx_n)), dma((ctx_n,)),
            dma((ctx_n, wide_n)), dma((ctx_n, wide_n)),
            dma((ctx_n, y_n)), dma((ctx_n, y_n)),
            dma((ctx_n,)), dma((ctx_n,)),
            dma((wide_n * ten_n,)), dma((wide_n * ten_n,)),
            dma((2,)),
        ],
        compiler_params=pltpu.CompilerParams(collective_id=1, has_side_effects=True),
    )(pack, small)


def gelu_parts(x):
    a = 0.7978845608028654
    x2 = x * x
    th = jnp.tanh(a * x * (1.0 + 0.044715 * x2))
    val = 0.5 * x * (1.0 + th)
    der = 0.5 * (1.0 + th) + 0.5 * x * (1.0 - th * th) * (a * (1.0 + 3 * 0.044715 * x2))
    return val, der


def expert_kernel(share, out, up, down, back, up_grad, down_grad, got, r32, ret, got2, sems):
    wide_n, ctx_n, y_n, w, c, y, k = spot()
    ten_n = y_n * 2
    n = wide_n * ctx_n * ten_n
    me = (w * ctx_n + c) * ten_n + y * 2 + k
    bar = pltpu.get_barrier_semaphore()

    def place(d):
        return {"wide": d // (ctx_n * ten_n), "context": lax.rem(d // ten_n, ctx_n), "tensor": lax.rem(d, ten_n)}

    def hello(o, _):
        pl.semaphore_signal(bar, inc=1, device_id=place(lax.rem(me + o, n)), device_id_type=pl.DeviceIdType.MESH)
        return _

    lax.fori_loop(1, n, hello, 0)
    got[me] = out[w * ctx_n + c]
    pl.semaphore_wait(bar, n - 1)

    def send_out(o, _):
        d = lax.rem(me + o, n)
        remote(out.at[d // ten_n], got.at[me], sems.at[0], sems.at[1], **place(d)).start()
        return _

    lax.fori_loop(1, n, send_out, 0)

    def drain(ref, sem):
        part = ref.at[pl.ds(0, n - 1)]
        pltpu.make_async_copy(part, part, sem).wait()

    drain(got, sems.at[1])

    def widen(i, _):
        r32[pl.ds(pl.multiple_of(i * 8, 8), 8), :] = got[i].astype(f32)
        return _

    lax.fori_loop(0, n, widen, 0)
    rows = n * 8
    low = r32[...].astype(bf16)
    first = lax.rem(lax.broadcasted_iota(jnp.int32, (rows, 1), 0), 8) < 4
    hidden = jnp.dot(low, up[...], preferred_element_type=f32)
    act_g = lax.dot_general(low, down[...], (((1,), (1,)), ((), ())), preferred_element_type=f32)
    act_g = pltpu.roll(act_g, rows - 4, 0)
    val, der = gelu_parts(hidden)
    active = jnp.where(first, val, 0.0).astype(bf16)
    hid_g = jnp.where(first, act_g * der, 0.0).astype(bf16)
    part_o = jnp.dot(active, down[...], preferred_element_type=f32)
    part_s = lax.dot_general(hid_g, up[...], (((1,), (1,)), ((), ())), preferred_element_type=f32)
    dexp = pltpu.roll(r32[...], rows - 4, 0).astype(bf16)
    r32[...] = jnp.where(first, part_o, pltpu.roll(part_s, 4, 0))

    def narrow(i, _):
        ret[i] = r32[pl.ds(pl.multiple_of(i * 8, 8), 8), :].astype(bf16)
        return _

    lax.fori_loop(0, n, narrow, 0)

    def send_back(o, _):
        d = lax.rem(me + o, n)
        remote(ret.at[d], got2.at[me], sems.at[2], sems.at[3], **place(d)).start()
        return _

    lax.fori_loop(1, n, send_back, 0)
    got2[me] = ret[me]
    tn = (((0,), (0,)), ((), ()))
    up_grad[...] = lax.dot_general(low, hid_g, tn, preferred_element_type=f32)
    down_grad[...] = lax.dot_general(active, dexp, tn, preferred_element_type=f32)
    drain(got2, sems.at[3])

    def total(e, _):
        s = got2[e * ten_n].astype(f32)
        for t in range(1, ten_n):
            s = s + got2[e * ten_n + t].astype(f32)
        back[e] = s.astype(bf16)
        return _

    lax.fori_loop(0, wide_n * ctx_n, total, 0)
    drain(ret, sems.at[2])

    def sent(o, _):
        pltpu.make_async_copy(out.at[0], out.at[0], sems.at[0]).wait()
        return _

    lax.fori_loop(1, n, sent, 0)


def run_experts(out, up, down, share):
    wide_n, ctx_n, ten_n = (lax.axis_size(a) for a in ("wide", "context", "tensor"))
    n = wide_n * ctx_n * ten_n
    width, ff = up.shape
    vm = pl.BlockSpec(memory_space=pltpu.VMEM)
    return pl.pallas_call(
        functools.partial(expert_kernel, share),
        out_shape=(
            jax.ShapeDtypeStruct(out.shape, bf16),
            jax.ShapeDtypeStruct((width, ff), f32),
            jax.ShapeDtypeStruct((ff, width), f32),
        ),
        in_specs=[vm, vm, vm],
        out_specs=(vm, vm, vm),
        scratch_shapes=[
            pltpu.VMEM((n, 8, width), bf16),
            pltpu.VMEM((n * 8, width), f32),
            pltpu.VMEM((n, 8, width), bf16),
            pltpu.VMEM((n, 8, width), bf16),
            pltpu.SemaphoreType.DMA((4,)),
        ],
        compiler_params=pltpu.CompilerParams(collective_id=2, has_side_effects=True),
    )(out, up, down)


def tail_kernel(n_arr, share, *refs):
    arrs = refs[:n_arr]
    part, small = refs[n_arr : n_arr + 2]
    outs = refs[n_arr + 2 : 2 * n_arr + 2]
    grad, smalls = refs[2 * n_arr + 2 : 2 * n_arr + 4]
    (rcv1, acc1, rcv2, acc2, rcv3, acc3, rcv4, srcv, gsem, grecv, lsem, ksem, krecv, s2, r2, s3, r3, s4, r4, ss, sr) = refs[2 * n_arr + 4 :]
    wide_n, ctx_n, y_n, w, c, y, k = spot()
    ten_n = 2 * y_n
    plane = wide_n * ten_n
    bar = pltpu.get_barrier_semaphore()
    met = greet_plane(bar, wide_n, y_n, w, y, k)
    for o in range(1, ctx_n):
        pl.semaphore_signal(bar, inc=1, device_id={"context": lax.rem(c + o, ctx_n)}, device_id_type=pl.DeviceIdType.MESH)
    own = []
    for a in range(n_arr):
        cp = pltpu.make_async_copy(arrs[a], outs[a].at[pl.ds(c * share, share)], lsem.at[a])
        cp.start()
        own.append(cp)
    pl.semaphore_wait(bar, met + ctx_n - 1)

    def along(a, cb, i, side, src=None):
        ref = outs[a].at[cb * share + i]
        return remote(ref if src is None else src, ref, gsem.at[a, side, cb, i], grecv.at[a, cb, i], context=c + 2 * side - 1)

    for a in range(n_arr):
        for i in range(share):
            for side in (0, 1):

                @pl.when((c > 0) if side == 0 else (c < ctx_n - 1))
                def _():
                    along(a, c, i, side, arrs[a].at[i]).start()

    me = (w * y_n + y) * 2 + k

    def small1(o):
        j = lax.rem(me + o, plane)
        return remote(small.at[j], srcv.at[o], ss.at[o], sr.at[o], wide=j // ten_n, tensor=lax.rem(j, ten_n))

    for o in range(1, plane):
        small1(o).start()

    def core(cc):
        return remote(part.at[cc, :, :, 1 - k], rcv1.at[cc], ksem.at[cc], krecv.at[cc], tensor=y * 2 + 1 - k)

    for cc in range(ctx_n):
        core(cc).start()

    def hop(cc, number, o):
        on_wide = (cc % 2 == 0) == (number == 2)
        src = acc1 if number == 2 else acc2
        dst = rcv2 if number == 2 else rcv3
        ss_, rr_ = (s2, r2) if number == 2 else (s3, r3)
        if on_wide:
            p = lax.rem(w + o, wide_n)
            to = {"wide": p}
            if number == 2:
                frm = src.at[cc, p]
                into = dst.at[cc, o, pl.ds(0, y_n)]
            else:
                frm = src.at[cc, p]
                into = dst.at[cc, o]
        else:
            p = lax.rem(y + o, y_n)
            to = {"tensor": p * 2 + k}
            if number == 2:
                frm = src.at[cc, :, p]
                into = dst.at[cc, o, pl.ds(0, wide_n)]
            else:
                frm = src.at[cc, p]
                into = dst.at[cc, o]
        return remote(frm, into, ss_.at[cc, o], rr_.at[cc, o], **to)

    def peers(cc, number):
        on_wide = (cc % 2 == 0) == (number == 2)
        return range(1, wide_n if on_wide else y_n)

    for cc in range(ctx_n):
        core(cc).wait_recv()
        for wi in range(wide_n):
            for yi in range(y_n):
                acc1[cc, wi, yi] = (part[cc, wi, yi, k].astype(f32) + rcv1[cc, wi, yi].astype(f32)).astype(bf16)
        for o in peers(cc, 2):
            hop(cc, 2, o).start()

    acc = small[me]
    for o in range(1, plane):
        small1(o).wait_recv()
        acc = acc + srcv[o]
    smalls[c] = acc

    def small2(o):
        return remote(smalls.at[c], smalls.at[c], ss.at[plane + o], sr.at[plane + o], context=lax.rem(c + o, ctx_n))

    def small2_in(o):
        ref = smalls.at[lax.rem(c + ctx_n - o, ctx_n)]
        return remote(ref, ref, ss.at[plane + o], sr.at[plane + o], context=lax.rem(c + o, ctx_n))

    for o in range(1, ctx_n):
        small2(o).start()

    def forward(step):
        cb = near_first(c, ctx_n)[step]
        for a in range(n_arr):
            for i in range(share):
                along(a, cb, i, 0).wait_recv()
                for side in (0, 1):
                    go = jnp.logical_and(cb > c, c > 0) if side == 0 else jnp.logical_and(cb < c, c < ctx_n - 1)

                    @pl.when(go)
                    def _():
                        along(a, cb, i, side).start()

    if ctx_n > 1:
        forward(1)
    for cc in range(ctx_n):
        on_wide = cc % 2 == 0
        for o in peers(cc, 2):
            hop(cc, 2, o).wait_recv()
        for j in range(y_n if on_wide else wide_n):
            tot = (acc1[cc, w, j] if on_wide else acc1[cc, j, y]).astype(f32)
            for o in peers(cc, 2):
                tot = tot + rcv2[cc, o, j].astype(f32)
            acc2[cc, j] = tot.astype(bf16)
        for o in peers(cc, 3):
            hop(cc, 3, o).start()
    if ctx_n > 2:
        forward(2)

    def last(cc):
        return remote(acc3.at[cc], rcv4.at[c], s4.at[cc], r4.at[c], context=cc)

    for cc in range(ctx_n):
        for o in peers(cc, 3):
            hop(cc, 3, o).wait_recv()
        tot = (acc2[cc, y] if cc % 2 == 0 else acc2[cc, w]).astype(f32)
        for o in peers(cc, 3):
            tot = tot + rcv3[cc, o].astype(f32)
        acc3[cc] = tot.astype(bf16)

        @pl.when(c != cc)
        def _():
            last(cc).start()

    for step in range(3, ctx_n):
        forward(step)
    tot = acc3[c].astype(f32)
    for o in range(1, ctx_n):
        p = lax.rem(c + o, ctx_n)
        remote(acc3.at[0], rcv4.at[p], s4.at[p], r4.at[p], context=p).wait_recv()
        tot = tot + rcv4[p].astype(f32)
    grad[...] = tot
    for o in range(1, ctx_n):
        small2_in(o).wait_recv()
        small2(o).wait_send()
        p = lax.rem(c + o, ctx_n)
        last(p).wait_send()
    for o in range(1, plane):
        small1(o).wait_send()
    for cc in range(ctx_n):
        core(cc).wait_send()
        for number in (2, 3):
            for o in peers(cc, number):
                hop(cc, number, o).wait_send()
    for a in range(n_arr):
        own[a].wait()
        for cb in range(ctx_n):
            for i in range(share):
                for side in (0, 1):
                    go = jnp.logical_and(c <= cb, c > 0) if side == 0 else jnp.logical_and(c >= cb, c < ctx_n - 1)

                    @pl.when(go)
                    def _():
                        along(a, cb, i, side).wait_send()


def finish(arrs, part, small, share):
    wide_n, ctx_n, ten_n = (lax.axis_size(a) for a in ("wide", "context", "tensor"))
    y_n = ten_n // 2
    most = max(wide_n, y_n)
    blk = part.shape[-2:]
    dma = pltpu.SemaphoreType.DMA
    vm = pl.BlockSpec(memory_space=pltpu.VMEM)
    hbm = pl.BlockSpec(memory_space=pl.ANY)
    n_arr = len(arrs)
    return pl.pallas_call(
        functools.partial(tail_kernel, n_arr, share),
        out_shape=tuple(
            jax.ShapeDtypeStruct((a.shape[0] * ctx_n,) + a.shape[1:], a.dtype) for a in arrs
        )
        + (
            jax.ShapeDtypeStruct(blk, f32),
            jax.ShapeDtypeStruct((ctx_n,) + small.shape[1:], f32),
        ),
        in_specs=[vm] * n_arr + [vm, vm],
        out_specs=(hbm,) * n_arr + (vm, vm),
        scratch_shapes=[
            pltpu.VMEM((ctx_n, wide_n, y_n) + blk, bf16),
            pltpu.VMEM((ctx_n, wide_n, y_n) + blk, bf16),
            pltpu.VMEM((ctx_n, most, most) + blk, bf16),
            pltpu.VMEM((ctx_n, most) + blk, bf16),
            pltpu.VMEM((ctx_n, most) + blk, bf16),
            pltpu.VMEM((ctx_n,) + blk, bf16),
            pltpu.VMEM((ctx_n,) + blk, bf16),
            pltpu.VMEM((wide_n * ten_n,) + small.shape[1:], f32),
            dma((n_arr, 2, ctx_n, share)), dma((n_arr, ctx_n, share)), dma((n_arr,)),
            dma((ctx_n,)), dma((ctx_n,)),
            dma((ctx_n, most)), dma((ctx_n, most)),
            dma((ctx_n, most)), dma((ctx_n, most)),
            dma((ctx_n,)), dma((ctx_n,)),
            dma((wide_n * ten_n + ctx_n,)), dma((wide_n * ten_n + ctx_n,)),
        ],
        compiler_params=pltpu.CompilerParams(collective_id=3, has_side_effects=True),
    )(*arrs, part, small)


def on_device(
    layer_input,
    qkv_weight,
    proj_weight,
    norm_gains,
    norm_biases,
    router_keys,
    up_weight,
    down_weight,
    out_cotangent,
):
    images, length, width = layer_input.shape
    wide_n, ctx_n, ten_n = (lax.axis_size(a) for a in ("wide", "context", "tensor"))
    share = images // ctx_n
    slots_n = router_keys.shape[1]
    rows, _, cols = qkv_weight.shape
    plane = wide_n * ten_n
    lanes = rows + -rows % 128

    pack = jnp.concatenate([qkv_weight.reshape(rows, 3 * cols), proj_weight.T], axis=1)
    small = jnp.concatenate([norm_gains, norm_biases, router_keys.T], axis=0)
    params = small.shape[0]
    small = jnp.pad(small, ((0, -params % 16), (0, lanes - rows)))
    weights, small = gather_weights(pack, small)
    weights = weights.reshape(ctx_n, width, 4 * cols)
    small = small.reshape((-1,) + small.shape[3:])[:, :params, :rows]
    small = small.transpose(1, 0, 2).reshape(params, width)
    *saved, send = run_forward(layer_input, out_cotangent, weights, small, share)
    back, up_grad, down_grad = run_experts(
        send.reshape(slots_n, 8, width), up_weight[0], down_weight[0], share
    )
    back = back.reshape(slots_n * 8, width)
    low, dx, dpack, dsmall, rms = run_backward(
        layer_input, out_cotangent, weights, small, saved, back, share
    )
    dpack = dpack.reshape(ctx_n, wide_n, ten_n // 2, 2, rows, 4 * cols)
    mark = dsmall.shape[0]
    dsmall = dsmall.reshape(mark, plane, rows).transpose(1, 0, 2)
    rms = jnp.broadcast_to(rms[:, 0, :3].reshape(1, 1, share * 3), (plane, 8, share * 3))
    me = lax.axis_index("wide") * ten_n + lax.axis_index("tensor")
    rms = jnp.where(lax.broadcasted_iota(jnp.int32, rms.shape, 0) == me, rms, 0.0)
    dsmall = jnp.concatenate(
        [
            jnp.pad(dsmall, ((0, 0), (0, 0), (0, lanes - rows))),
            jnp.pad(rms, ((0, 0), (0, 0), (0, lanes - share * 3))),
        ],
        axis=1,
    )
    layer_output, input_grad, dpack, dsmall = finish([low, dx], dpack, dsmall, share)
    rms = dsmall[:, mark, : share * 3].reshape(images, 3)
    dsmall = jnp.sum(dsmall[:, :params, :rows], axis=0)
    return (
        layer_output,
        rms,
        input_grad,
        dpack[:, : 3 * cols].reshape(rows, 3, cols),
        dpack[:, 3 * cols :].T,
        dsmall[0:2],
        dsmall[2:4],
        dsmall[4:].T,
        up_grad[None],
        down_grad[None],
    )


def solution(mesh):
    images = P(("wide", "tensor"), None, None)
    qkv = P(("wide", "tensor"), None, "context")
    proj = P("context", ("wide", "tensor"))
    lane = P(None, ("wide", "tensor"))
    rowed = P(("wide", "tensor"), None)
    up = P(("wide", "context"), None, "tensor")
    down = P(("wide", "context"), "tensor", None)
    return jax.shard_map(
        on_device,
        mesh=mesh,
        in_specs=(images, qkv, proj, lane, lane, rowed, up, down, images),
        out_specs=(images, rowed, images, qkv, proj, lane, lane, rowed, up, down),
        check_vma=False,
    )
```

time: 552 us -> 316 us (0.57); the launches traced: 542 us -> 316 us
  waiting for transfers between devices: 310 us -> 0 us
  Pallas kernels: 0 us -> 289 us
  matrix products: 72.2 us -> 0 us
  blocking collectives: 61 us -> 0 us
  other arithmetic: 47.8 us -> 3.55 us
  between operations: 15.1 us -> 0.73 us
  local copies, waits for them, and re-layouts: 35.6 us -> 22.9 us
    pallas_call x0 -> x5, Pallas kernels: none -> 289 us  [the longest x1 140 us: finish(): pl.pallas_call(functools.partial(tail_kernel, n_arr, share), out_shape=tu...]
    all_gather x3 -> x0, waiting for transfers between devices: 181 us -> none  [the longest x1 72.3 us: on_device(): lax.all_gather(result.astype(bf16), 'context', axis=0, tiled=True)]
    reduce_scatter x1 -> x0, waiting for transfers between devices: 111 us -> none  [on_device(): lax.psum_scatter(dpack.astype(bf16), everyone, scatter_dimension=0, tiled...]
    dot_general x27 -> x0, matrix products: 72.2 us -> none  [the longest x24 65.1 us: dot32(): return jnp.einsum(spec, a, b, preferred_element_type=f32, **kw)]
    all_gather x3 -> x0, blocking collectives: 28.7 us -> none  [the longest x1 11.9 us: on_device(): rms = lax.all_gather(rms, 'context', axis=0, tiled=True)]
    all_to_all x2 -> x0, blocking collectives: 23.4 us -> none  [the longest x1 12.6 us: on_device(): lax.all_to_all(back, ('wide', 'context'), split_axis=0, concat_axis=0, ti...]
    convert_element_type x4 -> x0, other arithmetic: 18.1 us -> none  [the longest x1 13.9 us: on_device(): (probs * (dprobs - jnp.sum(probs * dprobs, axis=-1, keepdims=True))).asty...]
    unnamed x8 -> x0, waiting for transfers between devices: 17.4 us -> none
  transfers between devices with their start and end apart: 6 -> 0, of which waited for: 5 -> 0; matrix products, arithmetic and copies ran while one was open for 6% -> 0% of each run, Pallas kernels for 0% -> 0%
where the time goes in v2:
time: 316 us
  Pallas kernels  289 us (91%)
  local copies, waits for them, and re-layouts  22.9 us (7%)
  other arithmetic  3.55 us (1%)
    pallas_call x1, Pallas kernels, finish(): pl.pallas_call(functools.partial(tail_kernel, n_arr, share), out_shape=tu...  140 us
    pallas_call x1, Pallas kernels, run_backward(): pl.pallas_call(functools.partial(backward_kernel, share), out_shape=(acts...  50.2 us
    pallas_call x1, Pallas kernels, gather_weights(): pl.pallas_call(gather_kernel, out_shape=(jax.ShapeDtypeStruct((ctx_n, wid...  41.1 us
    pallas_call x1, Pallas kernels, run_experts(): pl.pallas_call(functools.partial(expert_kernel, share), out_shape=(jax.Sh...  29.6 us
    pallas_call x1, Pallas kernels, run_forward(): pl.pallas_call(functools.partial(forward_kernel, share), out_shape=(jax.S...  27.2 us
    unnamed x16, local copies, waits for them, and re-layouts  16.2 us

profile of v2, /device:TPU:0, one launch (start us, length us, event | category | flops | bytes accessed | tf_op | source)
XLA Modules:
  0.0 315.7 jit_solution(14539074361014538420)
XLA Ops:
  0.6 1.1 copy.25
  1.7 0.2 copy.27
  1.9 0.9 copy.26
  2.8 0.7 pad_maximum_fusion.pack
  3.5 1.3 fusion.8.small
  4.8 41.1 %shard_map.168 = (bf16[4,2,2,2,96,768]{5,4,3,2,1,0:T(8,128)(2,1)}, bf16[2,2,2,16,128]{4,3,2,1,0:T(8,128)(2,1)}) custom-call(bf16[96,768]{1,0:T(8,128)(2,1)} %pad_maximum_fusion.pack, bf16[16,128]{1,0:T(8,128)(2,1)} %fusion.8.small), custom_call_target="tpu_custom_call" | custom-call | tf_op jit(solution)/shard_map/pallas_call | solution.py:442
  45.9 0.8 copy.38
  46.6 0.7 reshape.51.small
  47.4 27.2 %shard_map.169 = (bf16[3,4,197,576]{3,2,1,0:T(8,128)(2,1)}, bf16[3,4,197,192]{3,2,1,0:T(8,128)(2,1)}, f32[3,197,768]{2,1,0:T(8,128)}, f32[3,8,197]{2,1,0:T(8,128...) custom-call(bf16[12,197,768]{2,1,0:T(8,128)(2,1)} %x_all.3, bf16[12,197,768]{2,1,0:T(8,128)(2,1)} %g_all.3, ...), custom_call_target="tpu_custom_call" | custom-call | tf_op jit(solution)/shard_map/pallas_call | solution.py:126
  74.6 29.6 %shard_map.170 = (bf16[8,8,768]{2,1,0:T(8,128)(2,1)}, f32[768,768]{1,0:T(8,128)}, f32[768,768]{1,0:T(8,128)}) custom-call(bf16[8,8,768]{2,1,0:T(8,128)(2,1)} %bitcast.36, bf16[768,768]{1,0:T(8,128)(2,1)} %bitcast.29, bf16[768,768]{1,0:T(8,128)(2,1)} %bitcast.30), custom_call_target="tpu_custom_call" | custom-call | tf_op jit(solution)/shard_map/pallas_call | solution.py:561
  104.2 50.2 %shard_map.171 = (bf16[3,197,768]{2,1,0:T(8,128)(2,1)}, bf16[3,197,768]{2,1,0:T(8,128)(2,1)}, bf16[4,768,768]{2,1,0:T(8,128)(2,1)}, f32[16,768]{1,0:T(8,128)}, f32[3,8,128]{2,1,0:T(8,128)}) custom-call(bf16[12,197,768]{2,1,0:T(8,128)(2,1)} %x_all.3, bf16[12,197,768]{2,1,0:T(8,128)(2,1)} %g_all.3, bf16[4,768,768]{2,1,0:T(8,128)(2,1)} %bitcast.25, ...), custom_call_target="tpu_custom_call" | custom-call | tf_op jit(solution)/shard_map/pallas_call | solution.py:254
  154.5 0.7 slice_reduce_fusion.2
  155.2 0.1 broadcast_in_dim.17
  155.4 0.9 reshape.55
  156.3 0.7 select_maximum_fusion.refs_3_
  156.9 140.4 %shard_map.172 = (bf16[12,197,768]{2,1,0:T(8,128)(2,1)}, bf16[12,197,768]{2,1,0:T(8,128)(2,1)}, f32[96,768]{1,0:T(8,128)}, f32[4,24,128]{2,1,0:T(8,128)}) custom-call(bf16[3,197,768]{2,1,0:T(8,128)(2,1)} %get-tuple-element.39.refs_0_, bf16[3,197,768]{2,1,0:T(8,128)(2,1)} %get-tuple-element.40.refs_1_, bf16[4,2,2,2,96,768]{5,4,3,2,1,0:T(8,128)(2,1)} %bitcast.26, ...), custom_call_target="tpu_custom_call" | custom-call | tf_op jit(solution)/shard_map/pallas_call | solution.py:765
  297.3 1.0 slice.30
  298.3 0.1 copy.30
  298.4 0.9 copy.32
  299.3 1.0 slice_bitcast_fusion
  300.3 0.7 copy.33
  301.0 0.7 slice_reduce_fusion.1
  301.9 0.7 copy.31
  302.5 0.8 slice_reduce_fusion
  303.3 0.6 slice_bitcast_fusion.1
  303.9 0.6 fusion.9
  304.5 4.3 %copy.43 = bf16[12,197,768]{2,1,0:T(8,128)(2,1)} copy(bf16[12,197,768]{2,1,0:T(8,128)(2,1)} %get-tuple-element.82) | data formatting | bytes 7262208
  308.7 1.9 copy.44
  310.6 1.1 copy-done.2
  311.7 1.4 copy.45
  313.1 1.1 copy-done.1
  314.3 1.4 copy.46
  (8 shorter events, 0.2 us)
Async XLA Ops:
  304.5 4.3 %copy-start = (bf16[12,197,768]{2,1,0:T(8,128)(2,1)S(1)}, bf16[12,197,768]{2,1,0:T(8,128)(2,1)}, u32[]{:S(2)}) copy-start(bf16[12,197,768]{2,1,0:T(8,128)(2,1)} %get-tuple-element.84) | copy-start | bytes 10893316
  308.7 3.0 copy-start.2
  311.7 2.5 copy-start.1

commit v3 on v1

v3 whole, which is shorter than its diff:
```python
import functools
import math

import jax
import jax.numpy as jnp
from jax import lax
from jax.experimental import pallas as pl
from jax.experimental.pallas import tpu as pltpu
from jax.sharding import PartitionSpec as P

f32 = jnp.float32
bf16 = jnp.bfloat16

HEAD_DIM = 64
norm_eps = 1e-06
highest = lax.Precision.HIGHEST
NN = (((1,), (0,)), ((), ()))
NT = (((1,), (1,)), ((), ()))
TN = (((0,), (0,)), ((), ()))


def mm(a, b, dims=NN, precision=None):
    return lax.dot_general(a, b, dims, precision=precision, preferred_element_type=f32)


def layer_stats(values):
    center = values - jnp.mean(values, axis=-1, keepdims=True)
    spread = lax.rsqrt(jnp.mean(center * center, axis=-1, keepdims=True) + norm_eps)
    return (center * spread, spread)


def norm_back(upstream, scaled, spread):
    return spread * (
        upstream
        - jnp.mean(upstream, axis=-1, keepdims=True)
        - scaled * jnp.mean(upstream * scaled, axis=-1, keepdims=True)
    )


def soft(values, axis):
    e = jnp.exp(values - jnp.max(values, axis=axis, keepdims=True))
    return e / jnp.sum(e, axis=axis, keepdims=True)


def pick_rows(slots_n, row):
    r = lax.broadcasted_iota(jnp.int32, (slots_n * 8, slots_n), 0)
    s = lax.broadcasted_iota(jnp.int32, (slots_n * 8, slots_n), 1)
    return jnp.where(r == s * 8 + row, 1.0, 0.0).astype(bf16)


def router_unit(keys):
    scale = lax.rsqrt(jnp.sum(keys * keys, axis=1, keepdims=True) + norm_eps)
    return keys * scale, scale


def head_parts(block, h, per):
    at = [j * per * HEAD_DIM + h * HEAD_DIM for j in range(3)]
    return [block[:, a : a + HEAD_DIM] for a in at]


def remote(src, dst, ssem, rsem, **where):
    return pltpu.make_async_remote_copy(
        src_ref=src,
        dst_ref=dst,
        send_sem=ssem,
        recv_sem=rsem,
        device_id=where,
        device_id_type=pl.DeviceIdType.MESH,
    )


def spot():
    wide_n, ctx_n, ten_n = (lax.axis_size(a) for a in ("wide", "context", "tensor"))
    w, c, t = (lax.axis_index(a) for a in ("wide", "context", "tensor"))
    return wide_n, ctx_n, ten_n // 2, w, c, t // 2, lax.rem(t, 2)


def greet_plane(bar, wide_n, y_n, w, y, k):
    for o in range(1, wide_n * y_n * 2):
        j = lax.rem((w * y_n + y) * 2 + k + o, wide_n * y_n * 2)
        pl.semaphore_signal(
            bar,
            inc=1,
            device_id={"wide": j // (y_n * 2), "tensor": lax.rem(j, y_n * 2)},
            device_id_type=pl.DeviceIdType.MESH,
        )
    return wide_n * y_n * 2 - 1


def near_first(c, ctx_n):
    seq = []
    for j in range(ctx_n):
        cb = 0
        for p in range(ctx_n):
            order = sorted(range(ctx_n), key=lambda q: (abs(q - p), q))
            cb = jnp.where(c == p, order[j], cb)
        seq.append(cb)
    return seq


def gather_kernel(pack, small, full, smalls, csem, crecv, wsem, wrecv, ysem, yrecv, ksem, krecv, ssem, srecv, local):
    wide_n, ctx_n, y_n, w, c, y, k = spot()
    bar = pltpu.get_barrier_semaphore()
    met = greet_plane(bar, wide_n, y_n, w, y, k)

    @pl.when(c > 0)
    def _():
        pl.semaphore_signal(bar, inc=1, device_id={"context": c - 1}, device_id_type=pl.DeviceIdType.MESH)

    @pl.when(c < ctx_n - 1)
    def _():
        pl.semaphore_signal(bar, inc=1, device_id={"context": c + 1}, device_id_type=pl.DeviceIdType.MESH)

    mine = pltpu.make_async_copy(pack, full.at[c, w, y, k], local.at[0])
    mine_small = pltpu.make_async_copy(small, smalls.at[w, y, k], local.at[1])
    mine.start()
    mine_small.start()
    pl.semaphore_wait(bar, met + (c + ctx_n - 1) // ctx_n + (2 * ctx_n - 2 - c) // ctx_n)

    def along(cb, side, src):
        return remote(src, full.at[cb, w, y, k], csem.at[side, cb], crecv.at[cb], context=c + 2 * side - 1)

    for side in (0, 1):

        @pl.when((c > 0) if side == 0 else (c < ctx_n - 1))
        def _():
            along(c, side, pack).start()

    def small_copy(o):
        j = lax.rem((w * y_n + y) * 2 + k + o, wide_n * y_n * 2)
        return remote(
            small, smalls.at[w, y, k], ssem.at[o], srecv.at[o], wide=j // (y_n * 2), tensor=lax.rem(j, y_n * 2)
        )

    for o in range(1, wide_n * y_n * 2):
        small_copy(o).start()

    seq = near_first(c, ctx_n)

    def leg(cb, number, o, start):
        even = lax.rem(cb, 2) == 0
        for on_wide in (True, False):
            n = wide_n if on_wide else y_n
            if o >= n:
                continue
            first = number == 0
            want_even = on_wide == first

            @pl.when(even if want_even else jnp.logical_not(even))
            def _():
                if on_wide:
                    ref = full.at[cb, w, y, k] if first else full.at[cb, w, :, k]
                    to = {"wide": lax.rem(w + o, wide_n)}
                    sems = (wsem.at[cb, o], wrecv.at[cb, o])
                else:
                    ref = full.at[cb, w, y, k] if first else full.at[cb, :, y, k]
                    to = {"tensor": lax.rem(y + o, y_n) * 2 + k}
                    sems = (ysem.at[cb, o], yrecv.at[cb, o])
                cp = remote(ref, ref, *sems, **to)
                if start == "start":
                    cp.start()
                elif start == "recv":
                    cp.wait_recv()
                else:
                    cp.wait_send()

    most = max(wide_n, y_n)

    def core(cb):
        ref = full.at[cb, :, :, k]
        return remote(ref, ref, ksem.at[cb], krecv.at[cb], tensor=y * 2 + 1 - k)

    mine.wait()
    mine_small.wait()
    for step in range(ctx_n + 2):
        if step < ctx_n:
            cb = seq[step]
            if step > 0:
                along(cb, 0, pack).wait_recv()
                for side in (0, 1):
                    go = jnp.logical_and(cb > c, c > 0) if side == 0 else jnp.logical_and(cb < c, c < ctx_n - 1)

                    @pl.when(go)
                    def _():
                        along(cb, side, full.at[cb, w, y, k]).start()

            for o in range(1, most):
                leg(cb, 0, o, "start")
        if 0 < step <= ctx_n:
            cb = seq[step - 1]
            for o in range(1, most):
                leg(cb, 0, o, "recv")
            for o in range(1, most):
                leg(cb, 1, o, "start")
        if step > 1:
            cb = seq[step - 2]
            for o in range(1, most):
                leg(cb, 1, o, "recv")
            core(cb).start()
    for step in range(ctx_n):
        core(seq[step]).wait_recv()
    for o in range(1, wide_n * y_n * 2):
        cp = small_copy(o)
        cp.wait_recv()
        cp.wait_send()
    for step in range(ctx_n):
        cb = seq[step]
        for side in (0, 1):
            go = jnp.logical_and(cb >= c, c > 0) if side == 0 else jnp.logical_and(cb <= c, c < ctx_n - 1)

            @pl.when(go)
            def _():
                along(cb, side, pack).wait_send()

        for number in (0, 1):
            for o in range(1, most):
                leg(cb, number, o, "send")
        core(cb).wait_send()


def gather_weights(pack, small):
    wide_n, ctx_n, ten_n = (lax.axis_size(a) for a in ("wide", "context", "tensor"))
    y_n = ten_n // 2
    dma = pltpu.SemaphoreType.DMA
    vm = pl.BlockSpec(memory_space=pltpu.VMEM)
    return pl.pallas_call(
        gather_kernel,
        out_shape=(
            jax.ShapeDtypeStruct((ctx_n, wide_n, y_n, 2) + pack.shape, pack.dtype),
            jax.ShapeDtypeStruct((wide_n, y_n, 2) + small.shape, small.dtype),
        ),
        in_specs=[vm, vm],
        out_specs=(vm, vm),
        scratch_shapes=[
            dma((2, ctx_n)), dma((ctx_n,)),
            dma((ctx_n, wide_n)), dma((ctx_n, wide_n)),
            dma((ctx_n, y_n)), dma((ctx_n, y_n)),
            dma((ctx_n,)), dma((ctx_n,)),
            dma((wide_n * ten_n,)), dma((wide_n * ten_n,)),
            dma((2,)),
        ],
        compiler_params=pltpu.CompilerParams(collective_id=1, has_side_effects=True),
    )(pack, small)


def gelu_parts(x):
    a = 0.7978845608028654
    x2 = x * x
    th = jnp.tanh(a * x * (1.0 + 0.044715 * x2))
    val = 0.5 * x * (1.0 + th)
    der = 0.5 * (1.0 + th) + 0.5 * x * (1.0 - th * th) * (a * (1.0 + 3 * 0.044715 * x2))
    return val, der


def block_kernel(share, *refs):
    (
        x_all, g_all, full, small, up, down,
        lo, dxo, grad, smalls, e_in, e_act, e_hid, e_dexp,
        x_s, g_s, att_s, dx_s, nt_s, dt_s, qkv, heads, resid, logits, asq, dres_s, dn_s, rows_s,
        send_s, got, r32, e_s, ret, got2, eo_all, comb_all, dsm, sblk,
        part, rcv1, rcv2, rcv3, acc3, rcv4, srcv, a_buf, x_buf,
        lsem, esem, xsem, gsem, grecv, ksem, krecv, s2, r2, s3, r3, s4, r4, ss, sr, es, er, obuf_sem,
    ) = refs
    wide_n, ctx_n, y_n, w, c, y, k = spot()
    ten_n = 2 * y_n
    plane = wide_n * ten_n
    n = plane * ctx_n
    me = (w * ctx_n + c) * ten_n + y * 2 + k
    mine = (w * y_n + y) * 2 + k
    width, packed = full.shape[1:]
    cols = packed // 4
    per = cols // HEAD_DIM
    slots_n = small.shape[0] - 4
    length = x_s.shape[1]
    rows = grad.shape[0]
    logit_scale = 1.6 * math.sqrt(width)
    seq = near_first(c, ctx_n)
    bar = pltpu.get_barrier_semaphore()

    def place(d):
        return {"wide": d // (ctx_n * ten_n), "context": lax.rem(d // ten_n, ctx_n), "tensor": lax.rem(d, ten_n)}

    def hello(o, carry):
        pl.semaphore_signal(bar, inc=1, device_id=place(lax.rem(me + o, n)), device_id_type=pl.DeviceIdType.MESH)
        return carry

    lax.fori_loop(1, n, hello, 0)
    ins = [
        pltpu.make_async_copy(x_all.at[pl.ds(c * share, share)], x_s, lsem.at[0]),
        pltpu.make_async_copy(g_all.at[pl.ds(c * share, share)], g_s, lsem.at[1]),
    ]
    for cp in ins:
        cp.start()
    rows_s[...] = jnp.zeros_like(rows_s)
    dsm[...] = jnp.zeros_like(dsm)
    keys, key_scale = router_unit(small[4:, :].astype(f32))

    def along(a, cb, i, side, own):
        ref = (lo, dxo)[a].at[cb * share + i]
        src = (att_s, dx_s)[a].at[i] if own else ref
        return remote(src, ref, gsem.at[a, side, cb, i], grecv.at[a, cb, i], context=c + 2 * side - 1)

    def launch(a, i):
        for side in (0, 1):

            @pl.when((c > 0) if side == 0 else (c < ctx_n - 1))
            def _():
                along(a, c, i, side, True).start()

    def onward(cb, side):
        if side == 0:
            return jnp.logical_and(cb > c, c > 0)
        return jnp.logical_and(cb < c, c < ctx_n - 1)

    def pump(a, todo):
        for step, i in todo:
            cb = seq[step]
            along(a, cb, i, 0, False).wait_recv()
            for side in (0, 1):

                @pl.when(onward(cb, side))
                def _():
                    along(a, cb, i, side, False).start()

    pairs = [(s, i) for s in range(1, ctx_n) for i in range(share)]
    pairs.sort(key=lambda p: (p[0] + p[1], p[1]))
    early, middle, late = pairs[:1], pairs[1:3], pairs[3:5]
    rest = pairs[5:]
    waves = [[p for p in pairs if p[0] + p[1] == d] for d in range(1, ctx_n + share - 1)]
    for cp in ins:
        cp.wait()
    pl.semaphore_wait(bar, n - 1)

    def forward(i, carry):
        x = x_s[i].astype(f32)
        hat, spread = layer_stats(x)
        normed = (hat * small[0:1, :].astype(f32) + small[2:3, :].astype(f32)).astype(bf16)
        nt_s[i] = normed.T
        resid[i] = x

        def block(cb, carry):
            qkv_c = mm(normed, full[cb, :, : 3 * cols]).astype(bf16)
            qkv[i, cb] = qkv_c
            mixed = []
            for h in range(per):
                q, kk, v = head_parts(qkv_c, h, per)
                p = soft(mm(q, kk, NT) * 0.125, 1)
                mixed.append(mm(p.astype(bf16), v).astype(bf16))
            heads_c = jnp.concatenate(mixed, axis=1)
            heads[i, cb] = heads_c
            resid[i] += mm(heads_c, full[cb, :, 3 * cols :], NT)
            return carry

        lax.fori_loop(0, ctx_n, block, 0)
        res = resid[i]
        att = res - x
        att_s[i] = att.astype(bf16)
        asq[i] = jnp.full(asq.shape[1:], jnp.sum(att * att), f32)
        launch(0, i)

        @pl.when(i == 1)
        def _():
            pump(0, early)

        hat2, _ = layer_stats(res)
        second = hat2 * small[1:2, :].astype(f32) + small[3:4, :].astype(f32)
        unit = second * lax.rsqrt(jnp.sum(second * second, axis=-1, keepdims=True) + norm_eps)
        lg = logit_scale * mm(keys, unit, NT, highest)
        logits[i] = lg
        disp = soft(lg, 1).astype(bf16)
        comb = soft(lg, 0).astype(bf16)
        comb_all[c, i, :, :length] = comb
        slots = mm(disp, second.astype(bf16)).astype(bf16)
        dexp = mm(comb, g_s[i]).astype(bf16)
        rows_s[...] += mm(pick_rows(slots_n, i), slots) + mm(pick_rows(slots_n, i + 4), dexp)
        return carry

    lax.fori_loop(0, share, forward, 0)

    for e in range(slots_n):
        send_s[e] = rows_s[e * 8 : e * 8 + 8, :].astype(bf16)
    got[me] = send_s[w * ctx_n + c]

    def send_out(o, carry):
        d = lax.rem(me + o, n)
        remote(send_s.at[d // ten_n], got.at[me], esem.at[0], esem.at[1], **place(d)).start()
        return carry

    lax.fori_loop(1, n, send_out, 0)

    def drain(ref, sem):
        some = ref.at[pl.ds(0, n - 1)]
        pltpu.make_async_copy(some, some, sem).wait()

    pump(0, middle)
    drain(got, esem.at[1])

    group = min(n, 32)
    chunk = group * 8
    first = lax.rem(lax.broadcasted_iota(jnp.int32, (chunk, 1), 0), 8) < 4

    def expert_out(b, j):
        dst = (e_in, e_act, e_hid, e_dexp)[j]
        at = pl.ds(pl.multiple_of(b * chunk, chunk), chunk)
        return pltpu.make_async_copy(e_s.at[j], dst.at[at, :], xsem.at[j])

    def experts(b, carry):
        def widen(j, carry):
            r32[pl.ds(pl.multiple_of(j * 8, 8), 8), :] = got[b * group + j].astype(f32)
            return carry

        lax.fori_loop(0, group, widen, 0)

        @pl.when(b > 0)
        def _():
            for j in range(4):
                expert_out(b, j).wait()

        low = r32[...].astype(bf16)
        e_s[0] = low
        e_s[3] = pltpu.roll(r32[...], chunk - 4, 0).astype(bf16)
        hidden = mm(low, up[...])
        act_g = pltpu.roll(mm(low, down[...], NT), chunk - 4, 0)
        val, der = gelu_parts(hidden)
        active = jnp.where(first, val, 0.0).astype(bf16)
        hid_g = jnp.where(first, act_g * der, 0.0).astype(bf16)
        e_s[1] = active
        e_s[2] = hid_g
        part_o = mm(active, down[...])
        part_s = mm(hid_g, up[...], NT)
        r32[...] = jnp.where(first, part_o, pltpu.roll(part_s, 4, 0))
        for j in range(4):
            expert_out(b, j).start()

        def narrow(j, carry):
            ret[b * group + j] = r32[pl.ds(pl.multiple_of(j * 8, 8), 8), :].astype(bf16)
            return carry

        lax.fori_loop(0, group, narrow, 0)
        return carry

    lax.fori_loop(0, n // group, experts, 0)

    def send_back(o, carry):
        d = lax.rem(me + o, n)
        remote(ret.at[d], got2.at[me], esem.at[2], esem.at[3], **place(d)).start()
        return carry

    lax.fori_loop(1, n, send_back, 0)
    got2[me] = ret[me]
    pump(0, late)
    drain(got2, esem.at[3])

    def total(e, carry):
        s = got2[e * ten_n].astype(f32)
        for t in range(1, ten_n):
            s = s + got2[e * ten_n + t].astype(f32)
        rows_s[pl.ds(pl.multiple_of(e * 8, 8), 8), :] = s
        return carry

    lax.fori_loop(0, slots_n, total, 0)
    back = rows_s[...].astype(bf16)
    for i in range(share):
        eo_all[c, i] = mm(pick_rows(slots_n, i), back, TN).astype(bf16)

    def trade(o, ref, j, p):
        return remote(ref.at[p], ref.at[p], es.at[j, o], er.at[j, o], context=lax.rem(c + o, ctx_n))

    for o in range(1, ctx_n):
        trade(o, eo_all, 0, c).start()
        trade(o, comb_all, 1, c).start()

    def fetch(step, i, slot):
        img = seq[step] * share + i
        return (
            pltpu.make_async_copy(lo.at[img], a_buf.at[slot], obuf_sem.at[0, slot]),
            pltpu.make_async_copy(x_all.at[img], x_buf.at[slot], obuf_sem.at[1, slot]),
        )

    def put(step, i, slot):
        img = seq[step] * share + i
        return pltpu.make_async_copy(a_buf.at[slot], lo.at[img], obuf_sem.at[2, slot])

    def backward(i, carry):
        gain1, gain2 = small[0:1, :].astype(f32), small[1:2, :].astype(f32)
        g_low = g_s[i]
        res = resid[i]
        hat2, spread2 = layer_stats(res)
        second = hat2 * gain2 + small[3:4, :].astype(f32)
        tokens = second.astype(bf16)
        row_scale = lax.rsqrt(jnp.sum(second * second, axis=-1, keepdims=True) + norm_eps)
        unit = second * row_scale
        eo = eo_all[c, i]
        ds = mm(pick_rows(slots_n, i + 4), rows_s[...].astype(bf16), TN).astype(bf16)
        lg = logits[i]
        disp = soft(lg, 1)
        comb = soft(lg, 0)
        mixture = mm(comb.astype(bf16), eo, TN)
        result = res + mixture

        @pl.when(i > 1)
        def _():
            put(0, 0, 0).wait()

        a_buf[lax.rem(i, 2)] = result.astype(bf16)
        put(0, i, lax.rem(i, 2)).start()
        count = 1.0 / (length * width)
        lane = lax.broadcasted_iota(jnp.int32, (8, smalls.shape[2]), 1)
        sums = jnp.where(
            lane == 0,
            jnp.sum(result * result),
            jnp.where(lane == 1, asq[i], jnp.sum(mixture * mixture)),
        )
        at_row = lax.broadcasted_iota(jnp.int32, (8, smalls.shape[2]), 0)
        sblk[plane, :8, :] = jnp.where(at_row == i, jnp.sqrt(sums * count), sblk[plane, :8, :])
        dcomb = mm(eo, g_low, NT)
        ddisp = mm(ds, tokens, NT)
        dtok = mm(disp.astype(bf16), ds, TN)
        dlg = comb * (dcomb - jnp.sum(comb * dcomb, axis=0, keepdims=True)) + disp * (
            ddisp - jnp.sum(disp * ddisp, axis=1, keepdims=True)
        )
        dunit = logit_scale * mm(dlg, keys, TN, highest)
        dsm[4 : 4 + slots_n, :] += logit_scale * mm(dlg, unit, NN, highest)
        dsec = dtok + row_scale * (dunit - unit * jnp.sum(unit * dunit, axis=-1, keepdims=True))
        dsm[1:2, :] += jnp.sum(dsec * hat2, axis=0, keepdims=True)
        dsm[3:4, :] += jnp.sum(dsec, axis=0, keepdims=True)
        dres = g_low.astype(f32) + norm_back(dsec * gain2, hat2, spread2)
        dres_s[...] = dres
        dattn = dres.astype(bf16)
        dt_s[i] = dattn.T
        hat, spread = layer_stats(x_s[i].astype(f32))
        dn_s[...] = jnp.zeros_like(dn_s)

        @pl.when(i == 0)
        def _():
            pump(0, rest)

        def block(cb, carry):
            for j in range(1, share):

                @pl.when(jnp.logical_and(i == j, cb == ctx_n // 2))
                def _():
                    pump(1, waves[j - 1])

            proj = full[cb, :, 3 * cols :]
            dheads = mm(dattn, proj).astype(bf16)
            qkv_c = qkv[i, cb]
            grads = [[], [], []]
            for h in range(per):
                q, kk, v = head_parts(qkv_c, h, per)
                dh = dheads[:, h * HEAD_DIM : (h + 1) * HEAD_DIM]
                p = soft(mm(q, kk, NT) * 0.125, 1)
                dp = mm(dh, v, NT)
                dsc = (p * (dp - jnp.sum(p * dp, axis=1, keepdims=True))).astype(bf16)
                grads[0].append((mm(dsc, kk) * 0.125).astype(bf16))
                grads[1].append((mm(dsc, q, TN) * 0.125).astype(bf16))
                grads[2].append(mm(p.astype(bf16), dh, TN).astype(bf16))
            dqkv = jnp.concatenate(grads[0] + grads[1] + grads[2], axis=1)
            qkv[i, cb] = dqkv
            dn_s[...] += mm(dqkv, full[cb, :, : 3 * cols], NT)
            return carry

        lax.fori_loop(0, ctx_n, block, 0)
        dn = dn_s[...]
        dsm[0:1, :] += jnp.sum(dn * hat, axis=0, keepdims=True)
        dsm[2:3, :] += jnp.sum(dn, axis=0, keepdims=True)
        dx_s[i] = (dres_s[...] + norm_back(dn * gain1, hat, spread)).astype(bf16)
        launch(1, i)
        return carry

    sblk[plane] = jnp.zeros(sblk.shape[1:], f32)
    lax.fori_loop(0, share, backward, 0)
    outs = [pltpu.make_async_copy(dx_s, dxo.at[pl.ds(c * share, share)], lsem.at[1])]
    for cp in outs:
        cp.start()
    dkeys = dsm[4 : 4 + slots_n, :]
    dsm[4 : 4 + slots_n, :] = key_scale * (dkeys - keys * jnp.sum(keys * dkeys, axis=1, keepdims=True))

    def core(cc):
        return remote(part.at[cc, :, :, 1 - k], rcv1.at[cc], ksem.at[cc], krecv.at[cc], tensor=y * 2 + 1 - k)

    for cc in range(ctx_n):
        from_qkv = sum(mm(nt_s[i], qkv[i, cc]) for i in range(share)).astype(bf16)
        from_proj = sum(mm(dt_s[i], heads[i, cc]) for i in range(share)).astype(bf16)
        for j in range(plane):
            at = (cc, j // ten_n, (j // 2) % y_n, j % 2)
            part[at + (slice(None), slice(0, 3 * cols))] = from_qkv[j * rows : (j + 1) * rows]
            part[at + (slice(None), slice(3 * cols, packed))] = from_proj[j * rows : (j + 1) * rows]
        core(cc).start()
        if cc == ctx_n // 2:
            pump(1, waves[2] if len(waves) > 2 else [])
    for j in range(plane):
        sblk[j, :, :rows] = dsm[:, j * rows : (j + 1) * rows]

    def small1(o):
        j = lax.rem(mine + o, plane)
        return remote(sblk.at[j], srcv.at[o], ss.at[o], sr.at[o], wide=j // ten_n, tensor=lax.rem(j, ten_n))

    for o in range(1, plane):
        small1(o).start()

    def hop(cc, number, o):
        on_wide = (cc % 2 == 0) == (number == 2)
        ss_, rr_ = (s2, r2) if number == 2 else (s3, r3)
        if on_wide:
            p = lax.rem(w + o, wide_n)
            to = {"wide": p}
            frm = rcv1.at[cc, p] if number == 2 else rcv1.at[cc, p, y]
            into = rcv2.at[cc, pl.ds(o * y_n, y_n)] if number == 2 else rcv3.at[cc, o]
        else:
            p = lax.rem(y + o, y_n)
            to = {"tensor": p * 2 + k}
            frm = rcv1.at[cc, :, p] if number == 2 else rcv1.at[cc, w, p]
            into = rcv2.at[cc, pl.ds(o * wide_n, wide_n)] if number == 2 else rcv3.at[cc, o]
        return remote(frm, into, ss_.at[cc, o], rr_.at[cc, o], **to)

    def peers(cc, number):
        on_wide = (cc % 2 == 0) == (number == 2)
        return range(1, wide_n if on_wide else y_n)

    for cc in range(ctx_n):
        core(cc).wait_recv()
        for wi in range(wide_n):
            for yi in range(y_n):
                rcv1[cc, wi, yi] = (part[cc, wi, yi, k].astype(f32) + rcv1[cc, wi, yi].astype(f32)).astype(bf16)
        for o in peers(cc, 2):
            hop(cc, 2, o).start()
    pump(1, waves[3] if len(waves) > 3 else [])

    for o in range(1, ctx_n):
        p = lax.rem(c + ctx_n - o, ctx_n)
        trade(o, eo_all, 0, p).wait_recv()
        trade(o, comb_all, 1, p).wait_recv()

    order = [(s, i) for s in range(1, ctx_n) for i in range(share)]

    def mix_some(lo_n, hi_n):
        for j in range(lo_n, hi_n):
            step, i = order[j]
            cb = seq[step]
            slot = (j + share) % 2
            for side in (0, 1):

                @pl.when(onward(cb, side))
                def _():
                    along(0, cb, i, side, False).wait_send()

            put(step, i, slot).wait()
            for cp in fetch(step, i, slot):
                cp.start()
            for cp in fetch(step, i, slot):
                cp.wait()
            mixed = mm(comb_all[cb, i, :, :length], eo_all[cb, i], TN)
            out = x_buf[slot].astype(f32) + a_buf[slot].astype(f32) + mixed
            a_buf[slot] = out.astype(bf16)
            put(step, i, slot).start()

    third = len(order) // 3
    mix_some(0, third)
    for cc in range(ctx_n):
        on_wide = cc % 2 == 0
        for o in peers(cc, 2):
            hop(cc, 2, o).wait_recv()
        for j in range(y_n if on_wide else wide_n):
            spot_j = (cc, w, j) if on_wide else (cc, j, y)
            tot = rcv1[spot_j].astype(f32)
            for o in peers(cc, 2):
                tot = tot + rcv2[cc, o * (y_n if on_wide else wide_n) + j].astype(f32)
            rcv1[spot_j] = tot.astype(bf16)
        for o in peers(cc, 3):
            hop(cc, 3, o).start()

    tot = sblk[mine]
    for o in range(1, plane):
        small1(o).wait_recv()
        tot = tot + srcv[o]
    smalls[c, : sblk.shape[1], :] = tot
    smalls[c, sblk.shape[1] :, :] = sblk[plane, :8, :]

    def small2(o, p):
        return remote(
            smalls.at[p], smalls.at[p], ss.at[plane + o], sr.at[plane + o], context=lax.rem(c + o, ctx_n)
        )

    for o in range(1, ctx_n):
        small2(o, c).start()
    pump(1, waves[4] if len(waves) > 4 else [])
    mix_some(third, 2 * third)

    def last(cc):
        return remote(acc3.at[cc], rcv4.at[c], s4.at[cc], r4.at[c], context=cc)

    for cc in range(ctx_n):
        for o in peers(cc, 3):
            hop(cc, 3, o).wait_recv()
        tot = rcv1[cc, w, y].astype(f32)
        for o in peers(cc, 3):
            tot = tot + rcv3[cc, o].astype(f32)
        acc3[cc] = tot.astype(bf16)

        @pl.when(c != cc)
        def _():
            last(cc).start()

    mix_some(2 * third, len(order))
    for wave in waves[5:]:
        pump(1, wave)
    tot = acc3[c].astype(f32)
    for o in range(1, ctx_n):
        p = lax.rem(c + o, ctx_n)
        remote(acc3.at[0], rcv4.at[p], s4.at[p], r4.at[p], context=p).wait_recv()
        tot = tot + rcv4[p].astype(f32)
    grad[...] = tot

    for slot in (0, 1):
        put(0, 0, slot).wait()
    for j in range(4):
        expert_out(0, j).wait()
    drain(ret, esem.at[2])

    def sent(o, carry):
        pltpu.make_async_copy(send_s.at[0], send_s.at[0], esem.at[0]).wait()
        return carry

    lax.fori_loop(1, n, sent, 0)
    for o in range(1, ctx_n):
        p = lax.rem(c + ctx_n - o, ctx_n)
        small2(o, p).wait_recv()
        small2(o, c).wait_send()
        trade(o, eo_all, 0, c).wait_send()
        trade(o, comb_all, 1, c).wait_send()
        last(lax.rem(c + o, ctx_n)).wait_send()
    for o in range(1, plane):
        small1(o).wait_send()
    for cc in range(ctx_n):
        core(cc).wait_send()
        for number in (2, 3):
            for o in peers(cc, number):
                hop(cc, number, o).wait_send()
    for cp in outs:
        cp.wait()
    for a in (0, 1):
        for i in range(share):
            for side in (0, 1):

                @pl.when((c > 0) if side == 0 else (c < ctx_n - 1))
                def _():
                    along(a, c, i, side, True).wait_send()

    for step, i in order:
        for side in (0, 1):

            @pl.when(onward(seq[step], side))
            def _():
                along(1, seq[step], i, side, False).wait_send()


def run_block(x_all, g_all, full, small, up, down, rows, share):
    wide_n, ctx_n, ten_n = (lax.axis_size(a) for a in ("wide", "context", "tensor"))
    y_n = ten_n // 2
    plane = wide_n * ten_n
    n = plane * ctx_n
    most = max(wide_n, y_n)
    images, length, width = x_all.shape
    packed = full.shape[2]
    cols = packed // 4
    ff = up.shape[1]
    slots_n = small.shape[0] - 4
    par8 = 4 + slots_n + -(4 + slots_n) % 8
    lanes = rows + -rows % 128
    blk = (rows, packed)
    acts = (share, length, width)
    wide_len = length + -length % 128
    dma = pltpu.SemaphoreType.DMA
    vm = pl.BlockSpec(memory_space=pltpu.VMEM)
    hbm = pl.BlockSpec(memory_space=pl.ANY)
    V = pltpu.VMEM
    shape = jax.ShapeDtypeStruct
    return pl.pallas_call(
        functools.partial(block_kernel, share),
        out_shape=(
            shape((images, length, width), bf16),
            shape((images, length, width), bf16),
            shape(blk, f32),
            shape((ctx_n, par8 + 8, lanes), f32),
            shape((n * 8, width), bf16),
            shape((n * 8, ff), bf16),
            shape((n * 8, ff), bf16),
            shape((n * 8, width), bf16),
        ),
        in_specs=[hbm, hbm] + [vm] * 4,
        out_specs=(hbm, hbm, vm, vm) + (hbm,) * 4,
        scratch_shapes=[
            V(acts, bf16), V(acts, bf16), V(acts, bf16), V(acts, bf16),
            V((share, width, length), bf16),
            V((share, width, length), bf16),
            V((share, ctx_n, length, 3 * cols), bf16),
            V((share, ctx_n, length, cols), bf16),
            V(acts, f32),
            V((share, slots_n, length), f32),
            V((share, 8, lanes), f32),
            V((length, width), f32),
            V((length, width), f32),
            V((slots_n * 8, width), f32),
            V((slots_n, 8, width), bf16),
            V((n, 8, width), bf16),
            V((min(n, 32) * 8, width), f32),
            V((4, min(n, 32) * 8, width), bf16),
            V((n, 8, width), bf16),
            V((n, 8, width), bf16),
            V((ctx_n, share, slots_n, width), bf16),
            V((ctx_n, share, slots_n, wide_len), bf16),
            V((par8, width), f32),
            V((plane + 1, par8, lanes), f32),
            V((ctx_n, wide_n, y_n, 2) + blk, bf16),
            V((ctx_n, wide_n, y_n) + blk, bf16),
            V((ctx_n, wide_n * y_n) + blk, bf16),
            V((ctx_n, most) + blk, bf16),
            V((ctx_n,) + blk, bf16),
            V((ctx_n,) + blk, bf16),
            V((plane, par8, lanes), f32),
            V((2, length, width), bf16),
            V((2, length, width), bf16),
            dma((2,)), dma((4,)), dma((4,)),
            dma((2, 2, ctx_n, share)), dma((2, ctx_n, share)),
            dma((ctx_n,)), dma((ctx_n,)),
            dma((ctx_n, most)), dma((ctx_n, most)),
            dma((ctx_n, most)), dma((ctx_n, most)),
            dma((ctx_n,)), dma((ctx_n,)),
            dma((plane + ctx_n,)), dma((plane + ctx_n,)),
            dma((2, ctx_n)), dma((2, ctx_n)),
            dma((3, 2)),
        ],
        compiler_params=pltpu.CompilerParams(
            collective_id=2, has_side_effects=True, vmem_limit_bytes=67043328
        ),
    )(x_all, g_all, full, small, up, down)


def on_device(
    layer_input,
    qkv_weight,
    proj_weight,
    norm_gains,
    norm_biases,
    router_keys,
    up_weight,
    down_weight,
    out_cotangent,
):
    images, length, width = layer_input.shape
    wide_n, ctx_n, ten_n = (lax.axis_size(a) for a in ("wide", "context", "tensor"))
    share = images // ctx_n
    slots_n = router_keys.shape[1]
    rows, _, cols = qkv_weight.shape
    plane = wide_n * ten_n
    lanes = rows + -rows % 128

    pack = jnp.concatenate([qkv_weight.reshape(rows, 3 * cols), proj_weight.T], axis=1)
    small = jnp.concatenate([norm_gains, norm_biases, router_keys.T], axis=0)
    params = small.shape[0]
    small = jnp.pad(small, ((0, -params % 16), (0, lanes - rows)))
    weights, small = gather_weights(pack, small)
    weights = weights.reshape(ctx_n, width, 4 * cols)
    small = small.reshape((-1,) + small.shape[3:])[:, :params, :rows]
    small = small.transpose(1, 0, 2).reshape(params, width)
    layer_output, input_grad, dpack, dsmall, e_in, e_act, e_hid, e_dexp = run_block(
        layer_input, out_cotangent, weights, small, up_weight[0], down_weight[0], rows, share
    )
    up_grad = mm(e_in, e_hid, TN)
    down_grad = mm(e_act, e_dexp, TN)
    rms = dsmall[:, dsmall.shape[1] - 8 :, :3][:, :share].reshape(images, 3)
    dsmall = jnp.sum(dsmall[:, :params, :rows], axis=0)
    return (
        layer_output,
        rms,
        input_grad,
        dpack[:, : 3 * cols].reshape(rows, 3, cols),
        dpack[:, 3 * cols :].T,
        dsmall[0:2],
        dsmall[2:4],
        dsmall[4:].T,
        up_grad[None],
        down_grad[None],
    )


def solution(mesh):
    images = P(("wide", "tensor"), None, None)
    qkv = P(("wide", "tensor"), None, "context")
    proj = P("context", ("wide", "tensor"))
    lane = P(None, ("wide", "tensor"))
    rowed = P(("wide", "tensor"), None)
    up = P(("wide", "context"), None, "tensor")
    down = P(("wide", "context"), "tensor", None)
    return jax.shard_map(
        on_device,
        mesh=mesh,
        in_specs=(images, qkv, proj, lane, lane, rowed, up, down, images),
        out_specs=(images, rowed, images, qkv, proj, lane, lane, rowed, up, down),
        check_vma=False,
    )
```

time: 552 us -> 255 us (0.46); the launches traced: 542 us -> 254 us
  waiting for transfers between devices: 310 us -> 0 us
  Pallas kernels: 0 us -> 231 us
  matrix products: 72.2 us -> 4.95 us
  blocking collectives: 61 us -> 0 us
  other arithmetic: 47.8 us -> 2.97 us
  local copies, waits for them, and re-layouts: 35.6 us -> 15.3 us
  between operations: 15.1 us -> 0.71 us
    pallas_call x0 -> x2, Pallas kernels: none -> 231 us  [the longest x1 190 us: run_block(): pl.pallas_call(functools.partial(block_kernel, share), out_shape=(shape((...]
    all_gather x3 -> x0, waiting for transfers between devices: 181 us -> none  [the longest x1 72.3 us: on_device(): lax.all_gather(result.astype(bf16), 'context', axis=0, tiled=True)]
    reduce_scatter x1 -> x0, waiting for transfers between devices: 111 us -> none  [on_device(): lax.psum_scatter(dpack.astype(bf16), everyone, scatter_dimension=0, tiled...]
    dot_general x27 -> x2, matrix products: 72.2 us -> 4.95 us  [mm(): lax.dot_general(a, b, dims, precision=precision, preferred_element_type=f32)]
    all_gather x3 -> x0, blocking collectives: 28.7 us -> none  [the longest x1 11.9 us: on_device(): rms = lax.all_gather(rms, 'context', axis=0, tiled=True)]
    all_to_all x2 -> x0, blocking collectives: 23.4 us -> none  [the longest x1 12.6 us: on_device(): lax.all_to_all(back, ('wide', 'context'), split_axis=0, concat_axis=0, ti...]
    convert_element_type x4 -> x0, other arithmetic: 18.1 us -> none  [the longest x1 13.9 us: on_device(): (probs * (dprobs - jnp.sum(probs * dprobs, axis=-1, keepdims=True))).asty...]
    unnamed x8 -> x0, waiting for transfers between devices: 17.4 us -> none
  transfers between devices with their start and end apart: 6 -> 0, of which waited for: 5 -> 0; matrix products, arithmetic and copies ran while one was open for 6% -> 0% of each run, Pallas kernels for 0% -> 0%
where the time goes in v3:
time: 255 us; the launch traced here: 254 us
  Pallas kernels  231 us (91%)
  local copies, waits for them, and re-layouts  15.3 us (6%)
  matrix products  4.95 us (2%)
  other arithmetic  2.97 us (1%)
    pallas_call x1, Pallas kernels, run_block(): pl.pallas_call(functools.partial(block_kernel, share), out_shape=(shape((...  190 us
    pallas_call x1, Pallas kernels, gather_weights(): pl.pallas_call(gather_kernel, out_shape=(jax.ShapeDtypeStruct((ctx_n, wid...  41 us
    unnamed x15, local copies, waits for them, and re-layouts  9.58 us

profile of v3, /device:TPU:0, one launch (start us, length us, event | category | flops | bytes accessed | tf_op | source)
XLA Modules:
  0.0 254.5 jit_solution(9624105180016763065)
XLA Ops:
  0.6 0.9 copy.26
  1.5 1.1 copy.25
  2.6 0.2 copy.27
  2.8 0.8 pad_maximum_fusion.pack
  3.5 1.3 fusion.8.small
  4.8 41.0 %shard_map.168 = (bf16[4,2,2,2,96,768]{5,4,3,2,1,0:T(8,128)(2,1)}, bf16[2,2,2,16,128]{4,3,2,1,0:T(8,128)(2,1)}) custom-call(bf16[96,768]{1,0:T(8,128)(2,1)} %pad_maximum_fusion.pack, bf16[16,128]{1,0:T(8,128)(2,1)} %fusion.8.small), custom_call_target="tpu_custom_call" | custom-call | tf_op jit(solution)/shard_map/pallas_call | solution.py:226
  45.9 0.8 copy.35
  46.6 0.7 reshape.41.refs_3_
  47.3 189.6 %shard_map.169 = (bf16[12,197,768]{2,1,0:T(8,128)(2,1)}, bf16[12,197,768]{2,1,0:T(8,128)(2,1)}, f32[96,768]{1,0:T(8,128)}, f32[4,24,128]{2,1,0:T(8,128)}, bf16[2...) custom-call(bf16[12,197,768]{2,1,0:T(8,128)(2,1)} %refs_0_.1, ...), custom_call_target="tpu_custom_call" | custom-call | tf_op jit(solution)/shard_map/pallas_call | solution.py:779
  236.9 0.0 copy-start.2
  236.9 0.0 copy-start.3
  236.9 0.8 slice.27
  237.7 0.1 copy.29
  237.8 0.7 reshape.42
  238.5 1.0 slice.28
  239.5 0.1 copy.30
  239.6 0.9 copy.31
  240.5 1.0 slice_bitcast_fusion
  241.5 0.7 copy.32
  242.2 0.0 copy-start.1
  242.2 0.9 slice_reduce_fusion
  243.1 0.6 fusion.9
  243.7 0.6 slice_bitcast_fusion.1
  244.3 3.0 %convolution_bitcast_fusion.1 = f32[1,768,768]{2,1,0:T(8,128)} fusion(bf16[256,768]{1,0:T(8,128)(2,1)} %get-tuple-element.26, bf16[256,768]{1,0:T(8,128)(2,1)} %get-tuple-element.27), kind=kOutput, calls=%fused_computation.1 | convolution fusion | flops 301989888 | bytes 3145728 | tf_op jit(solution)/shard_map/dot_general | solution.py:23
  247.3 0.0 copy-done.2
  247.3 0.0 copy-done.3
  247.3 1.9 convolution_bitcast_fusion
  249.3 0.0 copy-done.1
  249.3 0.0 copy-start
  249.3 1.9 copy.38
  251.2 1.5 copy-done
  252.6 1.8 copy.39
Async XLA Ops:
  236.9 10.4 %copy-start.2 = (bf16[256,768]{1,0:T(8,128)(2,1)S(1)}, bf16[256,768]{1,0:T(8,128)(2,1)}, u32[]{:S(2)}) copy-start(bf16[256,768]{1,0:T(8,128)(2,1)} %get-tuple-element.28) | copy-start | bytes 1179652
  236.9 10.4 %copy-start.3 = (bf16[256,768]{1,0:T(8,128)(2,1)S(1)}, bf16[256,768]{1,0:T(8,128)(2,1)}, u32[]{:S(2)}) copy-start(bf16[256,768]{1,0:T(8,128)(2,1)} %get-tuple-element.29) | copy-start | bytes 1179652
  242.2 7.0 %copy-start.1 = (bf16[12,197,768]{2,1,0:T(8,128)(2,1)S(1)}, bf16[12,197,768]{2,1,0:T(8,128)(2,1)}, u32[]{:S(2)}) copy-start(bf16[12,197,768]{2,1,0:T(8,128)(2,1)} %get-tuple-element.62) | copy-start | bytes 10893316
  249.3 3.4 %copy-start = (bf16[12,197,768]{2,1,0:T(8,128)(2,1)S(1)}, bf16[12,197,768]{2,1,0:T(8,128)(2,1)}, u32[]{:S(2)}) copy-start(bf16[12,197,768]{2,1,0:T(8,128)(2,1)} %get-tuple-element.64) | copy-start | bytes 10893316

commit v4 on v3

--- a/solution.py
+++ b/solution.py
@@ -252,13 +252,19 @@
     return val, der
 
 
-def block_kernel(share, *refs):
+def halves(values):
+    high = values.astype(bf16).astype(f32)
+    return high, values - high
+
+
+def block_kernel(share, joined, *refs):
     (
-        x_all, g_all, full, small, up, down,
+        x_all, g_all, pack, small_in, up, down,
         lo, dxo, grad, smalls, e_in, e_act, e_hid, e_dexp,
-        x_s, g_s, att_s, dx_s, nt_s, dt_s, qkv, heads, resid, logits, asq, dres_s, dn_s, rows_s,
+        x_s, g_s, att_s, n1_s, da_s, qkv, heads, probs, resid, logits, asq, dres_s, dn_s, rows_s,
         send_s, got, r32, e_s, ret, got2, eo_all, comb_all, dsm, sblk,
         part, rcv1, rcv2, rcv3, acc3, rcv4, srcv, a_buf, x_buf,
+        full_s, small_s, small_g, wsem, wrecv,
         lsem, esem, xsem, gsem, grecv, ksem, krecv, s2, r2, s3, r3, s4, r4, ss, sr, es, er, obuf_sem,
     ) = refs
     wide_n, ctx_n, y_n, w, c, y, k = spot()
@@ -267,11 +273,18 @@
     n = plane * ctx_n
     me = (w * ctx_n + c) * ten_n + y * 2 + k
     mine = (w * y_n + y) * 2 + k
-    width, packed = full.shape[1:]
+    width, packed = x_s.shape[2], pack.shape[-1]
     cols = packed // 4
     per = cols // HEAD_DIM
-    slots_n = small.shape[0] - 4
+    slots_n = rows_s.shape[0] // 8
     length = x_s.shape[1]
+    small = small_s if joined else small_in
+
+    def weight(cb, lo_col, hi_col):
+        if joined:
+            return full_s[cb, :, :, :, :, lo_col:hi_col].reshape(width, hi_col - lo_col)
+        return pack[cb, :, lo_col:hi_col]
+
     rows = grad.shape[0]
     logit_scale = 1.6 * math.sqrt(width)
     seq = near_first(c, ctx_n)
@@ -293,11 +306,22 @@
         cp.start()
     rows_s[...] = jnp.zeros_like(rows_s)
     dsm[...] = jnp.zeros_like(dsm)
-    keys, key_scale = router_unit(small[4:, :].astype(f32))
+    tall = length + -length % 16
+    gap = tall - length // 16 * 16
+    for i in range(share):
+        edge = pl.ds(i * tall + tall - gap, gap)
+        n1_s[edge, :] = jnp.zeros((gap, width), bf16)
+        da_s[edge, :] = jnp.zeros((gap, width), bf16)
+        for cb in range(ctx_n):
+            heads[cb, edge, :] = jnp.zeros((gap, cols), bf16)
+
+    def of(i):
+        return pl.ds(pl.multiple_of(i * tall, 16), length)
+
 
     def along(a, cb, i, side, own):
         ref = (lo, dxo)[a].at[cb * share + i]
-        src = (att_s, dx_s)[a].at[i] if own else ref
+        src = (att_s, x_s)[a].at[i] if own else ref
         return remote(src, ref, gsem.at[a, side, cb, i], grecv.at[a, cb, i], context=c + 2 * side - 1)
 
     def launch(a, i):
@@ -324,48 +348,168 @@
 
     pairs = [(s, i) for s in range(1, ctx_n) for i in range(share)]
     pairs.sort(key=lambda p: (p[0] + p[1], p[1]))
-    early, middle, late = pairs[:1], pairs[1:3], pairs[3:5]
-    rest = pairs[5:]
+    middle, late, rest = pairs[:1], pairs[1:4], pairs[4:]
     waves = [[p for p in pairs if p[0] + p[1] == d] for d in range(1, ctx_n + share - 1)]
+    half = rows // 2
+
+    def w_ctx(cb, side, own):
+        ref = full_s.at[cb, w, y, k]
+        return remote(pack if own else ref, ref, wsem.at[0, cb, side], wrecv.at[0, cb, 0], context=c + 2 * side - 1)
+
+    def w_leg(cb, number, h, o):
+        at = pl.ds(h * half, half)
+        slot = number * 2 + h
+        if (number == 0) == (h == 0):
+            ref = full_s.at[cb, w, y, k, at] if number == 0 else full_s.at[cb, w, :, k, at]
+            to = {"wide": lax.rem(w + o, wide_n)}
+        else:
+            ref = full_s.at[cb, w, y, k, at] if number == 0 else full_s.at[cb, :, y, k, at]
+            to = {"tensor": lax.rem(y + o, y_n) * 2 + k}
+        return remote(ref, ref, wsem.at[1 + slot, cb, o], wrecv.at[1 + slot, cb, o], **to)
+
+    def w_legs(cb, number):
+        out = []
+        for h in (0, 1):
+            on_wide = (number == 0) == (h == 0)
+            out += [w_leg(cb, number, h, o) for o in range(1, wide_n if on_wide else y_n)]
+        return out
+
+    def w_core(cb):
+        ref = full_s.at[cb, :, :, k]
+        return remote(ref, ref, wsem.at[5, cb, 0], wrecv.at[5, cb, 0], tensor=y * 2 + 1 - k)
+
+    def w_small(o):
+        j = lax.rem(mine + o, plane)
+        to = {"wide": j // ten_n, "tensor": lax.rem(j, ten_n)}
+        return remote(small_in, small_g.at[w, y, k], wsem.at[6, 0, o], wrecv.at[6, 0, o], **to)
+
+    def w_arrive(j):
+        cb = seq[j]
+        if j > 0:
+            w_ctx(cb, 0, False).wait_recv()
+            for side in (0, 1):
+
+                @pl.when(onward(cb, side))
+                def _():
+                    w_ctx(cb, side, False).start()
+
+        for cp in w_legs(cb, 0):
+            cp.start()
+
+    def w_second(j):
+        for cp in w_legs(seq[j], 0):
+            cp.wait_recv()
+        for cp in w_legs(seq[j], 1):
+            cp.start()
+
+    def w_third(j):
+        for cp in w_legs(seq[j], 1):
+            cp.wait_recv()
+        w_core(seq[j]).start()
+
+    def w_ready(j):
+        if joined:
+            w_core(seq[j]).wait_recv()
+
+    if joined:
+        full_s[c, w, y, k] = pack[...]
+        small_g[w, y, k] = small_in[...]
+    pl.semaphore_wait(bar, n - 1)
+    if joined:
+        for side in (0, 1):
+
+            @pl.when((c > 0) if side == 0 else (c < ctx_n - 1))
+            def _():
+                w_ctx(c, side, True).start()
+
+        w_arrive(0)
+        for o in range(1, plane):
+            w_small(o).start()
+        for o in range(1, plane):
+            w_small(o).wait_recv()
+        pieces = [small_g[j // ten_n, (j // 2) % y_n, j % 2][:, :rows] for j in range(plane)]
+        small_s[...] = jnp.concatenate([p.astype(f32) for p in pieces], axis=1)
+    keys, key_scale = router_unit(small[4 : 4 + slots_n, :].astype(f32))
+    keys_hi, keys_lo = halves(keys)
+    keys_two = jnp.concatenate([keys_hi, keys_lo], axis=0).astype(bf16)
+    keys_three = jnp.concatenate([keys_hi, keys_lo, keys_hi], axis=0).astype(bf16)
     for cp in ins:
         cp.wait()
-    pl.semaphore_wait(bar, n - 1)
-
-    def forward(i, carry):
-        x = x_s[i].astype(f32)
-        hat, spread = layer_stats(x)
-        normed = (hat * small[0:1, :].astype(f32) + small[2:3, :].astype(f32)).astype(bf16)
-        nt_s[i] = normed.T
-        resid[i] = x
-
-        def block(cb, carry):
-            qkv_c = mm(normed, full[cb, :, : 3 * cols]).astype(bf16)
-            qkv[i, cb] = qkv_c
+
+    def norm_first(i, carry):
+        hat, _ = layer_stats(x_s[i].astype(f32))
+        n1_s[of(i), :] = (hat * small[0:1, :].astype(f32) + small[2:3, :].astype(f32)).astype(bf16)
+        return carry
+
+    lax.fori_loop(0, share, norm_first, 0)
+
+    def between(j, i):
+        todo = {}
+        if joined:
+            todo = {
+                (0, 0): lambda: w_third(1),
+                (0, 1): lambda: w_second(2),
+                (0, 2): lambda: w_arrive(3),
+                (1, 0): lambda: w_third(2),
+                (1, 1): lambda: w_second(3),
+                (2, 0): lambda: w_third(3),
+            }
+        return todo.get((j, i))
+
+    if joined:
+        w_second(0)
+        w_arrive(1)
+        w_third(0)
+        w_second(1)
+        w_arrive(2)
+    for j in range(ctx_n):
+        w_ready(j)
+        cb = seq[j]
+        qkv_f = mm(n1_s[...], weight(cb, 0, 3 * cols))
+        qkv[cb] = jnp.concatenate([qkv_f[:, :cols] * 0.125, qkv_f[:, cols:]], axis=1).astype(bf16)
+
+        def attend(i, carry):
+            for at in range(share):
+                if between(j, at) is not None:
+                    pl.when(i == at)(between(j, at))
+            qkv_c = qkv[cb, of(i), :]
             mixed = []
             for h in range(per):
                 q, kk, v = head_parts(qkv_c, h, per)
-                p = soft(mm(q, kk, NT) * 0.125, 1)
-                mixed.append(mm(p.astype(bf16), v).astype(bf16))
-            heads_c = jnp.concatenate(mixed, axis=1)
-            heads[i, cb] = heads_c
-            resid[i] += mm(heads_c, full[cb, :, 3 * cols :], NT)
+                s = mm(q, kk, NT)
+                e = jnp.exp(s - jnp.max(s, axis=1, keepdims=True))
+                p = (e * (1.0 / jnp.sum(e, axis=1, keepdims=True))).astype(bf16)
+                probs[i, cb, h] = p
+                mixed.append(mm(p, v).astype(bf16))
+            heads[cb, of(i), :] = jnp.concatenate(mixed, axis=1)
             return carry
 
-        lax.fori_loop(0, ctx_n, block, 0)
-        res = resid[i]
-        att = res - x
-        att_s[i] = att.astype(bf16)
+        lax.fori_loop(0, share, attend, 0)
+        add = mm(heads[cb], weight(cb, 3 * cols, packed), NT)
+        if j == 0:
+            resid[...] = add
+        else:
+            resid[...] += add
+
+    def attention_out(i, carry):
+        att_s[i] = resid[of(i), :].astype(bf16)
+        launch(0, i)
+        return carry
+
+    lax.fori_loop(0, share, attention_out, 0)
+
+    def route(i, carry):
+        att = resid[of(i), :]
         asq[i] = jnp.full(asq.shape[1:], jnp.sum(att * att), f32)
-        launch(0, i)
-
-        @pl.when(i == 1)
-        def _():
-            pump(0, early)
-
+        res = x_s[i].astype(f32) + att
+        resid[of(i), :] = res
         hat2, _ = layer_stats(res)
         second = hat2 * small[1:2, :].astype(f32) + small[3:4, :].astype(f32)
         unit = second * lax.rsqrt(jnp.sum(second * second, axis=-1, keepdims=True) + norm_eps)
-        lg = logit_scale * mm(keys, unit, NT, highest)
+        unit_hi, unit_lo = halves(unit)
+        lg = mm(keys_two, unit_hi.astype(bf16), NT)
+        lg = lg[:slots_n] + lg[slots_n:] + mm(keys_two[:slots_n], unit_lo.astype(bf16), NT)
+        lg = logit_scale * lg
         logits[i] = lg
         disp = soft(lg, 1).astype(bf16)
         comb = soft(lg, 0).astype(bf16)
@@ -375,7 +519,7 @@
         rows_s[...] += mm(pick_rows(slots_n, i), slots) + mm(pick_rows(slots_n, i + 4), dexp)
         return carry
 
-    lax.fori_loop(0, share, forward, 0)
+    lax.fori_loop(0, share, route, 0)
 
     for e in range(slots_n):
         send_s[e] = rows_s[e * 8 : e * 8 + 8, :].astype(bf16)
@@ -484,7 +628,7 @@
     def backward(i, carry):
         gain1, gain2 = small[0:1, :].astype(f32), small[1:2, :].astype(f32)
         g_low = g_s[i]
-        res = resid[i]
+        res = resid[of(i), :]
         hat2, spread2 = layer_stats(res)
         second = hat2 * gain2 + small[3:4, :].astype(f32)
         tokens = second.astype(bf16)
@@ -519,15 +663,21 @@
         dlg = comb * (dcomb - jnp.sum(comb * dcomb, axis=0, keepdims=True)) + disp * (
             ddisp - jnp.sum(disp * ddisp, axis=1, keepdims=True)
         )
-        dunit = logit_scale * mm(dlg, keys, TN, highest)
-        dsm[4 : 4 + slots_n, :] += logit_scale * mm(dlg, unit, NN, highest)
+        dlg_hi, dlg_lo = halves(dlg)
+        dlg_two = jnp.concatenate([dlg_hi, dlg_lo], axis=0).astype(bf16)
+        dlg_three = jnp.concatenate([dlg_hi, dlg_hi, dlg_lo], axis=0).astype(bf16)
+        dunit = logit_scale * mm(dlg_three, keys_three, TN)
+        unit_hi, unit_lo = halves(unit)
+        dk_part = mm(dlg_two, unit_hi.astype(bf16))
+        dk_part = dk_part[:slots_n] + dk_part[slots_n:] + mm(dlg_two[:slots_n], unit_lo.astype(bf16))
+        dsm[4 : 4 + slots_n, :] += logit_scale * dk_part
         dsec = dtok + row_scale * (dunit - unit * jnp.sum(unit * dunit, axis=-1, keepdims=True))
         dsm[1:2, :] += jnp.sum(dsec * hat2, axis=0, keepdims=True)
         dsm[3:4, :] += jnp.sum(dsec, axis=0, keepdims=True)
         dres = g_low.astype(f32) + norm_back(dsec * gain2, hat2, spread2)
         dres_s[...] = dres
         dattn = dres.astype(bf16)
-        dt_s[i] = dattn.T
+        da_s[of(i), :] = dattn
         hat, spread = layer_stats(x_s[i].astype(f32))
         dn_s[...] = jnp.zeros_like(dn_s)
 
@@ -542,35 +692,36 @@
                 def _():
                     pump(1, waves[j - 1])
 
-            proj = full[cb, :, 3 * cols :]
-            dheads = mm(dattn, proj).astype(bf16)
-            qkv_c = qkv[i, cb]
+            dheads = mm(dattn, weight(cb, 3 * cols, packed)).astype(bf16)
+            qkv_c = qkv[cb, of(i), :]
+            along_heads = dheads.astype(f32) * heads[cb, of(i), :].astype(f32)
             grads = [[], [], []]
             for h in range(per):
                 q, kk, v = head_parts(qkv_c, h, per)
-                dh = dheads[:, h * HEAD_DIM : (h + 1) * HEAD_DIM]
-                p = soft(mm(q, kk, NT) * 0.125, 1)
-                dp = mm(dh, v, NT)
-                dsc = (p * (dp - jnp.sum(p * dp, axis=1, keepdims=True))).astype(bf16)
+                at = slice(h * HEAD_DIM, (h + 1) * HEAD_DIM)
+                dh = dheads[:, at]
+                p = probs[i, cb, h]
+                dp = mm(dh, v, NT) - jnp.sum(along_heads[:, at], axis=1, keepdims=True)
+                dsc = (p.astype(f32) * dp).astype(bf16)
                 grads[0].append((mm(dsc, kk) * 0.125).astype(bf16))
-                grads[1].append((mm(dsc, q, TN) * 0.125).astype(bf16))
-                grads[2].append(mm(p.astype(bf16), dh, TN).astype(bf16))
+                grads[1].append(mm(dsc, q, TN).astype(bf16))
+                grads[2].append(mm(p, dh, TN).astype(bf16))
             dqkv = jnp.concatenate(grads[0] + grads[1] + grads[2], axis=1)
-            qkv[i, cb] = dqkv
-            dn_s[...] += mm(dqkv, full[cb, :, : 3 * cols], NT)
+            qkv[cb, of(i), :] = dqkv
+            dn_s[...] += mm(dqkv, weight(cb, 0, 3 * cols), NT)
             return carry
 
         lax.fori_loop(0, ctx_n, block, 0)
         dn = dn_s[...]
         dsm[0:1, :] += jnp.sum(dn * hat, axis=0, keepdims=True)
         dsm[2:3, :] += jnp.sum(dn, axis=0, keepdims=True)
-        dx_s[i] = (dres_s[...] + norm_back(dn * gain1, hat, spread)).astype(bf16)
+        x_s[i] = (dres_s[...] + norm_back(dn * gain1, hat, spread)).astype(bf16)
         launch(1, i)
         return carry
 
     sblk[plane] = jnp.zeros(sblk.shape[1:], f32)
     lax.fori_loop(0, share, backward, 0)
-    outs = [pltpu.make_async_copy(dx_s, dxo.at[pl.ds(c * share, share)], lsem.at[1])]
+    outs = [pltpu.make_async_copy(x_s, dxo.at[pl.ds(c * share, share)], lsem.at[1])]
     for cp in outs:
         cp.start()
     dkeys = dsm[4 : 4 + slots_n, :]
@@ -579,9 +730,11 @@
     def core(cc):
         return remote(part.at[cc, :, :, 1 - k], rcv1.at[cc], ksem.at[cc], krecv.at[cc], tensor=y * 2 + 1 - k)
 
+    normed_t = n1_s[...].T
+    dattn_t = da_s[...].T
     for cc in range(ctx_n):
-        from_qkv = sum(mm(nt_s[i], qkv[i, cc]) for i in range(share)).astype(bf16)
-        from_proj = sum(mm(dt_s[i], heads[i, cc]) for i in range(share)).astype(bf16)
+        from_qkv = mm(normed_t, qkv[cc]).astype(bf16)
+        from_proj = mm(dattn_t, heads[cc]).astype(bf16)
         for j in range(plane):
             at = (cc, j // ten_n, (j // 2) % y_n, j % 2)
             part[at + (slice(None), slice(0, 3 * cols))] = from_qkv[j * rows : (j + 1) * rows]
@@ -739,6 +892,21 @@
                 hop(cc, number, o).wait_send()
     for cp in outs:
         cp.wait()
+    if joined:
+        for o in range(1, plane):
+            w_small(o).wait_send()
+        for cb in range(ctx_n):
+            for number in (0, 1):
+                for cp in w_legs(cb, number):
+                    cp.wait_send()
+            w_core(cb).wait_send()
+            for side in (0, 1):
+                go = (cb >= c, c > 0) if side == 0 else (cb <= c, c < ctx_n - 1)
+
+                @pl.when(jnp.logical_and(*go))
+                def _():
+                    w_ctx(cb, side, True).wait_send()
+
     for a in (0, 1):
         for i in range(share):
             for side in (0, 1):
@@ -755,29 +923,30 @@
                 along(1, seq[step], i, side, False).wait_send()
 
 
-def run_block(x_all, g_all, full, small, up, down, rows, share):
+def run_block(x_all, g_all, pack, small, slots_n, up, down, rows, share):
     wide_n, ctx_n, ten_n = (lax.axis_size(a) for a in ("wide", "context", "tensor"))
     y_n = ten_n // 2
     plane = wide_n * ten_n
     n = plane * ctx_n
     most = max(wide_n, y_n)
     images, length, width = x_all.shape
-    packed = full.shape[2]
+    packed = pack.shape[-1]
+    joined = pack.ndim == 2
     cols = packed // 4
     ff = up.shape[1]
-    slots_n = small.shape[0] - 4
     par8 = 4 + slots_n + -(4 + slots_n) % 8
     lanes = rows + -rows % 128
     blk = (rows, packed)
     acts = (share, length, width)
     wide_len = length + -length % 128
+    tall = length + -length % 16
     dma = pltpu.SemaphoreType.DMA
     vm = pl.BlockSpec(memory_space=pltpu.VMEM)
     hbm = pl.BlockSpec(memory_space=pl.ANY)
     V = pltpu.VMEM
     shape = jax.ShapeDtypeStruct
     return pl.pallas_call(
-        functools.partial(block_kernel, share),
+        functools.partial(block_kernel, share, joined),
         out_shape=(
             shape((images, length, width), bf16),
             shape((images, length, width), bf16),
@@ -791,12 +960,13 @@
         in_specs=[hbm, hbm] + [vm] * 4,
         out_specs=(hbm, hbm, vm, vm) + (hbm,) * 4,
         scratch_shapes=[
-            V(acts, bf16), V(acts, bf16), V(acts, bf16), V(acts, bf16),
-            V((share, width, length), bf16),
-            V((share, width, length), bf16),
-            V((share, ctx_n, length, 3 * cols), bf16),
-            V((share, ctx_n, length, cols), bf16),
-            V(acts, f32),
+            V(acts, bf16), V(acts, bf16), V(acts, bf16),
+            V((share * tall, width), bf16),
+            V((share * tall, width), bf16),
+            V((ctx_n, share * tall, 3 * cols), bf16),
+            V((ctx_n, share * tall, cols), bf16),
+            V((share, ctx_n, cols // HEAD_DIM, length, length), bf16),
+            V((share * tall, width), f32),
             V((share, slots_n, length), f32),
             V((share, 8, lanes), f32),
             V((length, width), f32),
@@ -821,6 +991,10 @@
             V((plane, par8, lanes), f32),
             V((2, length, width), bf16),
             V((2, length, width), bf16),
+            V((ctx_n, wide_n, y_n, 2) + blk if joined else (8, 128), bf16),
+            V((small.shape[0], width) if joined else (8, 128), f32),
+            V((wide_n, y_n, 2) + small.shape if joined else (8, 128), bf16),
+            dma((7, ctx_n, plane) if joined else (1,)), dma((7, ctx_n, plane) if joined else (1,)),
             dma((2,)), dma((4,)), dma((4,)),
             dma((2, 2, ctx_n, share)), dma((2, ctx_n, share)),
             dma((ctx_n,)), dma((ctx_n,)),
@@ -834,7 +1008,7 @@
         compiler_params=pltpu.CompilerParams(
             collective_id=2, has_side_effects=True, vmem_limit_bytes=67043328
         ),
-    )(x_all, g_all, full, small, up, down)
+    )(x_all, g_all, pack, small, up, down)
 
 
 def on_device(
@@ -860,12 +1034,15 @@
     small = jnp.concatenate([norm_gains, norm_biases, router_keys.T], axis=0)
     params = small.shape[0]
     small = jnp.pad(small, ((0, -params % 16), (0, lanes - rows)))
-    weights, small = gather_weights(pack, small)
-    weights = weights.reshape(ctx_n, width, 4 * cols)
-    small = small.reshape((-1,) + small.shape[3:])[:, :params, :rows]
-    small = small.transpose(1, 0, 2).reshape(params, width)
+    if rows % 32 == 0:
+        weights = pack
+    else:
+        weights, small = gather_weights(pack, small)
+        weights = weights.reshape(ctx_n, width, 4 * cols)
+        small = small.reshape((-1,) + small.shape[3:])[:, :params, :rows]
+        small = small.transpose(1, 0, 2).reshape(params, width)
     layer_output, input_grad, dpack, dsmall, e_in, e_act, e_hid, e_dexp = run_block(
-        layer_input, out_cotangent, weights, small, up_weight[0], down_weight[0], rows, share
+        layer_input, out_cotangent, weights, small, slots_n, up_weight[0], down_weight[0], rows, share
     )
     up_grad = mm(e_in, e_hid, TN)
     down_grad = mm(e_act, e_dexp, TN)

time: 255 us -> 250 us (0.980)
  Pallas kernels: 231 us -> 226 us
    pallas_call x2 -> x1, Pallas kernels: 231 us -> 226 us  [run_block(): pl.pallas_call(functools.partial(block_kernel, share, joined), out_shape=...]
    unnamed x15 -> x14, local copies, waits for them, and re-layouts: 9.58 us -> 8.81 us
where the time goes in v4:
time: 250 us; the launch traced here: 249 us
  Pallas kernels  226 us (90%)
  local copies, waits for them, and re-layouts  13.8 us (6%)
  matrix products  4.95 us (2%)
  other arithmetic  2.97 us (1%)
    pallas_call x1, Pallas kernels, run_block(): pl.pallas_call(functools.partial(block_kernel, share, joined), out_shape=...  226 us
    unnamed x14, local copies, waits for them, and re-layouts  8.81 us

profile of v4, /device:TPU:0, one launch (start us, length us, event | category | flops | bytes accessed | tf_op | source)
XLA Modules:
  0.0 248.7 jit_solution(10825153276576290263)
XLA Ops:
  0.6 0.9 copy.25
  1.5 1.1 copy.24
  2.6 0.2 copy.26
  2.8 0.8 pad_maximum_fusion.refs_2_
  3.5 1.3 fusion.8.refs_3_
  4.8 226.3 %shard_map.168 = (bf16[12,197,768]{2,1,0:T(8,128)(2,1)}, bf16[12,197,768]{2,1,0:T(8,128)(2,1)}, f32[96,768]{1,0:T(8,128)}, f32[4,24,128]{2,1,0:T(8,128)}, bf16[2...) custom-call(bf16[12,197,768]{2,1,0:T(8,128)(2,1)} %refs_0_.1, ...), custom_call_target="tpu_custom_call" | custom-call | tf_op jit(solution)/shard_map/pallas_call | solution.py:948
  231.1 0.0 copy-start.2
  231.1 0.0 copy-start.3
  231.1 0.8 slice.23
  231.9 0.1 copy.27
  232.0 0.7 reshape.30
  232.7 1.0 slice.24
  233.7 0.1 copy.28
  233.8 0.9 copy.29
  234.7 1.0 slice_bitcast_fusion
  235.7 0.7 copy.30
  236.4 0.0 copy-start.1
  236.4 0.9 slice_reduce_fusion
  237.3 0.6 fusion.9
  237.9 0.6 slice_bitcast_fusion.1
  238.5 3.0 %convolution_bitcast_fusion.1 = f32[1,768,768]{2,1,0:T(8,128)} fusion(bf16[256,768]{1,0:T(8,128)(2,1)} %get-tuple-element.22, bf16[256,768]{1,0:T(8,128)(2,1)} %get-tuple-element.23), kind=kOutput, calls=%fused_computation.1 | convolution fusion | flops 301989888 | bytes 3145728 | tf_op jit(solution)/shard_map/dot_general | solution.py:23
  241.5 0.0 copy-done.2
  241.5 0.0 copy-done.3
  241.5 1.9 convolution_bitcast_fusion
  243.5 0.0 copy-done.1
  243.5 0.0 copy-start
  243.5 1.9 copy.33
  245.3 1.5 copy-done
  246.8 1.8 copy.34
Async XLA Ops:
  231.1 10.4 %copy-start.2 = (bf16[256,768]{1,0:T(8,128)(2,1)S(1)}, bf16[256,768]{1,0:T(8,128)(2,1)}, u32[]{:S(2)}) copy-start(bf16[256,768]{1,0:T(8,128)(2,1)} %get-tuple-element.24) | copy-start | bytes 1179652
  231.1 10.4 %copy-start.3 = (bf16[256,768]{1,0:T(8,128)(2,1)S(1)}, bf16[256,768]{1,0:T(8,128)(2,1)}, u32[]{:S(2)}) copy-start(bf16[256,768]{1,0:T(8,128)(2,1)} %get-tuple-element.25) | copy-start | bytes 1179652
  236.4 7.0 %copy-start.1 = (bf16[12,197,768]{2,1,0:T(8,128)(2,1)S(1)}, bf16[12,197,768]{2,1,0:T(8,128)(2,1)}, u32[]{:S(2)}) copy-start(bf16[12,197,768]{2,1,0:T(8,128)(2,1)} %get-tuple-element.58) | copy-start | bytes 10893316
  243.5 3.4 %copy-start = (bf16[12,197,768]{2,1,0:T(8,128)(2,1)S(1)}, bf16[12,197,768]{2,1,0:T(8,128)(2,1)}, u32[]{:S(2)}) copy-start(bf16[12,197,768]{2,1,0:T(8,128)(2,1)} %get-tuple-element.60) | copy-start | bytes 10893316

commit v5 on v4

--- a/solution.py
+++ b/solution.py
@@ -262,7 +262,7 @@
         x_all, g_all, pack, small_in, up, down,
         lo, dxo, grad, smalls, e_in, e_act, e_hid, e_dexp,
         x_s, g_s, att_s, n1_s, da_s, qkv, heads, probs, resid, logits, asq, dres_s, dn_s, rows_s,
-        send_s, got, r32, e_s, ret, got2, eo_all, comb_all, dsm, sblk,
+        send_s, got, r32, e_s, ret, got2, back_g, eo_all, comb_all, dsm, sblk,
         part, rcv1, rcv2, rcv3, acc3, rcv4, srcv, a_buf, x_buf,
         full_s, small_s, small_g, wsem, wrecv,
         lsem, esem, xsem, gsem, grecv, ksem, krecv, s2, r2, s3, r3, s4, r4, ss, sr, es, er, obuf_sem,
@@ -336,20 +336,25 @@
             return jnp.logical_and(cb > c, c > 0)
         return jnp.logical_and(cb < c, c < ctx_n - 1)
 
-    def pump(a, todo):
-        for step, i in todo:
+    def pump(a, steps, i):
+        for step in steps:
             cb = seq[step]
-            along(a, cb, i, 0, False).wait_recv()
             for side in (0, 1):
 
                 @pl.when(onward(cb, side))
                 def _():
+                    along(a, cb, i, 0, False).wait_recv()
                     along(a, cb, i, side, False).start()
 
-    pairs = [(s, i) for s in range(1, ctx_n) for i in range(share)]
-    pairs.sort(key=lambda p: (p[0] + p[1], p[1]))
-    middle, late, rest = pairs[:1], pairs[1:4], pairs[4:]
-    waves = [[p for p in pairs if p[0] + p[1] == d] for d in range(1, ctx_n + share - 1)]
+    def arrived(a, step, i):
+        cb = seq[step]
+
+        @pl.when(jnp.logical_not(jnp.logical_or(onward(cb, 0), onward(cb, 1))))
+        def _():
+            along(a, cb, i, 0, False).wait_recv()
+
+    near, far = list(range(1, min(3, ctx_n))), list(range(3, ctx_n))
+
     half = rows // 2
 
     def w_ctx(cb, side, own):
@@ -493,7 +498,6 @@
 
     def attention_out(i, carry):
         att_s[i] = resid[of(i), :].astype(bf16)
-        launch(0, i)
         return carry
 
     lax.fori_loop(0, share, attention_out, 0)
@@ -523,21 +527,29 @@
 
     for e in range(slots_n):
         send_s[e] = rows_s[e * 8 : e * 8 + 8, :].astype(bf16)
-    got[me] = send_s[w * ctx_n + c]
-
-    def send_out(o, carry):
-        d = lax.rem(me + o, n)
-        remote(send_s.at[d // ten_n], got.at[me], esem.at[0], esem.at[1], **place(d)).start()
-        return carry
-
-    lax.fori_loop(1, n, send_out, 0)
-
-    def drain(ref, sem):
-        some = ref.at[pl.ds(0, n - 1)]
+    spot_e = w * ctx_n + c
+    spot_t = y * 2 + k
+    pairs_n = wide_n * ctx_n
+
+    def expert_at(o):
+        p = lax.rem(spot_e + o, pairs_n)
+        return p, {"wide": p // ctx_n, "context": lax.rem(p, ctx_n)}
+
+    def drain(ref, count, sem):
+        some = ref.at[pl.ds(0, count)]
         pltpu.make_async_copy(some, some, sem).wait()
 
-    pump(0, middle)
-    drain(got, esem.at[1])
+    for o in range(1, pairs_n):
+        p, to = expert_at(o)
+        remote(send_s.at[p], got.at[spot_t, spot_e], esem.at[0], esem.at[1], **to).start()
+    got[spot_t, spot_e] = send_s[spot_e]
+    for i in range(share):
+        launch(0, i)
+    drain(got.at[spot_t], pairs_n - 1, esem.at[1])
+    for o in range(1, ten_n):
+        mine_in = got.at[spot_t]
+        remote(mine_in, mine_in, esem.at[2], esem.at[3], tensor=lax.rem(spot_t + o, ten_n)).start()
+    drain(got, ten_n - 1, esem.at[3])
 
     group = min(n, 32)
     chunk = group * 8
@@ -550,7 +562,7 @@
 
     def experts(b, carry):
         def widen(j, carry):
-            r32[pl.ds(pl.multiple_of(j * 8, 8), 8), :] = got[b * group + j].astype(f32)
+            r32[pl.ds(pl.multiple_of(j * 8, 8), 8), :] = got[(b * group + j) // pairs_n, lax.rem(b * group + j, pairs_n)].astype(f32)
             return carry
 
         lax.fori_loop(0, group, widen, 0)
@@ -577,7 +589,7 @@
             expert_out(b, j).start()
 
         def narrow(j, carry):
-            ret[b * group + j] = r32[pl.ds(pl.multiple_of(j * 8, 8), 8), :].astype(bf16)
+            ret[(b * group + j) // pairs_n, lax.rem(b * group + j, pairs_n)] = r32[pl.ds(pl.multiple_of(j * 8, 8), 8), :].astype(bf16)
             return carry
 
         lax.fori_loop(0, group, narrow, 0)
@@ -585,24 +597,34 @@
 
     lax.fori_loop(0, n // group, experts, 0)
 
-    def send_back(o, carry):
-        d = lax.rem(me + o, n)
-        remote(ret.at[d], got2.at[me], esem.at[2], esem.at[3], **place(d)).start()
+    for o in range(1, ten_n):
+        p = lax.rem(spot_t + o, ten_n)
+        remote(ret.at[p], got2.at[spot_t], esem.at[4], esem.at[5], tensor=p).start()
+    got2[spot_t] = ret[spot_t]
+    drain(got2, ten_n - 1, esem.at[5])
+    drain(send_s, pairs_n - 1, esem.at[0])
+
+    def total(e, carry):
+        s = got2[0, e].astype(f32)
+        for t in range(1, ten_n):
+            s = s + got2[t, e].astype(f32)
+        send_s[e] = s.astype(bf16)
         return carry
 
-    lax.fori_loop(1, n, send_back, 0)
-    got2[me] = ret[me]
-    pump(0, late)
-    drain(got2, esem.at[3])
-
-    def total(e, carry):
-        s = got2[e * ten_n].astype(f32)
-        for t in range(1, ten_n):
-            s = s + got2[e * ten_n + t].astype(f32)
-        rows_s[pl.ds(pl.multiple_of(e * 8, 8), 8), :] = s
+    lax.fori_loop(0, pairs_n, total, 0)
+    for o in range(1, pairs_n):
+        p, to = expert_at(o)
+        remote(send_s.at[p], back_g.at[spot_e], esem.at[6], esem.at[7], **to).start()
+    back_g[spot_e] = send_s[spot_e]
+    for i in range(share):
+        pump(0, near, i)
+    drain(back_g, pairs_n - 1, esem.at[7])
+
+    def spread(e, carry):
+        rows_s[pl.ds(pl.multiple_of(e * 8, 8), 8), :] = back_g[e].astype(f32)
         return carry
 
-    lax.fori_loop(0, slots_n, total, 0)
+    lax.fori_loop(0, slots_n, spread, 0)
     back = rows_s[...].astype(bf16)
     for i in range(share):
         eo_all[c, i] = mm(pick_rows(slots_n, i), back, TN).astype(bf16)
@@ -618,7 +640,7 @@
         img = seq[step] * share + i
         return (
             pltpu.make_async_copy(lo.at[img], a_buf.at[slot], obuf_sem.at[0, slot]),
-            pltpu.make_async_copy(x_all.at[img], x_buf.at[slot], obuf_sem.at[1, slot]),
+            pltpu.make_async_copy(x_all.at[img], x_buf, obuf_sem.at[1, slot]),
         )
 
     def put(step, i, slot):
@@ -681,16 +703,19 @@
         hat, spread = layer_stats(x_s[i].astype(f32))
         dn_s[...] = jnp.zeros_like(dn_s)
 
-        @pl.when(i == 0)
-        def _():
-            pump(0, rest)
-
         def block(cb, carry):
-            for j in range(1, share):
-
-                @pl.when(jnp.logical_and(i == j, cb == ctx_n // 2))
+            for at, a, steps, img in (
+                ((0, 1), 0, far, 0),
+                ((0, 3), 0, far, 1),
+                ((1, 0), 0, far, 2),
+                ((1, 3), 1, near, 0),
+                ((2, 2), 1, far, 0),
+                ((2, 3), 1, near, 1),
+            ):
+
+                @pl.when(jnp.logical_and(i == at[0], cb == at[1]))
                 def _():
-                    pump(1, waves[j - 1])
+                    pump(a, steps, img)
 
             dheads = mm(dattn, weight(cb, 3 * cols, packed)).astype(bf16)
             qkv_c = qkv[cb, of(i), :]
@@ -740,8 +765,9 @@
             part[at + (slice(None), slice(0, 3 * cols))] = from_qkv[j * rows : (j + 1) * rows]
             part[at + (slice(None), slice(3 * cols, packed))] = from_proj[j * rows : (j + 1) * rows]
         core(cc).start()
-        if cc == ctx_n // 2:
-            pump(1, waves[2] if len(waves) > 2 else [])
+        if cc == ctx_n - 1:
+            pump(1, far, 1)
+            pump(1, near, 2)
     for j in range(plane):
         sblk[j, :, :rows] = dsm[:, j * rows : (j + 1) * rows]
 
@@ -778,7 +804,6 @@
                 rcv1[cc, wi, yi] = (part[cc, wi, yi, k].astype(f32) + rcv1[cc, wi, yi].astype(f32)).astype(bf16)
         for o in peers(cc, 2):
             hop(cc, 2, o).start()
-    pump(1, waves[3] if len(waves) > 3 else [])
 
     for o in range(1, ctx_n):
         p = lax.rem(c + ctx_n - o, ctx_n)
@@ -798,13 +823,14 @@
                 def _():
                     along(0, cb, i, side, False).wait_send()
 
+            arrived(0, step, i)
             put(step, i, slot).wait()
             for cp in fetch(step, i, slot):
                 cp.start()
             for cp in fetch(step, i, slot):
                 cp.wait()
             mixed = mm(comb_all[cb, i, :, :length], eo_all[cb, i], TN)
-            out = x_buf[slot].astype(f32) + a_buf[slot].astype(f32) + mixed
+            out = x_buf[...].astype(f32) + a_buf[slot].astype(f32) + mixed
             a_buf[slot] = out.astype(bf16)
             put(step, i, slot).start()
 
@@ -837,7 +863,7 @@
 
     for o in range(1, ctx_n):
         small2(o, c).start()
-    pump(1, waves[4] if len(waves) > 4 else [])
+    pump(1, far, 2)
     mix_some(third, 2 * third)
 
     def last(cc):
@@ -856,8 +882,8 @@
             last(cc).start()
 
     mix_some(2 * third, len(order))
-    for wave in waves[5:]:
-        pump(1, wave)
+    for step, i in order:
+        arrived(1, step, i)
     tot = acc3[c].astype(f32)
     for o in range(1, ctx_n):
         p = lax.rem(c + o, ctx_n)
@@ -869,13 +895,9 @@
         put(0, 0, slot).wait()
     for j in range(4):
         expert_out(0, j).wait()
-    drain(ret, esem.at[2])
-
-    def sent(o, carry):
-        pltpu.make_async_copy(send_s.at[0], send_s.at[0], esem.at[0]).wait()
-        return carry
-
-    lax.fori_loop(1, n, sent, 0)
+    drain(got, ten_n - 1, esem.at[2])
+    drain(ret, ten_n - 1, esem.at[4])
+    drain(send_s, pairs_n - 1, esem.at[6])
     for o in range(1, ctx_n):
         p = lax.rem(c + ctx_n - o, ctx_n)
         small2(o, p).wait_recv()
@@ -973,11 +995,12 @@
             V((length, width), f32),
             V((slots_n * 8, width), f32),
             V((slots_n, 8, width), bf16),
-            V((n, 8, width), bf16),
+            V((ten_n, slots_n, 8, width), bf16),
             V((min(n, 32) * 8, width), f32),
             V((4, min(n, 32) * 8, width), bf16),
-            V((n, 8, width), bf16),
-            V((n, 8, width), bf16),
+            V((ten_n, slots_n, 8, width), bf16),
+            V((ten_n, slots_n, 8, width), bf16),
+            V((slots_n, 8, width), bf16),
             V((ctx_n, share, slots_n, width), bf16),
             V((ctx_n, share, slots_n, wide_len), bf16),
             V((par8, width), f32),
@@ -990,12 +1013,12 @@
             V((ctx_n,) + blk, bf16),
             V((plane, par8, lanes), f32),
             V((2, length, width), bf16),
-            V((2, length, width), bf16),
+            V((length, width), bf16),
             V((ctx_n, wide_n, y_n, 2) + blk if joined else (8, 128), bf16),
             V((small.shape[0], width) if joined else (8, 128), f32),
             V((wide_n, y_n, 2) + small.shape if joined else (8, 128), bf16),
             dma((7, ctx_n, plane) if joined else (1,)), dma((7, ctx_n, plane) if joined else (1,)),
-            dma((2,)), dma((4,)), dma((4,)),
+            dma((2,)), dma((8,)), dma((4,)),
             dma((2, 2, ctx_n, share)), dma((2, ctx_n, share)),
             dma((ctx_n,)), dma((ctx_n,)),
             dma((ctx_n, most)), dma((ctx_n, most)),

time: 250 us -> 213 us (0.85)
  Pallas kernels: 226 us -> 190 us
    pallas_call x1, Pallas kernels: 226 us -> 190 us  [run_block(): pl.pallas_call(functools.partial(block_kernel, share, joined), out_shape=...]
where the time goes in v5:
time: 213 us; the launch traced here: 212 us
  Pallas kernels  190 us (89%)
  local copies, waits for them, and re-layouts  13.8 us (6%)
  matrix products  4.95 us (2%)
  other arithmetic  2.97 us (1%)
    pallas_call x1, Pallas kernels, run_block(): pl.pallas_call(functools.partial(block_kernel, share, joined), out_shape=...  190 us
    unnamed x14, local copies, waits for them, and re-layouts  8.81 us
    dot_general x2, matrix products, mm(): lax.dot_general(a, b, dims, precision=precision, preferred_element_type=f32)  4.95 us

profile of v5, /device:TPU:0, one launch (start us, length us, event | category | flops | bytes accessed | tf_op | source)
XLA Modules:
  0.0 212.2 jit_solution(12604708050020345264)
XLA Ops:
  0.6 0.9 copy.25
  1.5 1.1 copy.24
  2.6 0.2 copy.26
  2.8 0.8 pad_maximum_fusion.refs_2_
  3.5 1.3 fusion.8.refs_3_
  4.8 189.8 %shard_map.168 = (bf16[12,197,768]{2,1,0:T(8,128)(2,1)}, bf16[12,197,768]{2,1,0:T(8,128)(2,1)}, f32[96,768]{1,0:T(8,128)}, f32[4,24,128]{2,1,0:T(8,128)}, bf16[2...) custom-call(bf16[12,197,768]{2,1,0:T(8,128)(2,1)} %refs_0_.1, ...), custom_call_target="tpu_custom_call" | custom-call | tf_op jit(solution)/shard_map/pallas_call | solution.py:970
  194.7 0.0 copy-start.2
  194.7 0.0 copy-start.3
  194.7 0.8 slice.23
  195.5 0.1 copy.27
  195.6 0.7 reshape.30
  196.2 1.0 slice.24
  197.2 0.1 copy.28
  197.4 0.9 copy.29
  198.2 1.0 slice_bitcast_fusion
  199.2 0.7 copy.30
  200.0 0.0 copy-start.1
  200.0 0.9 slice_reduce_fusion
  200.9 0.6 fusion.9
  201.5 0.6 slice_bitcast_fusion.1
  202.1 3.0 %convolution_bitcast_fusion.1 = f32[1,768,768]{2,1,0:T(8,128)} fusion(bf16[256,768]{1,0:T(8,128)(2,1)} %get-tuple-element.22, bf16[256,768]{1,0:T(8,128)(2,1)} %get-tuple-element.23), kind=kOutput, calls=%fused_computation.1 | convolution fusion | flops 301989888 | bytes 3145728 | tf_op jit(solution)/shard_map/dot_general | solution.py:23
  205.1 0.0 copy-done.2
  205.1 0.0 copy-done.3
  205.1 1.9 convolution_bitcast_fusion
  207.0 0.0 copy-done.1
  207.0 0.0 copy-start
  207.0 1.9 copy.33
  208.9 1.5 copy-done
  210.4 1.8 copy.34
Async XLA Ops:
  194.7 10.4 %copy-start.2 = (bf16[256,768]{1,0:T(8,128)(2,1)S(1)}, bf16[256,768]{1,0:T(8,128)(2,1)}, u32[]{:S(2)}) copy-start(bf16[256,768]{1,0:T(8,128)(2,1)} %get-tuple-element.24) | copy-start | bytes 1179652
  194.7 10.4 %copy-start.3 = (bf16[256,768]{1,0:T(8,128)(2,1)S(1)}, bf16[256,768]{1,0:T(8,128)(2,1)}, u32[]{:S(2)}) copy-start(bf16[256,768]{1,0:T(8,128)(2,1)} %get-tuple-element.25) | copy-start | bytes 1179652
  200.0 7.0 %copy-start.1 = (bf16[12,197,768]{2,1,0:T(8,128)(2,1)S(1)}, bf16[12,197,768]{2,1,0:T(8,128)(2,1)}, u32[]{:S(2)}) copy-start(bf16[12,197,768]{2,1,0:T(8,128)(2,1)} %get-tuple-element.58) | copy-start | bytes 10893316
  207.0 3.4 %copy-start = (bf16[12,197,768]{2,1,0:T(8,128)(2,1)S(1)}, bf16[12,197,768]{2,1,0:T(8,128)(2,1)}, u32[]{:S(2)}) copy-start(bf16[12,197,768]{2,1,0:T(8,128)(2,1)} %get-tuple-element.60) | copy-start | bytes 10893316

commit v6 on v5

--- a/solution.py
+++ b/solution.py
@@ -259,12 +259,12 @@
 
 def block_kernel(share, joined, *refs):
     (
-        x_all, g_all, pack, small_in, up, down,
+        x_all, g_all, qkv_w, proj_w, gains_w, biases_w, router_w, up, down,
         lo, dxo, grad, smalls, e_in, e_act, e_hid, e_dexp,
         x_s, g_s, att_s, n1_s, da_s, qkv, heads, probs, resid, logits, asq, dres_s, dn_s, rows_s,
         send_s, got, r32, e_s, ret, got2, back_g, eo_all, comb_all, dsm, sblk,
         part, rcv1, rcv2, rcv3, acc3, rcv4, srcv, a_buf, x_buf,
-        full_s, small_s, small_g, wsem, wrecv,
+        full_s, small_s, small_g, pack_s, small_p, turn, wsem, wrecv,
         lsem, esem, xsem, gsem, grecv, ksem, krecv, s2, r2, s3, r3, s4, r4, ss, sr, es, er, obuf_sem,
     ) = refs
     wide_n, ctx_n, y_n, w, c, y, k = spot()
@@ -273,7 +273,8 @@
     n = plane * ctx_n
     me = (w * ctx_n + c) * ten_n + y * 2 + k
     mine = (w * y_n + y) * 2 + k
-    width, packed = x_s.shape[2], pack.shape[-1]
+    width, packed = x_s.shape[2], grad.shape[1]
+    pack, small_in = (pack_s, small_p) if joined else (qkv_w, proj_w)
     cols = packed // 4
     per = cols // HEAD_DIM
     slots_n = rows_s.shape[0] // 8
@@ -417,6 +418,12 @@
             w_core(seq[j]).wait_recv()
 
     if joined:
+        turn[:cols, :rows] = proj_w[...].astype(f32)
+        pieces = [qkv_w[j] for j in range(3)] + [turn[...].T[:rows, :cols].astype(bf16)]
+        pack_s[...] = jnp.concatenate(pieces, axis=1)
+        lines = jnp.concatenate([r[...].astype(f32) for r in (gains_w, biases_w, router_w)], axis=0)
+        turn[: lines.shape[0], :rows] = lines
+        small_p[...] = turn[: small_p.shape[0], : small_p.shape[1]].astype(bf16)
         full_s[c, w, y, k] = pack[...]
         small_g[w, y, k] = small_in[...]
     pl.semaphore_wait(bar, n - 1)
@@ -945,15 +952,19 @@
                 along(1, seq[step], i, side, False).wait_send()
 
 
-def run_block(x_all, g_all, pack, small, slots_n, up, down, rows, share):
+def run_block(x_all, g_all, given, slots_n, up, down, rows, share):
     wide_n, ctx_n, ten_n = (lax.axis_size(a) for a in ("wide", "context", "tensor"))
     y_n = ten_n // 2
     plane = wide_n * ten_n
     n = plane * ctx_n
     most = max(wide_n, y_n)
     images, length, width = x_all.shape
-    packed = pack.shape[-1]
-    joined = pack.ndim == 2
+    packed = 4 * (width // ctx_n)
+    joined = len(given) == 5
+    small_rows = 4 + slots_n + -(4 + slots_n) % 16
+    if not joined:
+        given = tuple(given) + (given[1],) * 3
+    up8 = lambda v, m: v + -v % m
     cols = packed // 4
     ff = up.shape[1]
     par8 = 4 + slots_n + -(4 + slots_n) % 8
@@ -979,7 +990,7 @@
             shape((n * 8, ff), bf16),
             shape((n * 8, width), bf16),
         ),
-        in_specs=[hbm, hbm] + [vm] * 4,
+        in_specs=[hbm, hbm] + [vm] * 2 + [vm if joined else hbm] * 3 + [vm] * 2,
         out_specs=(hbm, hbm, vm, vm) + (hbm,) * 4,
         scratch_shapes=[
             V(acts, bf16), V(acts, bf16), V(acts, bf16),
@@ -1015,8 +1026,11 @@
             V((2, length, width), bf16),
             V((length, width), bf16),
             V((ctx_n, wide_n, y_n, 2) + blk if joined else (8, 128), bf16),
-            V((small.shape[0], width) if joined else (8, 128), f32),
-            V((wide_n, y_n, 2) + small.shape if joined else (8, 128), bf16),
+            V((small_rows, width) if joined else (8, 128), f32),
+            V((wide_n, y_n, 2, small_rows, lanes) if joined else (8, 128), bf16),
+            V(blk if joined else (8, 128), bf16),
+            V((small_rows, lanes) if joined else (8, 128), bf16),
+            V((up8(cols, 128), up8(rows, 128)) if joined else (8, 128), f32),
             dma((7, ctx_n, plane) if joined else (1,)), dma((7, ctx_n, plane) if joined else (1,)),
             dma((2,)), dma((8,)), dma((4,)),
             dma((2, 2, ctx_n, share)), dma((2, ctx_n, share)),
@@ -1031,7 +1045,86 @@
         compiler_params=pltpu.CompilerParams(
             collective_id=2, has_side_effects=True, vmem_limit_bytes=67043328
         ),
-    )(x_all, g_all, pack, small, up, down)
+    )(x_all, g_all, *given, up, down)
+
+
+def last_kernel(share, params, *refs):
+    (
+        lo_in, dx_in, e_in, e_act, e_hid, e_dexp, grad, smalls,
+        lo, dx, up_grad, down_grad, qkv_grad, proj_grad, gains, biases, router, rms,
+        hold, turn, lines, isem, osem, usem,
+    ) = refs
+    groups = lo_in.shape[0] // share
+    moves = [(a, b) for b in range(groups) for a in (0, 1)]
+
+    def take(a, b):
+        at = pl.ds(b * share, share)
+        return pltpu.make_async_copy((lo_in, dx_in)[a].at[at], hold.at[a, at], isem.at[a, b])
+
+    def give(a, b):
+        at = pl.ds(b * share, share)
+        return pltpu.make_async_copy(hold.at[a, at], (lo, dx)[a].at[at], osem.at[a, b])
+
+    for m in moves:
+        take(*m).start()
+    up_grad[...] = mm(e_in[...], e_hid[...], TN)
+    for m in moves[: len(moves) // 2]:
+        take(*m).wait()
+        give(*m).start()
+    down_grad[...] = mm(e_act[...], e_dexp[...], TN)
+    for m in moves[len(moves) // 2 :]:
+        take(*m).wait()
+        give(*m).start()
+    rows, packed = grad.shape
+    cols = packed // 4
+    for j in range(3):
+        qkv_grad[j] = grad[:, j * cols : (j + 1) * cols]
+    turn[:rows, :cols] = grad[:, 3 * cols :]
+    proj_grad[...] = turn[...].T[:cols, :rows]
+    total = smalls[0]
+    for b in range(1, groups):
+        total = total + smalls[b]
+    gains[...] = total[0:2, :rows]
+    biases[...] = total[2:4, :rows]
+    router[...] = total[4:params, :rows]
+    mark = smalls.shape[1] - 8
+    for b in range(groups):
+        lines[b * share : (b + 1) * share, :] = smalls[b, mark : mark + share, :]
+    rms[...] = lines[...].T[:3, : groups * share]
+    for m in moves:
+        give(*m).wait()
+
+
+def run_last(lo, dx, e_in, e_act, e_hid, e_dexp, grad, smalls, share, params):
+    rows, packed = grad.shape
+    cols = packed // 4
+    width, ff = e_in.shape[1], e_act.shape[1]
+    images = lo.shape[0]
+    groups = images // share
+    vm = pl.BlockSpec(memory_space=pltpu.VMEM)
+    hbm = pl.BlockSpec(memory_space=pl.ANY)
+    shape = jax.ShapeDtypeStruct
+    V = pltpu.VMEM
+    up8 = lambda v, m: v + -v % m
+    dma = pltpu.SemaphoreType.DMA
+    return pl.pallas_call(
+        functools.partial(last_kernel, share, params),
+        out_shape=(
+            shape(lo.shape, bf16), shape(dx.shape, bf16),
+            shape((width, ff), f32), shape((ff, width), f32),
+            shape((3, rows, cols), f32), shape((cols, rows), f32),
+            shape((2, rows), f32), shape((2, rows), f32), shape((params - 4, rows), f32),
+            shape((3, images), f32),
+        ),
+        in_specs=[hbm, hbm] + [vm] * 6,
+        out_specs=(hbm, hbm) + (vm,) * 8,
+        scratch_shapes=[
+            V((2,) + lo.shape, bf16),
+            V((up8(rows, 128), up8(cols, 128)), f32),
+            V((128, 128), f32),
+            dma((2, groups)), dma((2, groups)), dma((2,)),
+        ],
+    )(lo, dx, e_in, e_act, e_hid, e_dexp, grad, smalls)
 
 
 def on_device(
@@ -1050,36 +1143,35 @@
     share = images // ctx_n
     slots_n = router_keys.shape[1]
     rows, _, cols = qkv_weight.shape
-    plane = wide_n * ten_n
     lanes = rows + -rows % 128
 
-    pack = jnp.concatenate([qkv_weight.reshape(rows, 3 * cols), proj_weight.T], axis=1)
-    small = jnp.concatenate([norm_gains, norm_biases, router_keys.T], axis=0)
-    params = small.shape[0]
-    small = jnp.pad(small, ((0, -params % 16), (0, lanes - rows)))
+    params = 4 + slots_n
     if rows % 32 == 0:
-        weights = pack
+        given = (qkv_weight.transpose(1, 0, 2), proj_weight, norm_gains, norm_biases, router_keys.T)
     else:
+        pack = jnp.concatenate([qkv_weight.reshape(rows, 3 * cols), proj_weight.T], axis=1)
+        small = jnp.concatenate([norm_gains, norm_biases, router_keys.T], axis=0)
+        small = jnp.pad(small, ((0, -params % 16), (0, lanes - rows)))
         weights, small = gather_weights(pack, small)
         weights = weights.reshape(ctx_n, width, 4 * cols)
         small = small.reshape((-1,) + small.shape[3:])[:, :params, :rows]
         small = small.transpose(1, 0, 2).reshape(params, width)
-    layer_output, input_grad, dpack, dsmall, e_in, e_act, e_hid, e_dexp = run_block(
-        layer_input, out_cotangent, weights, small, slots_n, up_weight[0], down_weight[0], rows, share
+        given = (weights, small)
+    lo, dx, dpack, dsmall, *sides = run_block(
+        layer_input, out_cotangent, given, slots_n, up_weight[0], down_weight[0], rows, share
     )
-    up_grad = mm(e_in, e_hid, TN)
-    down_grad = mm(e_act, e_dexp, TN)
-    rms = dsmall[:, dsmall.shape[1] - 8 :, :3][:, :share].reshape(images, 3)
-    dsmall = jnp.sum(dsmall[:, :params, :rows], axis=0)
+    lo, dx, up_grad, down_grad, qkv_grad, proj_grad, gains, biases, router, rms = run_last(
+        lo, dx, *sides, dpack, dsmall, share, params
+    )
     return (
-        layer_output,
-        rms,
-        input_grad,
-        dpack[:, : 3 * cols].reshape(rows, 3, cols),
-        dpack[:, 3 * cols :].T,
-        dsmall[0:2],
-        dsmall[2:4],
-        dsmall[4:].T,
+        lo,
+        rms.T,
+        dx,
+        qkv_grad.transpose(1, 0, 2),
+        proj_grad,
+        gains,
+        biases,
+        router.T,
         up_grad[None],
         down_grad[None],
     )

time: 213 us -> 201 us (0.944)
  local copies, waits for them, and re-layouts: 13.8 us -> 0 us
  Pallas kernels: 190 us -> 200 us
  matrix products: 4.95 us -> 0 us
  other arithmetic: 2.97 us -> 0 us
    pallas_call x0 -> x1, Pallas kernels: none -> 9.89 us  [run_last(): pl.pallas_call(functools.partial(last_kernel, share, params), out_shape=(...]
    unnamed x14 -> x0, local copies, waits for them, and re-layouts: 8.81 us -> none
    dot_general x2 -> x0, matrix products: 4.95 us -> none  [mm(): lax.dot_general(a, b, dims, precision=precision, preferred_element_type=f32)]
    slice x5 -> x0, local copies, waits for them, and re-layouts: 2.58 us -> none  [the longest x2 1.11 us: on_device(): dpack[:, :3 * cols].reshape(rows, 3, cols)]
where the time goes in v6:
time: 201 us
  Pallas kernels  200 us (100%)
    pallas_call x1, Pallas kernels, run_block(): pl.pallas_call(functools.partial(block_kernel, share, joined), out_shape=...  190 us
    pallas_call x1, Pallas kernels, run_last(): pl.pallas_call(functools.partial(last_kernel, share, params), out_shape=(...  9.89 us

profile of v6, /device:TPU:0, one launch (start us, length us, event | category | flops | bytes accessed | tf_op | source)
XLA Modules:
  0.0 200.6 jit_solution(2307314319848454506)
XLA Ops:
  0.6 189.9 %shard_map.168 = (bf16[12,197,768]{2,1,0:T(8,128)(2,1)}, bf16[12,197,768]{2,1,0:T(8,128)(2,1)}, f32[96,768]{1,0:T(8,128)}, f32[4,24,128]{2,1,0:T(8,128)}, bf16[2...) custom-call(bf16[12,197,768]{2,1,0:T(8,128)(2,1)} %refs_0_.1, ...), custom_call_target="tpu_custom_call" | custom-call | tf_op jit(solution)/shard_map/pallas_call | solution.py:981
  190.5 9.9 %shard_map.169 = (bf16[12,197,768]{2,1,0:T(8,128)(2,1)}, bf16[12,197,768]{2,1,0:T(8,128)(2,1)}, f32[768,768]{1,0:T(8,128)}, f32[768,768]{1,0:T(8,128)}, f32[3,96...) custom-call(bf16[12,197,768]{2,1,0:T(8,128)(2,1)} %get-tuple-element, ...), custom_call_target="tpu_custom_call" | custom-call | tf_op jit(solution)/shard_map/pallas_call | solution.py:1110

commit v7 on v6

--- a/solution.py
+++ b/solution.py
@@ -332,25 +332,37 @@
             def _():
                 along(a, c, i, side, True).start()
 
-    def onward(cb, side):
+    spare = ctx_n > 2
+
+    def onward(cb, side, a=1):
         if side == 0:
-            return jnp.logical_and(cb > c, c > 0)
-        return jnp.logical_and(cb < c, c < ctx_n - 1)
+            go, end = jnp.logical_and(cb > c, c > 0), jnp.logical_and(c == 1, cb == ctx_n - 1)
+        else:
+            go, end = jnp.logical_and(cb < c, c < ctx_n - 1), jnp.logical_and(c == ctx_n - 2, cb == 0)
+        return jnp.logical_and(go, jnp.logical_not(end)) if a == 0 and spare else go
+
+    def at_end(cb):
+        return jnp.logical_or(
+            jnp.logical_and(c == 0, cb == ctx_n - 1), jnp.logical_and(c == ctx_n - 1, cb == 0)
+        )
 
     def pump(a, steps, i):
         for step in steps:
             cb = seq[step]
             for side in (0, 1):
 
-                @pl.when(onward(cb, side))
+                @pl.when(onward(cb, side, a))
                 def _():
                     along(a, cb, i, 0, False).wait_recv()
                     along(a, cb, i, side, False).start()
 
     def arrived(a, step, i):
         cb = seq[step]
-
-        @pl.when(jnp.logical_not(jnp.logical_or(onward(cb, 0), onward(cb, 1))))
+        passed = jnp.logical_or(onward(cb, 0, a), onward(cb, 1, a))
+        if a == 0 and spare:
+            passed = jnp.logical_or(passed, at_end(cb))
+
+        @pl.when(jnp.logical_not(passed))
         def _():
             along(a, cb, i, 0, False).wait_recv()
 
@@ -818,31 +830,65 @@
         trade(o, comb_all, 1, p).wait_recv()
 
     order = [(s, i) for s in range(1, ctx_n) for i in range(share)]
-
-    def mix_some(lo_n, hi_n):
-        for j in range(lo_n, hi_n):
-            step, i = order[j]
+    used = [share]
+
+    def attend_here():
+        hat, _ = layer_stats(x_buf[...].astype(f32))
+        normed = (hat * small[0:1, :].astype(f32) + small[2:3, :].astype(f32)).astype(bf16)
+        dn_s[...] = jnp.zeros_like(dn_s)
+
+        def block(cb, carry):
+            qkv_f = mm(normed, weight(cb, 0, 3 * cols))
+            qkv_c = jnp.concatenate([qkv_f[:, :cols] * 0.125, qkv_f[:, cols:]], axis=1).astype(bf16)
+            mixed = []
+            for h in range(per):
+                q, kk, v = head_parts(qkv_c, h, per)
+                s = mm(q, kk, NT)
+                e = jnp.exp(s - jnp.max(s, axis=1, keepdims=True))
+                p = (e * (1.0 / jnp.sum(e, axis=1, keepdims=True))).astype(bf16)
+                mixed.append(mm(p, v).astype(bf16))
+            dn_s[...] += mm(jnp.concatenate(mixed, axis=1), weight(cb, 3 * cols, packed), NT)
+            return carry
+
+        lax.fori_loop(0, ctx_n, block, 0)
+
+    def mix(todo):
+        for step, i in todo:
             cb = seq[step]
-            slot = (j + share) % 2
+            slot = used[0] % 2
+            used[0] += 1
             for side in (0, 1):
 
-                @pl.when(onward(cb, side))
+                @pl.when(onward(cb, side, 0))
                 def _():
                     along(0, cb, i, side, False).wait_send()
 
             arrived(0, step, i)
             put(step, i, slot).wait()
-            for cp in fetch(step, i, slot):
-                cp.start()
-            for cp in fetch(step, i, slot):
-                cp.wait()
+            far_att, own_x = fetch(step, i, slot)
+            own_x.start()
+            if spare and step == ctx_n - 1:
+
+                @pl.when(jnp.logical_not(at_end(cb)))
+                def _():
+                    far_att.start()
+                    far_att.wait()
+                    dn_s[...] = a_buf[slot].astype(f32)
+
+                own_x.wait()
+                pl.when(at_end(cb))(attend_here)
+                att = dn_s[...]
+            else:
+                far_att.start()
+                far_att.wait()
+                own_x.wait()
+                att = a_buf[slot].astype(f32)
             mixed = mm(comb_all[cb, i, :, :length], eo_all[cb, i], TN)
-            out = x_buf[...].astype(f32) + a_buf[slot].astype(f32) + mixed
-            a_buf[slot] = out.astype(bf16)
+            a_buf[slot] = (x_buf[...].astype(f32) + att + mixed).astype(bf16)
             put(step, i, slot).start()
 
     third = len(order) // 3
-    mix_some(0, third)
+    mix(order[:third] + order[2 * third : 2 * third + 1])
     for cc in range(ctx_n):
         on_wide = cc % 2 == 0
         for o in peers(cc, 2):
@@ -871,7 +917,7 @@
     for o in range(1, ctx_n):
         small2(o, c).start()
     pump(1, far, 2)
-    mix_some(third, 2 * third)
+    mix(order[third : 2 * third])
 
     def last(cc):
         return remote(acc3.at[cc], rcv4.at[c], s4.at[cc], r4.at[c], context=cc)
@@ -888,7 +934,7 @@
         def _():
             last(cc).start()
 
-    mix_some(2 * third, len(order))
+    mix(order[2 * third + 1 :])
     for step, i in order:
         arrived(1, step, i)
     tot = acc3[c].astype(f32)

time: 201 us -> 186 us (0.925)
  Pallas kernels: 200 us -> 185 us
    pallas_call x1, Pallas kernels: 190 us -> 175 us  [run_block(): pl.pallas_call(functools.partial(block_kernel, share, joined), out_shape=...]
where the time goes in v7:
time: 186 us
  Pallas kernels  185 us (99%)
    pallas_call x1, Pallas kernels, run_block(): pl.pallas_call(functools.partial(block_kernel, share, joined), out_shape=...  175 us
    pallas_call x1, Pallas kernels, run_last(): pl.pallas_call(functools.partial(last_kernel, share, params), out_shape=(...  9.89 us

profile of v7, /device:TPU:0, one launch (start us, length us, event | category | flops | bytes accessed | tf_op | source)
XLA Modules:
  0.0 185.8 jit_solution(10793614903143025785)
XLA Ops:
  0.6 175.0 %shard_map.168 = (bf16[12,197,768]{2,1,0:T(8,128)(2,1)}, bf16[12,197,768]{2,1,0:T(8,128)(2,1)}, f32[96,768]{1,0:T(8,128)}, f32[4,24,128]{2,1,0:T(8,128)}, bf16[2...) custom-call(bf16[12,197,768]{2,1,0:T(8,128)(2,1)} %refs_0_.1, ...), custom_call_target="tpu_custom_call" | custom-call | tf_op jit(solution)/shard_map/pallas_call | solution.py:1027
  175.7 9.9 %shard_map.169 = (bf16[12,197,768]{2,1,0:T(8,128)(2,1)}, bf16[12,197,768]{2,1,0:T(8,128)(2,1)}, f32[768,768]{1,0:T(8,128)}, f32[768,768]{1,0:T(8,128)}, f32[3,96...) custom-call(bf16[12,197,768]{2,1,0:T(8,128)(2,1)} %get-tuple-element, ...), custom_call_target="tpu_custom_call" | custom-call | tf_op jit(solution)/shard_map/pallas_call | solution.py:1156
